TPU v7x, 128 devices: a whole 4x4x4 slice. The times are simulated.
128 devices in a mesh: heads: 16 (over z, y), model: 8 (over x, core).
Axes of the slice: x: 4, y: 4, z: 4, core: 2. Of those that a mesh axis runs over, the one named last changes fastest.
Arguments:
- hidden_in: bfloat16 [4096, 3072], P(None, 'model')
- seg_ids: int32 [4096], replicated
- positions: int32 [4096], replicated
- w_query: bfloat16 [2, 3072, 4096], P(None, 'model', 'heads')
- w_key: bfloat16 [2, 3072, 4096], P(None, 'model', 'heads')
- w_value: bfloat16 [2, 3072, 4096], P(None, 'model', 'heads')
- w_out: bfloat16 [2, 4096, 3072], P(None, 'heads', 'model')
- w_gate: bfloat16 [2, 3072, 24576], P(None, 'model', 'heads')
- w_up: bfloat16 [2, 3072, 24576], P(None, 'model', 'heads')
- w_down: bfloat16 [2, 24576, 3072], P(None, 'heads', 'model')
- norm_scales: float32 [2, 4, 3072], P(None, None, 'model')
- qk_scales: float32 [2, 2, 256], replicated
Outputs:
- output 1: bfloat16 [4096, 3072], P(None, 'model')
- output 2: bfloat16 [2, 4096, 16, 256], P(None, None, 'heads')
- output 3: bfloat16 [2, 4096, 16, 256], P(None, None, 'heads')
All inputs are finite; a program needn't handle non-finite values.
Results may differ from a plain program's by a relative error of at most 0.02.
Values are sent between devices in bfloat16 or wider.
A program may use at most 1 GiB of HBM per device.

v0:
```python
import jax
import jax.numpy as jnp
from jax import lax
from jax.sharding import PartitionSpec as P

NORM_EPS = 1e-6
Q_BLOCK = 256
WINDOW = 1024
GLOBAL_BASE = 1000000.0
GLOBAL_FACTOR = 8.0
LOCAL_BASE = 10000.0


def head_norm(values, scale_row):
    mean_sq = jnp.mean(values * values, axis=-1, keepdims=True)
    return values * lax.rsqrt(mean_sq + NORM_EPS) * (1.0 + scale_row)


def rope_tables(positions, head_dim, rope_base, pos_factor):
    exponents = jnp.arange(0, head_dim, 2).astype(jnp.float32) / head_dim
    inv_freq = rope_base ** (-exponents)
    angles = (positions.astype(jnp.float32) / pos_factor)[:, None] * inv_freq[None, :]
    return jnp.cos(angles), jnp.sin(angles)


def apply_rope(values, cos_tab, sin_tab):
    half_dim = values.shape[-1] // 2
    first_half = values[..., :half_dim]
    second_half = values[..., half_dim:]
    cos_bcast = cos_tab[:, None, :]
    sin_bcast = sin_tab[:, None, :]
    return jnp.concatenate([first_half * cos_bcast - second_half * sin_bcast, second_half * cos_bcast + first_half * sin_bcast], axis=-1)


def attend(query_heads, key_heads, value_heads, seg_ids, positions, window):
    n_tok, kv_count, head_dim = key_heads.shape
    group_size = query_heads.shape[1] // kv_count
    n_blocks = n_tok // Q_BLOCK
    q_scale = head_dim ** -0.5
    q_blocks = query_heads.reshape(n_blocks, Q_BLOCK, kv_count, group_size, head_dim)
    seg_blocks = seg_ids.reshape(n_blocks, Q_BLOCK)
    pos_blocks = positions.reshape(n_blocks, Q_BLOCK)

    def one_block(block_args):
        q_blk, seg_blk, pos_blk = block_args
        scores = jnp.einsum('qkgd,tkd->kgqt', q_blk, key_heads, preferred_element_type=jnp.float32) * q_scale
        pos_gap = pos_blk[:, None] - positions[None, :]
        allowed = (seg_blk[:, None] == seg_ids[None, :]) & (pos_gap >= 0) & (pos_gap < window)
        scores = jnp.where(allowed[None, None], scores, -1e30)
        row_max = jnp.max(scores, axis=-1, keepdims=True)
        exp_scores = jnp.exp(scores - row_max)
        probs_bf = (exp_scores / jnp.sum(exp_scores, axis=-1, keepdims=True)).astype(jnp.bfloat16)
        blk_out = jnp.einsum('kgqt,tkd->qkgd', probs_bf, value_heads, preferred_element_type=jnp.float32)
        return blk_out.astype(jnp.bfloat16)

    attn_out = lax.map(one_block, (q_blocks, seg_blocks, pos_blocks))
    return attn_out.reshape(n_tok, -1)


def solution(mesh):
    n_model = mesh.shape['model']
    col_spec = P(None, 'model', 'heads')
    row_spec = P(None, 'heads', 'model')
    cache_spec = P(None, None, 'heads', None)

    def body(hidden_in, seg_ids, positions, w_query, w_key, w_value, w_out, w_gate, w_up, w_down, norm_scales, qk_scales):
        n_tok = hidden_in.shape[0]
        head_dim = qk_scales.shape[-1]
        full_width = hidden_in.shape[1] * n_model

        def width_norm(values, scale_row):
            sq_sum = lax.psum(jnp.sum(values * values, axis=-1, keepdims=True), 'model')
            return values * lax.rsqrt(sq_sum / full_width + NORM_EPS) * (1.0 + scale_row)

        settings = ((GLOBAL_BASE, GLOBAL_FACTOR, n_tok), (LOCAL_BASE, 1.0, WINDOW))
        hidden = hidden_in
        key_list = []
        value_list = []
        for layer_idx in range(2):
            rope_base, pos_factor, window = settings[layer_idx]
            resid_f32 = hidden.astype(jnp.float32)
            normed = width_norm(resid_f32, norm_scales[layer_idx, 0]).astype(jnp.bfloat16)
            q_part, k_part, v_part = lax.psum((
                jnp.dot(normed, w_query[layer_idx], preferred_element_type=jnp.float32),
                jnp.dot(normed, w_key[layer_idx], preferred_element_type=jnp.float32),
                jnp.dot(normed, w_value[layer_idx], preferred_element_type=jnp.float32)), 'model')
            cos_tab, sin_tab = rope_tables(positions, head_dim, rope_base, pos_factor)
            query_heads = apply_rope(head_norm(q_part.astype(jnp.bfloat16).astype(jnp.float32).reshape(n_tok, -1, head_dim), qk_scales[layer_idx, 0]), cos_tab, sin_tab).astype(jnp.bfloat16)
            key_heads = apply_rope(head_norm(k_part.astype(jnp.bfloat16).astype(jnp.float32).reshape(n_tok, -1, head_dim), qk_scales[layer_idx, 1]), cos_tab, sin_tab).astype(jnp.bfloat16)
            value_heads = v_part.astype(jnp.bfloat16).reshape(n_tok, -1, head_dim)
            attn_out = attend(query_heads, key_heads, value_heads, seg_ids, positions, window)
            attn_sum = lax.psum(jnp.dot(attn_out, w_out[layer_idx], preferred_element_type=jnp.float32), 'heads').astype(jnp.bfloat16)
            hidden_mid = (resid_f32 + width_norm(attn_sum.astype(jnp.float32), norm_scales[layer_idx, 1])).astype(jnp.bfloat16)
            mid_f32 = hidden_mid.astype(jnp.float32)
            normed_ffn = width_norm(mid_f32, norm_scales[layer_idx, 2]).astype(jnp.bfloat16)
            gate_part, up_part = lax.psum((
                jnp.dot(normed_ffn, w_gate[layer_idx], preferred_element_type=jnp.float32),
                jnp.dot(normed_ffn, w_up[layer_idx], preferred_element_type=jnp.float32)), 'model')
            gate_act = jax.nn.gelu(gate_part.astype(jnp.bfloat16).astype(jnp.float32), approximate=True)
            ffn_in = (gate_act * up_part.astype(jnp.bfloat16).astype(jnp.float32)).astype(jnp.bfloat16)
            ffn_sum = lax.psum(jnp.dot(ffn_in, w_down[layer_idx], preferred_element_type=jnp.float32), 'heads').astype(jnp.bfloat16)
            hidden = (mid_f32 + width_norm(ffn_sum.astype(jnp.float32), norm_scales[layer_idx, 3])).astype(jnp.bfloat16)
            key_list.append(key_heads)
            value_list.append(value_heads)
        return hidden, jnp.stack(key_list), jnp.stack(value_list)

    return jax.shard_map(body, mesh=mesh,
                         in_specs=(P(None, 'model'), P(), P(), col_spec, col_spec, col_spec, row_spec, col_spec, col_spec, row_spec, P(None, None, 'model'), P()),
                         out_specs=(P(None, 'model'), cache_spec, cache_spec),
                         check_vma=False)
```

profile of v0, /device:TPU:0, one launch (start us, length us, event | category | flops | bytes accessed | tf_op | source)
XLA Modules:
  0.0 2481.2 jit_solution(29401514989391630)
XLA Ops:
  7.8 25.8 %psum.154 = f32[4096,1]{0,1:T(1,128)S(1)} all-reduce(f32[4096,1]{0,1:T(1,128)S(1)} %bitcast.256), channel_id=1, replica_groups=mesh['heads'=16,'model'=8] {'model'}, use_global_device_ids=true, to_apply=%region_1.0 | all-reduce | flops 4096 | bytes 32768 | tf_op jit(solution)/shard_map/psum | solution.py:72
  48.2 131.4 %all-reduce.12 = (bf16[4096,256]{1,0:T(8,128)(2,1)}, bf16[4096,256]{1,0:T(8,128)(2,1)}, bf16[4096,256]{1,0:T(8,128)(2,1)}) all-reduce(f32[4096,256]{1,0:T(8,128)} %fusion.174, f32[4096,256]{1,0:T(8,128)} %fusion.172, f32[4096,256]{1,0:T(8,128)} %fusion.170), channel_id=1, replica_groups=mesh['heads'=16,'model'=8] {'model'}, use_global_device_ids=true, to_apply=%region_2.0 | all-reduce | flops 3145728 | bytes 18874368 | tf_op jit(solution)/shard_map/psum | solution.py:83
  200.1 114.9 %while.20 = (s32[]{:T(128)}, bf16[16,256,1,1,256]{4,1,3,2,0:T(8,128)(2,1)}, s32[16,256]{1,0:T(8,128)}, s32[4096]{0:T(1024)}, s32[16,256]{1,0:T(8,128)}, /*index=...) while((s32[]{:T(128)}, ...), condition=%wide.region_10.11_spmd, body=%wide.region_7.10_spmd.sunk | while | flops 1088486912 | bytes 25472148 | solution.py:56
  320.5 148.4 %all-reduce.13 = bf16[4096,384]{1,0:T(8,128)(2,1)} all-reduce(f32[4096,384]{1,0:T(8,128)} %fusion.168), channel_id=1, replica_groups=mesh['heads'=16,'model'=8] {'heads'}, use_global_device_ids=true, to_apply=%region_11.12 | all-reduce | flops 1572864 | bytes 9437184 | tf_op jit(solution)/shard_map/psum | solution.py:92
  471.5 23.6 psum.159
  499.8 24.0 psum.160
  523.9 13.6 fusion.146
  537.5 11.7 fusion.148
  549.2 502.9 %all-reduce.14 = (bf16[4096,1536]{1,0:T(8,128)(2,1)}, bf16[4096,1536]{1,0:T(8,128)(2,1)}) all-reduce(f32[4096,1536]{1,0:T(8,128)} %fusion.146, f32[4096,1536]{1,0:T(8,128)} %fusion.148), channel_id=1, replica_groups=mesh['heads'=16,'model'=8] {'model'}, use_global_device_ids=true, to_apply=%region_17.18 | all-reduce | flops 12582912 | bytes 75497472 | tf_op jit(solution)/shard_map/psum | solution.py:96
  1052.2 17.5 fusion.70
  1069.7 144.3 %all-reduce.15 = bf16[4096,384]{1,0:T(8,128)(2,1)S(1)} all-reduce(f32[4096,384]{1,0:T(8,128)} %fusion.70), channel_id=1, replica_groups=mesh['heads'=16,'model'=8] {'heads'}, use_global_device_ids=true, to_apply=%region_18.19 | all-reduce | flops 1572864 | bytes 9437184 | tf_op jit(solution)/shard_map/psum | solution.py:101
  1214.7 23.6 psum.164
  1243.1 24.7 psum.165
  1277.9 131.4 %all-reduce.16 = (bf16[4096,256]{1,0:T(8,128)(2,1)}, bf16[4096,256]{1,0:T(8,128)(2,1)}, bf16[4096,256]{1,0:T(8,128)(2,1)}) all-reduce(f32[4096,256]{1,0:T(8,128)} %fusion.166, f32[4096,256]{1,0:T(8,128)} %fusion.164, f32[4096,256]{1,0:T(8,128)} %fusion.162), channel_id=1, replica_groups=mesh['heads'=16,'model'=8] {'model'}, use_global_device_ids=true, to_apply=%region_23.24 | all-reduce | flops 3145728 | bytes 18874368 | tf_op jit(solution)/shard_map/psum | solution.py:83
  1433.0 116.9 %while.21 = (s32[]{:T(128)}, bf16[16,256,1,1,256]{4,1,3,2,0:T(8,128)(2,1)}, s32[16,256]{1,0:T(8,128)}, s32[4096]{0:T(1024)S(1)}, s32[16,256]{1,0:T(8,128)}, /*in...) while((s32[]{:T(128)}, ...), condition=%wide.region_31.32_spmd, body=%wide.region_28.31_spmd.sunk | while | flops 1088486912 | bytes 25472148 | solution.py:56
  1558.6 146.5 %all-reduce.17 = bf16[4096,384]{1,0:T(8,128)(2,1)} all-reduce(f32[4096,384]{1,0:T(8,128)} %fusion.160), channel_id=1, replica_groups=mesh['heads'=16,'model'=8] {'heads'}, use_global_device_ids=true, to_apply=%region_32.33 | all-reduce | flops 1572864 | bytes 9437184 | tf_op jit(solution)/shard_map/psum | solution.py:92
  1707.7 23.8 psum.170
  1736.3 23.5 psum.171
  1759.9 13.7 fusion.141
  1773.6 11.7 fusion.143
  1785.3 503.0 %all-reduce.18 = (bf16[4096,1536]{1,0:T(8,128)(2,1)}, bf16[4096,1536]{1,0:T(8,128)(2,1)}) all-reduce(f32[4096,1536]{1,0:T(8,128)} %fusion.141, f32[4096,1536]{1,0:T(8,128)} %fusion.143), channel_id=1, replica_groups=mesh['heads'=16,'model'=8] {'model'}, use_global_device_ids=true, to_apply=%region_38.39 | all-reduce | flops 12582912 | bytes 75497472 | tf_op jit(solution)/shard_map/psum | solution.py:96
  2288.3 17.8 fusion.68
  2306.1 144.8 %all-reduce.19 = bf16[4096,384]{1,0:T(8,128)(2,1)} all-reduce(f32[4096,384]{1,0:T(8,128)} %fusion.68), channel_id=1, replica_groups=mesh['heads'=16,'model'=8] {'heads'}, use_global_device_ids=true, to_apply=%region_39.40 | all-reduce | flops 1572864 | bytes 9437184 | tf_op jit(solution)/shard_map/psum | solution.py:101
  2453.5 23.6 psum.175
  (316 shorter events, 348.2 us)
Async XLA Ops:
  37.2 5.4 copy-start
  37.2 5.4 copy-start.18
  179.7 3.6 copy-start.11
  195.2 3.4 copy-start.5
  195.2 3.4 copy-start.7
  200.1 114.9 %copy-start.22 = (bf16[2,256,384]{2,1,0:T(8,128)(2,1)S(1)}, bf16[2,256,384]{2,1,0:T(8,128)(2,1)}, u32[]{:S(2)}) copy-start(bf16[2,256,384]{2,1,0:T(8,128)(2,1)} %param.22) | copy-start | bytes 1179652
  320.5 174.6 %copy-start.32 = (f32[384]{0:T(512)S(1)}, f32[384]{0:T(512)}, u32[]{:S(2)}) copy-start(f32[384]{0:T(512)} %get-tuple-element.122) | copy-start | bytes 4612
  495.1 28.7 %copy-start.27 = (f32[384]{0:T(512)S(1)}, f32[384]{0:T(512)}, u32[]{:S(2)}) copy-start(f32[384]{0:T(512)} %get-tuple-element.121) | copy-start | bytes 4612
  523.8 13.7 copy-start.1
  523.9 13.7 copy-start.13
  549.2 502.9 %copy-start.36 = (bf16[2,1536,384]{2,1,0:T(8,128)(2,1)S(1)}, bf16[2,1536,384]{2,1,0:T(8,128)(2,1)}, u32[]{:S(2)}) copy-start(bf16[2,1536,384]{2,1,0:T(8,128)(2,1)} %param.25) | copy-start | bytes 7077892
  1214.0 24.3 copy-start.3
  1238.3 30.3 %copy-start.17 = (bf16[2,384,256]{2,1,0:T(8,128)(2,1)S(1)}, bf16[2,384,256]{2,1,0:T(8,128)(2,1)}, u32[]{:S(2)}) copy-start(bf16[2,384,256]{2,1,0:T(8,128)(2,1)} %param.20) | copy-start | bytes 1179652
  1268.6 3.6 copy-start.19
  1268.6 3.6 copy-start.25
  1409.3 4.8 copy-start.12
  1409.3 4.8 copy-start.34
  1549.9 4.8 copy-start.4
  1549.9 4.8 copy-start.23
  1558.6 172.9 %copy-start.31 = (f32[384]{0:T(512)S(1)}, f32[384]{0:T(512)}, u32[]{:S(2)}) copy-start(f32[384]{0:T(512)} %get-tuple-element.118) | copy-start | bytes 4612
  1731.5 28.3 %copy-start.26 = (f32[384]{0:T(512)S(1)}, f32[384]{0:T(512)}, u32[]{:S(2)}) copy-start(f32[384]{0:T(512)} %get-tuple-element.117) | copy-start | bytes 4612
  1759.9 13.7 copy-start.2
  1759.9 13.7 copy-start.14
  2306.1 171.0 %copy-start.30 = (f32[384]{0:T(512)S(1)}, f32[384]{0:T(512)}, u32[]{:S(2)}) copy-start(f32[384]{0:T(512)} %get-tuple-element.124) | copy-start | bytes 4612
  (43 other events, 76.3 us)
where the time goes:
time: 2490 us; the launch traced here: 2480 us
  blocking collectives  2050 us (82%)
  matrix products  273 us (11%)
  other arithmetic  102 us (4%)
  local copies, waits for them, and re-layouts  58.5 us (2%)
    psum x2, blocking collectives, body(): lax.psum((jnp.dot(normed_ffn, w_gate[layer_idx], preferred_element_type=j...  1010 us
    psum x2, blocking collectives, body(): lax.psum(jnp.dot(attn_out, w_out[layer_idx], preferred_element_type=jnp.f...  295 us
    psum x2, blocking collectives, body(): lax.psum(jnp.dot(ffn_in, w_down[layer_idx], preferred_element_type=jnp.fl...  289 us
    psum x2, blocking collectives, body(): lax.psum((jnp.dot(normed, w_query[layer_idx], preferred_element_type=jnp....  263 us
    psum x8, blocking collectives, width_norm(): sq_sum = lax.psum(jnp.sum(values * values, axis=-1, keepdims=True), 'model')  192 us
    dot_general x32, matrix products, one_block(): jnp.einsum('qkgd,tkd->kgqt', q_blk, key_heads, preferred_element_type=jnp...  108 us

commit v1 on v0

v1 whole, which is shorter than its diff:
```python
import jax
import jax.numpy as jnp
from jax import lax
from jax.sharding import PartitionSpec as P

NORM_EPS = 1e-6
WINDOW = 1024
GLOBAL_BASE = 1000000.0
GLOBAL_FACTOR = 8.0
LOCAL_BASE = 10000.0


def norm(values, scale_row):
    mean_sq = jnp.mean(values * values, axis=-1, keepdims=True)
    return values * lax.rsqrt(mean_sq + NORM_EPS) * (1.0 + scale_row)


def rope_tables(positions, head_dim, rope_base, pos_factor):
    exponents = jnp.arange(0, head_dim, 2).astype(jnp.float32) / head_dim
    inv_freq = rope_base ** (-exponents)
    angles = (positions.astype(jnp.float32) / pos_factor)[:, None] * inv_freq[None, :]
    return jnp.cos(angles), jnp.sin(angles)


def apply_rope(values, cos_tab, sin_tab):
    half_dim = values.shape[-1] // 2
    first_half = values[..., :half_dim]
    second_half = values[..., half_dim:]
    return jnp.concatenate([first_half * cos_tab - second_half * sin_tab, second_half * cos_tab + first_half * sin_tab], axis=-1)


def attend(q, k, v, seg_q, pos_q, seg_ids, positions, window):
    scores = jnp.dot(q, k.T, preferred_element_type=jnp.float32) * (q.shape[-1] ** -0.5)
    gap = pos_q[:, None] - positions[None, :]
    allowed = (seg_q[:, None] == seg_ids[None, :]) & (gap >= 0) & (gap < window)
    scores = jnp.where(allowed, scores, -1e30)
    row_max = jnp.max(scores, axis=-1, keepdims=True)
    e = jnp.exp(scores - row_max)
    p = (e / jnp.sum(e, axis=-1, keepdims=True)).astype(jnp.bfloat16)
    return jnp.dot(p, v, preferred_element_type=jnp.float32).astype(jnp.bfloat16)


def solution(mesh):
    n_model = mesh.shape['model']
    n_heads = mesh.shape['heads']
    col_spec = P(None, 'model', 'heads')
    row_spec = P(None, 'heads', 'model')
    cache_spec = P(None, None, 'heads', None)

    def body(hidden_in, seg_ids, positions, w_query, w_key, w_value, w_out, w_gate, w_up, w_down, norm_scales, qk_scales):
        n_tok, width_loc = hidden_in.shape
        width = width_loc * n_model
        head_dim = qk_scales.shape[-1]
        tok_m = n_tok // n_model
        tok_own = tok_m // n_heads
        hd = lax.axis_index('heads')
        md = lax.axis_index('model')

        def gather_rows(w):
            return lax.all_gather(w, 'model', axis=0, tiled=True)

        def gather_cols(w):
            return lax.all_gather(w, 'model', axis=0)

        def dot_cols(a, w):
            parts = [jnp.dot(a, w[i], preferred_element_type=jnp.float32) for i in range(n_model)]
            return jnp.concatenate(parts, axis=1)

        scales = lax.all_gather(norm_scales, 'model', axis=2, tiled=True)
        mine = lax.dynamic_index_in_dim(hidden_in.reshape(n_model, n_heads, tok_own, width_loc), hd, 1, keepdims=False)
        mine = lax.all_to_all(mine, 'model', split_axis=0, concat_axis=0)
        resid = mine.transpose(1, 0, 2).reshape(tok_own, width)

        pos_m = lax.dynamic_slice_in_dim(positions, md * tok_m, tok_m)
        seg_m = lax.dynamic_slice_in_dim(seg_ids, md * tok_m, tok_m)

        settings = ((GLOBAL_BASE, GLOBAL_FACTOR, n_tok), (LOCAL_BASE, 1.0, WINDOW))
        keys, values = [], []
        for l in range(2):
            rope_base, pos_factor, window = settings[l]
            resid_f32 = resid.astype(jnp.float32)
            h_own = norm(resid_f32, scales[l, 0]).astype(jnp.bfloat16)
            h = lax.all_gather(h_own, 'heads', axis=0, tiled=True)
            wq, wk, wv = gather_rows(w_query[l]), gather_rows(w_key[l]), gather_rows(w_value[l])
            q = jnp.dot(h, wq, preferred_element_type=jnp.float32).astype(jnp.bfloat16)
            k = jnp.dot(h, wk, preferred_element_type=jnp.float32).astype(jnp.bfloat16)
            v = jnp.dot(h, wv, preferred_element_type=jnp.float32).astype(jnp.bfloat16)
            cos_tab, sin_tab = rope_tables(pos_m, head_dim, rope_base, pos_factor)
            q = apply_rope(norm(q.astype(jnp.float32), qk_scales[l, 0]), cos_tab, sin_tab).astype(jnp.bfloat16)
            k = apply_rope(norm(k.astype(jnp.float32), qk_scales[l, 1]), cos_tab, sin_tab).astype(jnp.bfloat16)
            k_all = lax.all_gather(k, 'model', axis=0, tiled=True)
            v_all = lax.all_gather(v, 'model', axis=0, tiled=True)
            keys.append(k_all[:, None, :])
            values.append(v_all[:, None, :])
            o = attend(q, k_all, v_all, seg_m, pos_m, seg_ids, positions, window)
            wo = gather_cols(w_out[l])
            a = lax.psum_scatter(dot_cols(o, wo), 'heads', scatter_dimension=0, tiled=True).astype(jnp.bfloat16)
            x1 = (resid_f32 + norm(a.astype(jnp.float32), scales[l, 1])).astype(jnp.bfloat16)
            x1_f32 = x1.astype(jnp.float32)
            h2_own = norm(x1_f32, scales[l, 2]).astype(jnp.bfloat16)
            h2 = lax.all_gather(h2_own, 'heads', axis=0, tiled=True)
            wg, wu = gather_rows(w_gate[l]), gather_rows(w_up[l])
            g = jnp.dot(h2, wg, preferred_element_type=jnp.float32).astype(jnp.bfloat16)
            u = jnp.dot(h2, wu, preferred_element_type=jnp.float32).astype(jnp.bfloat16)
            mid = (jax.nn.gelu(g.astype(jnp.float32), approximate=True) * u.astype(jnp.float32)).astype(jnp.bfloat16)
            wd = gather_cols(w_down[l])
            f = lax.psum_scatter(dot_cols(mid, wd), 'heads', scatter_dimension=0, tiled=True).astype(jnp.bfloat16)
            resid = (x1_f32 + norm(f.astype(jnp.float32), scales[l, 3])).astype(jnp.bfloat16)
        out = resid.reshape(tok_own, n_model, width_loc).transpose(1, 0, 2)
        out = lax.all_to_all(out, 'model', split_axis=0, concat_axis=0)
        out = lax.all_gather(out, 'heads', axis=1).reshape(n_tok, width_loc)
        return out, jnp.stack(keys), jnp.stack(values)

    return jax.shard_map(body, mesh=mesh,
                         in_specs=(P(None, 'model'), P(), P(), col_spec, col_spec, col_spec, row_spec, col_spec, col_spec, row_spec, P(None, None, 'model'), P()),
                         out_specs=(P(None, 'model'), cache_spec, cache_spec),
                         check_vma=False)
```

time: 2490 us -> 1350 us (0.54)
  blocking collectives: 2050 us -> 24.9 us
  waiting for transfers between devices: 0 us -> 1070 us
  matrix products: 273 us -> 145 us
  other arithmetic: 102 us -> 29.3 us
    psum x16 -> x0, blocking collectives: 2050 us -> none  [the longest x2 1010 us: body(): lax.psum((jnp.dot(normed_ffn, w_gate[layer_idx], preferred_element_type=j...]
    all_gather x0 -> x23, waiting for transfers between devices: none -> 743 us  [the longest x10 295 us: gather_rows(): return lax.all_gather(w, 'model', axis=0, tiled=True)]
    reduce_scatter x0 -> x4, waiting for transfers between devices: none -> 324 us  [the longest x2 164 us: body(): lax.psum_scatter(dot_cols(mid, wd), 'heads', scatter_dimension=0, tiled=T...]
    dot_general x78 -> x46, matrix products: 273 us -> 145 us  [the longest x32 61.4 us: dot_cols(): jnp.dot(a, w[i], preferred_element_type=jnp.float32)]
    reduce_sum x43 -> x10, other arithmetic: 56.2 us -> 11 us  [the longest x8 8.44 us: norm(): mean_sq = jnp.mean(values * values, axis=-1, keepdims=True)]
    unnamed x70 -> x41, local copies, waits for them, and re-layouts: 1.6 us -> 41 us
    while x64 -> x0, local copies, waits for them, and re-layouts: 28.2 us -> none
  transfers between devices with their start and end apart: 0 -> 28, of which waited for: 0 -> 27; matrix products, arithmetic and copies ran while one was open for 0% -> 9% of each run, Pallas kernels for 0% -> 0%
where the time goes in v1:
time: 1350 us
  waiting for transfers between devices  1070 us (79%)
  matrix products  145 us (11%)
  local copies, waits for them, and re-layouts  57.2 us (4%)
  other arithmetic  29.3 us (2%)
  blocking collectives  24.9 us (2%)
  between operations  15.2 us (1%)
    all_gather x10, waiting for transfers between devices, gather_rows(): return lax.all_gather(w, 'model', axis=0, tiled=True)  295 us
    reduce_scatter x2, waiting for transfers between devices, body(): lax.psum_scatter(dot_cols(mid, wd), 'heads', scatter_dimension=0, tiled=T...  164 us
    reduce_scatter x2, waiting for transfers between devices, body(): lax.psum_scatter(dot_cols(o, wo), 'heads', scatter_dimension=0, tiled=True)  160 us
    all_gather x4, waiting for transfers between devices, gather_cols(): return lax.all_gather(w, 'model', axis=0)  134 us
    all_gather x2, waiting for transfers between devices, body(): h = lax.all_gather(h_own, 'heads', axis=0, tiled=True)  102 us
    all_gather x2, waiting for transfers between devices, body(): h2 = lax.all_gather(h2_own, 'heads', axis=0, tiled=True)  101 us
    dot_general x32, matrix products, dot_cols(): jnp.dot(a, w[i], preferred_element_type=jnp.float32)  61.4 us
    all_gather x2, waiting for transfers between devices, body(): k_all = lax.all_gather(k, 'model', axis=0, tiled=True)  44 us
  transfers between devices with their start and end apart: 28, of which 27 were waited for; matrix products, arithmetic and copies ran while one was open for 9% of the time, Pallas kernels for 0%

profile of v1, /device:TPU:0, one launch (start us, length us, event | category | flops | bytes accessed | tf_op | source)
XLA Modules:
  0.0 1349.2 jit_solution(7585206118221082382)
XLA Ops:
  37.1 50.8 %all-gather.35.cloned.1.call-done = bf16[512,3072]{1,0:T(8,128)(2,1)} async-done(((bf16[32,3072]{1,0:T(8,128)(2,1)}), bf16[512,3072]{1,0:T(8,128)(2,1)}) %all-gather.35.cloned.1.call-update) | async-done | bytes 3145744 | tf_op jit(solution)/shard_map/all_gather | solution.py:83
  91.3 21.2 %all-gather.59.cloned.1.call-done = bf16[1,3072,256]{2,1,0:T(8,128)(2,1)} async-done(((bf16[1,384,256]{2,1,0:T(8,128)(2,1)}), bf16[1,3072,256]{2,1,0:T(8,128)(2,1)}) %all-gather.59.cloned.1.call-update) | async-done | bytes 1572880 | tf_op jit(solution)/shard_map/all_gather | solution.py:60
  118.1 21.0 %all-gather.63.cloned.1.call-done = bf16[1,3072,256]{2,1,0:T(8,128)(2,1)} async-done(((bf16[1,384,256]{2,1,0:T(8,128)(2,1)}), bf16[1,3072,256]{2,1,0:T(8,128)(2,1)}) %all-gather.63.cloned.1.call-update) | async-done | bytes 1572880 | tf_op jit(solution)/shard_map/all_gather | solution.py:60
  144.6 21.8 %all-gather.37.cloned.1.call-done = bf16[4096,256]{0,1:T(8,128)(2,1)} async-done(((bf16[512,256]{0,1:T(8,128)(2,1)}), bf16[4096,256]{0,1:T(8,128)(2,1)}) %all-gather.37.cloned.1.call-update) | async-done | bytes 2097168 | tf_op jit(solution)/shard_map/all_gather | solution.py:91
  199.8 21.7 %all-gather.41.cloned.1.call-done = bf16[8,256,384]{2,1,0:T(8,128)(2,1)} async-done(((bf16[1,256,384]{2,1,0:T(8,128)(2,1)}), bf16[8,256,384]{2,1,0:T(8,128)(2,1)}) %all-gather.41.cloned.1.call-update) | async-done | bytes 1572880 | tf_op jit(solution)/shard_map/all_gather | solution.py:63
  244.1 78.8 %reduce-scatter.13.cloned.1.call-done = f32[32,3072]{1,0:T(8,128)} async-done(((f32[512,3072]{1,0:T(8,128)}), f32[32,3072]{1,0:T(8,128)}) %reduce-scatter.13.cloned.1.call-update) | async-done | bytes 393232 | tf_op jit(solution)/shard_map/reduce_scatter | solution.py:97
  331.4 47.0 %all-gather.67.cloned.1.call-done = bf16[1,3072,1536]{2,1,0:T(8,128)(2,1)} async-done(((bf16[1,384,1536]{2,1,0:T(8,128)(2,1)}), bf16[1,3072,1536]{2,1,0:T(8,128)(2,1)}) %all-gather.67.cloned.1.call-update) | async-done | bytes 9437200 | tf_op jit(solution)/shard_map/all_gather | solution.py:60
  378.4 50.2 %all-gather.43.cloned.1.call-done = bf16[512,3072]{1,0:T(8,128)(2,1)} async-done(((bf16[32,3072]{1,0:T(8,128)(2,1)}), bf16[512,3072]{1,0:T(8,128)(2,1)}) %all-gather.43.cloned.1.call-update) | async-done | bytes 3145744 | tf_op jit(solution)/shard_map/all_gather | solution.py:101
  439.0 43.9 %all-gather.65.cloned.1.call-done = bf16[1,3072,1536]{2,1,0:T(8,128)(2,1)} async-done(((bf16[1,384,1536]{2,1,0:T(8,128)(2,1)}), bf16[1,3072,1536]{2,1,0:T(8,128)(2,1)}) %all-gather.65.cloned.1.call-update) | async-done | bytes 9437200 | tf_op jit(solution)/shard_map/all_gather | solution.py:60
  493.1 45.6 %all-gather.45.cloned.1.call-done = bf16[8,1536,384]{2,1,0:T(8,128)(2,1)} async-done(((bf16[1,1536,384]{2,1,0:T(8,128)(2,1)}), bf16[8,1536,384]{2,1,0:T(8,128)(2,1)}) %all-gather.45.cloned.1.call-update) | async-done | bytes 9437200 | tf_op jit(solution)/shard_map/all_gather | solution.py:63
  563.9 81.5 %reduce-scatter.15.cloned.1.call-done = f32[32,3072]{1,0:T(8,128)} async-done(((f32[512,3072]{1,0:T(8,128)}), f32[32,3072]{1,0:T(8,128)}) %reduce-scatter.15.cloned.1.call-update) | async-done | bytes 393232 | tf_op jit(solution)/shard_map/reduce_scatter | solution.py:107
  650.1 20.3 %all-gather.71.cloned.1.call-done = bf16[1,3072,256]{2,1,0:T(8,128)(2,1)} async-done(((bf16[1,384,256]{2,1,0:T(8,128)(2,1)}), bf16[1,3072,256]{2,1,0:T(8,128)(2,1)}) %all-gather.71.cloned.1.call-update) | async-done | bytes 1572880 | tf_op jit(solution)/shard_map/all_gather | solution.py:60
  670.5 50.7 %all-gather.47.cloned.1.call-done = bf16[512,3072]{1,0:T(8,128)(2,1)} async-done(((bf16[32,3072]{1,0:T(8,128)(2,1)}), bf16[512,3072]{1,0:T(8,128)(2,1)}) %all-gather.47.cloned.1.call-update) | async-done | bytes 3145744 | tf_op jit(solution)/shard_map/all_gather | solution.py:83
  724.6 21.0 %all-gather.69.cloned.1.call-done = bf16[1,3072,256]{2,1,0:T(8,128)(2,1)} async-done(((bf16[1,384,256]{2,1,0:T(8,128)(2,1)}), bf16[1,3072,256]{2,1,0:T(8,128)(2,1)}) %all-gather.69.cloned.1.call-update) | async-done | bytes 1572880 | tf_op jit(solution)/shard_map/all_gather | solution.py:60
  751.3 20.4 %all-gather.73.cloned.1.call-done = bf16[1,3072,256]{2,1,0:T(8,128)(2,1)} async-done(((bf16[1,384,256]{2,1,0:T(8,128)(2,1)}), bf16[1,3072,256]{2,1,0:T(8,128)(2,1)}) %all-gather.73.cloned.1.call-update) | async-done | bytes 1572880 | tf_op jit(solution)/shard_map/all_gather | solution.py:60
  776.4 22.1 %all-gather.49.cloned.1.call-done = bf16[4096,256]{0,1:T(8,128)(2,1)} async-done(((bf16[512,256]{0,1:T(8,128)(2,1)}), bf16[4096,256]{0,1:T(8,128)(2,1)}) %all-gather.49.cloned.1.call-update) | async-done | bytes 2097168 | tf_op jit(solution)/shard_map/all_gather | solution.py:91
  831.9 21.0 %all-gather.53.cloned.1.call-done = bf16[8,256,384]{2,1,0:T(8,128)(2,1)} async-done(((bf16[1,256,384]{2,1,0:T(8,128)(2,1)}), bf16[8,256,384]{2,1,0:T(8,128)(2,1)}) %all-gather.53.cloned.1.call-update) | async-done | bytes 1572880 | tf_op jit(solution)/shard_map/all_gather | solution.py:63
  873.3 81.2 %reduce-scatter.17.cloned.1.call-done = f32[32,3072]{1,0:T(8,128)} async-done(((f32[512,3072]{1,0:T(8,128)}), f32[32,3072]{1,0:T(8,128)}) %reduce-scatter.17.cloned.1.call-update) | async-done | bytes 393232 | tf_op jit(solution)/shard_map/reduce_scatter | solution.py:97
  959.1 50.8 %all-gather.77.cloned.1.call-done = bf16[1,3072,1536]{2,1,0:T(8,128)(2,1)} async-done(((bf16[1,384,1536]{2,1,0:T(8,128)(2,1)}), bf16[1,3072,1536]{2,1,0:T(8,128)(2,1)}) %all-gather.77.cloned.1.call-update) | async-done | bytes 9437200 | tf_op jit(solution)/shard_map/all_gather | solution.py:60
  1009.8 51.0 %all-gather.55.cloned.1.call-done = bf16[512,3072]{1,0:T(8,128)(2,1)} async-done(((bf16[32,3072]{1,0:T(8,128)(2,1)}), bf16[512,3072]{1,0:T(8,128)(2,1)}) %all-gather.55.cloned.1.call-update) | async-done | bytes 3145744 | tf_op jit(solution)/shard_map/all_gather | solution.py:101
  1071.2 44.3 %all-gather.75.cloned.1.call-done = bf16[1,3072,1536]{2,1,0:T(8,128)(2,1)} async-done(((bf16[1,384,1536]{2,1,0:T(8,128)(2,1)}), bf16[1,3072,1536]{2,1,0:T(8,128)(2,1)}) %all-gather.75.cloned.1.call-update) | async-done | bytes 9437200 | tf_op jit(solution)/shard_map/all_gather | solution.py:60
  1125.7 45.7 %all-gather.57.cloned.1.call-done = bf16[8,1536,384]{2,1,0:T(8,128)(2,1)} async-done(((bf16[1,1536,384]{2,1,0:T(8,128)(2,1)}), bf16[8,1536,384]{2,1,0:T(8,128)(2,1)}) %all-gather.57.cloned.1.call-update) | async-done | bytes 9437200 | tf_op jit(solution)/shard_map/all_gather | solution.py:63
  1196.1 82.4 %reduce-scatter.19.cloned.1.call-done = f32[32,3072]{1,0:T(8,128)} async-done(((f32[512,3072]{1,0:T(8,128)}), f32[32,3072]{1,0:T(8,128)}) %reduce-scatter.19.cloned.1.call-update) | async-done | bytes 393232 | tf_op jit(solution)/shard_map/reduce_scatter | solution.py:107
  1307.5 30.4 %all-gather.79.cloned.1.call-done = bf16[8,512,384]{2,0,1:T(8,128)(2,1)} async-done(((bf16[8,32,384]{2,0,1:T(8,128)(2,1)}), bf16[8,512,384]{2,0,1:T(8,128)(2,1)}) %all-gather.79.cloned.1.call-update) | async-done | bytes 3145744 | tf_op jit(solution)/shard_map/all_gather | solution.py:111
  (204 shorter events, 309.1 us)
Async XLA Ops:
  30.3 82.2 %all-gather.59.cloned.1.call-start = ((), (), s32[]{:S(2)}) async-start(), calls=%async_computation.18 | async-start | bytes 1769472 | tf_op jit(solution)/shard_map/all_gather | solution.py:60
  31.2 107.9 %all-gather.63.cloned.1.call-start = ((), (), s32[]{:S(2)}) async-start(), calls=%async_computation.20 | async-start | bytes 1769472 | tf_op jit(solution)/shard_map/all_gather | solution.py:60
  32.0 134.5 %all-gather.37.cloned.1.call-start = ((), (), s32[]{:S(2)}) async-start(), calls=%async_computation.7 | async-start | bytes 2359296 | tf_op jit(solution)/shard_map/all_gather | solution.py:91
  118.1 76.3 %all-gather.39.cloned.1.call-start = ((), (), s32[]{:S(2)}) async-start(), calls=%async_computation.8 | async-start | bytes 2359296 | tf_op jit(solution)/shard_map/all_gather | solution.py:92
  143.2 78.4 %all-gather.41.cloned.1.call-start = ((), (), s32[]{:S(2)}) async-start(), calls=%async_computation.9 | async-start | bytes 1769472 | tf_op jit(solution)/shard_map/all_gather | solution.py:63
  144.0 178.9 %reduce-scatter.13.cloned.1.call-start = ((), (), s32[]{:S(2)}) async-start(), calls=%async_computation.29 | async-start | bytes 6684672 | tf_op jit(solution)/shard_map/reduce_scatter | solution.py:97
  240.8 137.6 %all-gather.67.cloned.1.call-start = ((), (), s32[]{:S(2)}) async-start(), calls=%async_computation.22 | async-start | bytes 10616832 | tf_op jit(solution)/shard_map/all_gather | solution.py:60
  244.0 184.6 %all-gather.43.cloned.1.call-start = ((), (), s32[]{:S(2)}) async-start(), calls=%async_computation.10 | async-start | bytes 3342336 | tf_op jit(solution)/shard_map/all_gather | solution.py:101
  326.1 156.7 %all-gather.65.cloned.1.call-start = ((), (), s32[]{:S(2)}) async-start(), calls=%async_computation.21 | async-start | bytes 10616832 | tf_op jit(solution)/shard_map/all_gather | solution.py:60
  327.8 210.8 %all-gather.45.cloned.1.call-start = ((), (), s32[]{:S(2)}) async-start(), calls=%async_computation.11 | async-start | bytes 10616832 | tf_op jit(solution)/shard_map/all_gather | solution.py:63
  331.2 314.3 %reduce-scatter.15.cloned.1.call-start = ((), (), s32[]{:S(2)}) async-start(), calls=%async_computation.30 | async-start | bytes 6684672 | tf_op jit(solution)/shard_map/reduce_scatter | solution.py:107
  563.3 107.2 %all-gather.71.cloned.1.call-start = ((), (), s32[]{:S(2)}) async-start(), calls=%async_computation.24 | async-start | bytes 1769472 | tf_op jit(solution)/shard_map/all_gather | solution.py:60
  563.9 157.3 %all-gather.47.cloned.1.call-start = ((), (), s32[]{:S(2)}) async-start(), calls=%async_computation.12 | async-start | bytes 3342336 | tf_op jit(solution)/shard_map/all_gather | solution.py:83
  648.7 96.9 %all-gather.69.cloned.1.call-start = ((), (), s32[]{:S(2)}) async-start(), calls=%async_computation.23 | async-start | bytes 1769472 | tf_op jit(solution)/shard_map/all_gather | solution.py:60
  649.3 122.4 %all-gather.73.cloned.1.call-start = ((), (), s32[]{:S(2)}) async-start(), calls=%async_computation.25 | async-start | bytes 1769472 | tf_op jit(solution)/shard_map/all_gather | solution.py:60
  649.9 148.6 %all-gather.49.cloned.1.call-start = ((), (), s32[]{:S(2)}) async-start(), calls=%async_computation.13 | async-start | bytes 2359296 | tf_op jit(solution)/shard_map/all_gather | solution.py:91
  775.7 77.2 %all-gather.53.cloned.1.call-start = ((), (), s32[]{:S(2)}) async-start(), calls=%async_computation.15 | async-start | bytes 1769472 | tf_op jit(solution)/shard_map/all_gather | solution.py:63
  776.3 178.1 %reduce-scatter.17.cloned.1.call-start = ((), (), s32[]{:S(2)}) async-start(), calls=%async_computation.31 | async-start | bytes 6684672 | tf_op jit(solution)/shard_map/reduce_scatter | solution.py:97
  872.2 137.6 %all-gather.77.cloned.1.call-start = ((), (), s32[]{:S(2)}) async-start(), calls=%async_computation.27 | async-start | bytes 10616832 | tf_op jit(solution)/shard_map/all_gather | solution.py:60
  873.0 187.8 %all-gather.55.cloned.1.call-start = ((), (), s32[]{:S(2)}) async-start(), calls=%async_computation.16 | async-start | bytes 3342336 | tf_op jit(solution)/shard_map/all_gather | solution.py:101
  957.7 157.8 %all-gather.75.cloned.1.call-start = ((), (), s32[]{:S(2)}) async-start(), calls=%async_computation.26 | async-start | bytes 10616832 | tf_op jit(solution)/shard_map/all_gather | solution.py:60
  958.3 213.1 %all-gather.57.cloned.1.call-start = ((), (), s32[]{:S(2)}) async-start(), calls=%async_computation.17 | async-start | bytes 10616832 | tf_op jit(solution)/shard_map/all_gather | solution.py:63
  959.0 319.5 %reduce-scatter.19.cloned.1.call-start = ((), (), s32[]{:S(2)}) async-start(), calls=%async_computation.32 | async-start | bytes 6684672 | tf_op jit(solution)/shard_map/reduce_scatter | solution.py:107
  1196.1 141.8 %all-gather.79.cloned.1.call-start = ((), (), s32[]{:S(2)}) async-start(), calls=%async_computation.28 | async-start | bytes 3342336 | tf_op jit(solution)/shard_map/all_gather | solution.py:111
  (22 other events, 684.6 us)
Sparse Core Ops, SparseCore 0:
  10.3 26.7 all-gather.60
  39.8 48.0 all-gather.34
  114.6 24.4 all-gather.62
  141.2 25.2 all-gather.36
  168.6 25.6 all-gather.38
  196.6 24.8 all-gather.40
  240.9 81.9 reduce-scatter.12
  325.2 53.1 all-gather.66
  380.4 48.2 all-gather.42
  430.3 52.4 all-gather.64
  484.4 54.2 all-gather.44
  563.4 82.0 reduce-scatter.14
  673.0 48.1 all-gather.46
  747.2 24.4 all-gather.72
  773.2 25.2 all-gather.48
  800.8 25.6 all-gather.50
  828.0 24.8 all-gather.52
  872.3 82.0 reduce-scatter.16
  956.7 53.0 all-gather.76
  1012.6 48.2 all-gather.54
  1062.9 52.4 all-gather.74
  1117.2 54.2 all-gather.56
  1196.2 82.2 reduce-scatter.18
  1292.6 45.3 all-gather.78
  (3 shorter events, 69.0 us)

commit v2 on v1

v2 whole, which is shorter than its diff:
```python
import functools

import jax
import jax.numpy as jnp
from jax import lax
from jax.experimental import pallas as pl
from jax.experimental.pallas import tpu as pltpu
from jax.sharding import PartitionSpec as P

NORM_EPS = 1e-6
WINDOW = 1024
GLOBAL_BASE = 1000000.0
GLOBAL_FACTOR = 8.0
LOCAL_BASE = 10000.0
MESH = pl.DeviceIdType.MESH
SIDE = 4
COLORS = 4
VMEM_LIMIT = 60 * 1024 * 1024


def norm(values, scale_row):
    mean_sq = jnp.mean(values * values, axis=-1, keepdims=True)
    return values * lax.rsqrt(mean_sq + NORM_EPS) * (1.0 + scale_row)


def rope_tables(positions, head_dim, rope_base, pos_factor):
    exponents = jnp.arange(0, head_dim, 2).astype(jnp.float32) / head_dim
    inv_freq = rope_base ** (-exponents)
    angles = (positions.astype(jnp.float32) / pos_factor)[:, None] * inv_freq[None, :]
    return jnp.cos(angles), jnp.sin(angles)


def apply_rope(values, cos_tab, sin_tab):
    half_dim = values.shape[-1] // 2
    first_half = values[..., :half_dim]
    second_half = values[..., half_dim:]
    return jnp.concatenate([first_half * cos_tab - second_half * sin_tab, second_half * cos_tab + first_half * sin_tab], axis=-1)


def attend(q, k, v, seg_q, pos_q, seg_ids, positions, window):
    scores = jnp.dot(q, k.T, preferred_element_type=jnp.float32) * (q.shape[-1] ** -0.5)
    gap = pos_q[:, None] - positions[None, :]
    allowed = (seg_q[:, None] == seg_ids[None, :]) & (gap >= 0) & (gap < window)
    scores = jnp.where(allowed, scores, -1e30)
    row_max = jnp.max(scores, axis=-1, keepdims=True)
    e = jnp.exp(scores - row_max)
    p = (e / jnp.sum(e, axis=-1, keepdims=True)).astype(jnp.bfloat16)
    return jnp.dot(p, v, preferred_element_type=jnp.float32).astype(jnp.bfloat16)


def wrap(i):
    return lax.rem(i + 2 * SIDE, SIDE)


class Torus:
    def __init__(self):
        me = lax.axis_index('heads')
        self.z = me // SIDE
        self.y = lax.rem(me, SIDE)

    def own(self, axis):
        return self.y if axis == 0 else self.z

    def block(self, axis, along, across):
        return across * SIDE + along if axis == 0 else along * SIDE + across

    def peer(self, axis, step):
        moved = wrap(self.own(axis) + step)
        return self.block(axis, moved, self.own(1 - axis))

    def meet(self):
        barrier = pltpu.get_barrier_semaphore()
        for axis in (0, 1):
            for step in (1, -1):
                pl.semaphore_signal(barrier, inc=1, device_id={'heads': self.peer(axis, step)}, device_id_type=MESH)
        pl.semaphore_wait(barrier, 4)


def gather_blocks(torus, h_ref, send1, recv1, send2, recv2):
    rows = h_ref.shape[0] // (SIDE * SIDE)
    cols = h_ref.shape[1] // COLORS

    def view(q, axis, along, across):
        b = torus.block(axis, along, across)
        return h_ref.at[pl.ds(pl.multiple_of(b * rows, rows), rows), pl.ds(q * cols, cols)]

    def hop1(q, s):
        axis, d = q // 2, 1 - 2 * (q % 2)
        i, j = torus.own(axis), torus.own(1 - axis)
        v = view(q, axis, i, wrap(j - d * s))
        return pltpu.make_async_remote_copy(v, v, send1.at[q, s], recv1.at[q, s], device_id={'heads': torus.peer(1 - axis, d)}, device_id_type=MESH)

    def hop2(q, t, n):
        axis, d = q // 2, 1 - 2 * (q % 2)
        i, j = torus.own(axis), torus.own(1 - axis)
        v = view(q, axis, wrap(i - d * t), wrap(j - d * n))
        return pltpu.make_async_remote_copy(v, v, send2.at[q, t, n], recv2.at[q, t, n], device_id={'heads': torus.peer(axis, d)}, device_id_type=MESH)

    for q in range(COLORS):
        hop1(q, 0).start()
    for q in range(COLORS):
        hop2(q, 0, 0).start()
    for s in range(SIDE - 1):
        for q in range(COLORS):
            hop1(q, s).wait_recv()
            if s < SIDE - 2:
                hop1(q, s + 1).start()
            hop2(q, 0, s + 1).start()
    for t in range(SIDE - 1):
        for n in range(SIDE):
            for q in range(COLORS):
                hop2(q, t, n).wait_recv()
                if t < SIDE - 2:
                    hop2(q, t + 1, n).start()
    for q in range(COLORS):
        for s in range(SIDE - 1):
            hop1(q, s).wait_send()
            for n in range(SIDE):
                hop2(q, s, n).wait_send()


GATHER_SEMS = [pltpu.SemaphoreType.DMA((COLORS, SIDE - 1)), pltpu.SemaphoreType.DMA((COLORS, SIDE - 1)),
               pltpu.SemaphoreType.DMA((COLORS, SIDE - 1, SIDE)), pltpu.SemaphoreType.DMA((COLORS, SIDE - 1, SIDE))]


def gather_kernel(x_ref, h_ref, send1, recv1, send2, recv2):
    torus = Torus()
    rows = x_ref.shape[0]
    torus.meet()
    mine = torus.block(0, torus.y, torus.z)
    h_ref[pl.ds(pl.multiple_of(mine * rows, rows), rows), :] = x_ref[...]
    gather_blocks(torus, h_ref, send1, recv1, send2, recv2)


def all_gather_heads(x, cid):
    rows, width = x.shape
    vmem = pl.BlockSpec(memory_space=pltpu.VMEM)
    return pl.pallas_call(
        gather_kernel,
        out_shape=jax.ShapeDtypeStruct((rows * SIDE * SIDE, width), x.dtype),
        in_specs=[vmem], out_specs=vmem,
        scratch_shapes=list(GATHER_SEMS),
        compiler_params=pltpu.CompilerParams(collective_id=cid, has_side_effects=True, vmem_limit_bytes=VMEM_LIMIT),
        cost_estimate=pl.CostEstimate(flops=20_000_000_000, bytes_accessed=4_000_000, transcendentals=0),
        name='gather_heads',
    )(x)


def project_kernel(transposed, gather, a_ref, w_ref, res_ref, sa_ref, sb_ref, x_ref, h_ref,
                   first, slots1, slots2, s1, r1, s2, r2, gs1=None, gr1=None, gs2=None, gr2=None):
    torus = Torus()
    rows = res_ref.shape[0]
    cols = slots1.shape[-1]
    torus.meet()

    def ring1(q, s, n):
        axis, d = q // 2, 1 - 2 * (q % 2)
        src = first.at[q, n] if s == 0 else slots1.at[q, s - 1, n]
        return pltpu.make_async_remote_copy(src, slots1.at[q, s, n], s1.at[q, s, n], r1.at[q, s, n],
                                            device_id={'heads': torus.peer(axis, d)}, device_id_type=MESH)

    def ring2(q, t):
        axis, d = q // 2, 1 - 2 * (q % 2)
        src = slots1.at[q, SIDE - 2, 0] if t == 0 else slots2.at[q, t - 1]
        return pltpu.make_async_remote_copy(src, slots2.at[q, t], s2.at[q, t], r2.at[q, t],
                                            device_id={'heads': torus.peer(1 - axis, d)}, device_id_type=MESH)

    def product(q, s):
        axis, d = q // 2, 1 - 2 * (q % 2)
        along = wrap(torus.own(axis) - d * (1 + s))
        parts = []
        for n in range(SIDE):
            b = torus.block(axis, along, wrap(torus.own(1 - axis) - d * (1 + n)))
            parts.append(a_ref[pl.ds(pl.multiple_of(b * rows, rows), rows), :])
        lhs = jnp.concatenate(parts, axis=0)
        if transposed:
            return [lax.dot_general(lhs, w_ref[q * cols:(q + 1) * cols, :], (((1,), (1,)), ((), ())), preferred_element_type=jnp.float32)]
        per = cols // w_ref.shape[2]
        return [jnp.dot(lhs, w_ref[q * per + p], preferred_element_type=jnp.float32) for p in range(per)]

    for s in range(SIDE):
        for q in range(COLORS):
            pieces = product(q, s)
            for n in range(SIDE):
                if s > 0:
                    ring1(q, s - 1, n).wait_recv()
                at = 0
                for piece in pieces:
                    part = piece[n * rows:(n + 1) * rows]
                    span = slice(at, at + part.shape[1])
                    at += part.shape[1]
                    if s == 0:
                        first[q, n, :, span] = part
                    else:
                        slots1[q, s - 1, n, :, span] += part
                if s < SIDE - 1:
                    ring1(q, s, n).start()
                elif n == 0:
                    ring2(q, 0).start()
    for t in range(SIDE - 1):
        for q in range(COLORS):
            ring2(q, t).wait_recv()
            slots2[q, t] += slots1[q, SIDE - 2, t + 1]
            if t < SIDE - 2:
                ring2(q, t + 1).start()
    total = jnp.concatenate([slots2[q, SIDE - 2] for q in range(COLORS)], axis=1)
    out = total.astype(jnp.bfloat16).astype(jnp.float32)
    x_new = (res_ref[...].astype(jnp.float32) + norm(out, sa_ref[...])).astype(jnp.bfloat16)
    x_ref[...] = x_new
    if gather:
        mine = torus.block(0, torus.y, torus.z)
        h_ref[pl.ds(pl.multiple_of(mine * rows, rows), rows), :] = norm(x_new.astype(jnp.float32), sb_ref[...]).astype(jnp.bfloat16)
    for q in range(COLORS):
        for s in range(SIDE - 1):
            ring2(q, s).wait_send()
            for n in range(SIDE):
                ring1(q, s, n).wait_send()
    if gather:
        gather_blocks(torus, h_ref, gs1, gr1, gs2, gr2)


def project(a, w, resid, scale_a, scale_b, cid, transposed, gather):
    rows, width = resid.shape
    cols = width // COLORS
    vmem = pl.BlockSpec(memory_space=pltpu.VMEM)
    ring_sems = [pltpu.SemaphoreType.DMA((COLORS, SIDE - 1, SIDE)), pltpu.SemaphoreType.DMA((COLORS, SIDE - 1, SIDE)),
                 pltpu.SemaphoreType.DMA((COLORS, SIDE - 1)), pltpu.SemaphoreType.DMA((COLORS, SIDE - 1))]
    scratch = [pltpu.VMEM((COLORS, SIDE, rows, cols), jnp.float32),
               pltpu.VMEM((COLORS, SIDE - 1, SIDE, rows, cols), jnp.float32),
               pltpu.VMEM((COLORS, SIDE - 1, rows, cols), jnp.float32)] + ring_sems
    x_shape = jax.ShapeDtypeStruct((rows, width), jnp.bfloat16)
    h_shape = jax.ShapeDtypeStruct((rows * SIDE * SIDE, width), jnp.bfloat16)
    if gather:
        kernel = functools.partial(project_kernel, transposed, True)
        out_shape, out_specs, scratch = (x_shape, h_shape), (vmem, vmem), scratch + GATHER_SEMS
    else:
        def kernel(a_ref, w_ref, res_ref, sa_ref, sb_ref, x_ref, *rest):
            project_kernel(transposed, False, a_ref, w_ref, res_ref, sa_ref, sb_ref, x_ref, None, *rest)
        out_shape, out_specs = x_shape, vmem
    return pl.pallas_call(
        kernel, out_shape=out_shape, in_specs=[vmem] * 5, out_specs=out_specs, scratch_shapes=scratch,
        compiler_params=pltpu.CompilerParams(collective_id=cid, has_side_effects=True, vmem_limit_bytes=VMEM_LIMIT),
        cost_estimate=pl.CostEstimate(flops=50_000_000_000, bytes_accessed=20_000_000, transcendentals=0),
        name='project_reduce',
    )(a, w, resid, scale_a, scale_b)


def exchange_kernel(n_chips, k_ref, v_ref, ka_ref, va_ref, send, recv):
    md = lax.axis_index('model')
    chip, core = md // 2, lax.rem(md, 2)
    right = lax.rem(chip + 1, n_chips) * 2 + core
    left = lax.rem(chip + n_chips - 1, n_chips) * 2 + core
    mate = chip * 2 + 1 - core
    rows = k_ref.shape[0]
    half = rows // 2
    barrier = pltpu.get_barrier_semaphore()
    for other in (right, left, mate):
        pl.semaphore_signal(barrier, inc=1, device_id={'model': other}, device_id_type=MESH)
    pl.semaphore_wait(barrier, 3)
    refs = (ka_ref, va_ref)
    here = pl.ds(pl.multiple_of(md * rows, rows), rows)
    ka_ref[here, :] = k_ref[...]
    va_ref[here, :] = v_ref[...]

    def copy(a, slot, owner, to, part):
        start = owner * rows if part != 2 else owner * rows + half
        size = rows if part == 0 else half
        v = refs[a].at[pl.ds(pl.multiple_of(start, half), size), :]
        return pltpu.make_async_remote_copy(v, v, send.at[a, slot], recv.at[a, slot], device_id={'model': to}, device_id_type=MESH)

    far = lax.rem(chip + 2, n_chips) * 2 + core
    plan = [(0, md, right, 0), (1, md, left, 0), (2, md, mate, 0), (3, left, right, 1), (4, right, left, 2),
            (5, left, mate, 0), (6, right, mate, 0), (7, far, mate, 1), (8, far, mate, 2)]
    for slot in (0, 1, 2):
        for a in (0, 1):
            copy(a, *plan[slot]).start()
    for a in (0, 1):
        copy(a, *plan[0]).wait_recv()
        copy(a, *plan[3]).start()
        copy(a, *plan[1]).wait_recv()
        copy(a, *plan[4]).start()
        copy(a, *plan[5]).start()
        copy(a, *plan[6]).start()
    for a in (0, 1):
        copy(a, *plan[3]).wait_recv()
        copy(a, *plan[7]).start()
        copy(a, *plan[4]).wait_recv()
        copy(a, *plan[8]).start()
    for a in (0, 1):
        for slot in (2, 5, 6, 7, 8):
            copy(a, *plan[slot]).wait_recv()
        for slot in range(9):
            copy(a, *plan[slot]).wait_send()


def exchange(k, v, n_model, cid):
    rows, dim = k.shape
    vmem = pl.BlockSpec(memory_space=pltpu.VMEM)
    full = jax.ShapeDtypeStruct((rows * n_model, dim), k.dtype)
    return pl.pallas_call(
        functools.partial(exchange_kernel, n_model // 2),
        out_shape=(full, full), in_specs=[vmem] * 2, out_specs=(vmem, vmem),
        scratch_shapes=[pltpu.SemaphoreType.DMA((2, 9)), pltpu.SemaphoreType.DMA((2, 9))],
        compiler_params=pltpu.CompilerParams(collective_id=cid, has_side_effects=True, vmem_limit_bytes=VMEM_LIMIT),
        cost_estimate=pl.CostEstimate(flops=20_000_000_000, bytes_accessed=5_000_000, transcendentals=0),
        name='exchange_kv',
    )(k, v)


def solution(mesh):
    n_model = mesh.shape['model']
    n_heads = mesh.shape['heads']
    col_spec = P(None, 'model', 'heads')
    row_spec = P(None, 'heads', 'model')
    cache_spec = P(None, None, 'heads', None)

    def body(hidden_in, seg_ids, positions, w_query, w_key, w_value, w_out, w_gate, w_up, w_down, norm_scales, qk_scales):
        n_tok, width_loc = hidden_in.shape
        width = width_loc * n_model
        head_dim = qk_scales.shape[-1]
        tok_m = n_tok // n_model
        tok_own = tok_m // n_heads
        hd = lax.axis_index('heads')
        md = lax.axis_index('model')

        attn_w, gate_w, up_w, down_w = [], [], [], []
        for l in range(2):
            packed = jnp.concatenate([w_query[l], w_key[l], w_value[l], w_out[l].T], axis=1)
            attn_w.append(lax.all_gather(packed, 'model', axis=0, tiled=True))
            gate_w.append(lax.all_gather(w_gate[l], 'model', axis=0, tiled=True))
            up_w.append(lax.all_gather(w_up[l], 'model', axis=0, tiled=True))
            down_w.append(lax.all_gather(w_down[l], 'model', axis=0))

        scales = lax.all_gather(norm_scales, 'model', axis=2, tiled=True)
        mine = lax.dynamic_index_in_dim(hidden_in.reshape(n_model, n_heads, tok_own, width_loc), hd, 1, keepdims=False)
        mine = lax.all_to_all(mine, 'model', split_axis=0, concat_axis=0)
        resid = mine.transpose(1, 0, 2).reshape(tok_own, width)

        pos_m = lax.dynamic_slice_in_dim(positions, md * tok_m, tok_m)
        seg_m = lax.dynamic_slice_in_dim(seg_ids, md * tok_m, tok_m)

        settings = ((GLOBAL_BASE, GLOBAL_FACTOR, n_tok), (LOCAL_BASE, 1.0, WINDOW))
        keys, values = [], []
        h = all_gather_heads(norm(resid.astype(jnp.float32), scales[0, 0]).astype(jnp.bfloat16), 0)
        for l in range(2):
            rope_base, pos_factor, window = settings[l]
            wa = attn_w[l]
            qkv = jnp.dot(h, wa[:, :3 * head_dim], preferred_element_type=jnp.float32).astype(jnp.bfloat16)
            q, k, v = qkv[:, :head_dim], qkv[:, head_dim:2 * head_dim], qkv[:, 2 * head_dim:]
            cos_tab, sin_tab = rope_tables(pos_m, head_dim, rope_base, pos_factor)
            q = apply_rope(norm(q.astype(jnp.float32), qk_scales[l, 0]), cos_tab, sin_tab).astype(jnp.bfloat16)
            k = apply_rope(norm(k.astype(jnp.float32), qk_scales[l, 1]), cos_tab, sin_tab).astype(jnp.bfloat16)
            k_all, v_all = exchange(k, v, n_model, 1 + 3 * l)
            keys.append(k_all[:, None, :])
            values.append(v_all[:, None, :])
            o = attend(q, k_all, v_all, seg_m, pos_m, seg_ids, positions, window)
            x1, h2 = project(o, wa[:, 3 * head_dim:], resid, scales[l, 1:2], scales[l, 2:3], 2 + 3 * l, True, True)
            g = jnp.dot(h2, gate_w[l], preferred_element_type=jnp.float32).astype(jnp.bfloat16)
            u = jnp.dot(h2, up_w[l], preferred_element_type=jnp.float32).astype(jnp.bfloat16)
            mid = (jax.nn.gelu(g.astype(jnp.float32), approximate=True) * u.astype(jnp.float32)).astype(jnp.bfloat16)
            if l == 0:
                resid, h = project(mid, down_w[l], x1, scales[0, 3:4], scales[1, 0:1], 3 + 3 * l, False, True)
            else:
                resid = project(mid, down_w[l], x1, scales[1, 3:4], scales[1, 3:4], 3 + 3 * l, False, False)
        out = resid.reshape(tok_own, n_model, width_loc).transpose(1, 0, 2)
        out = lax.all_to_all(out, 'model', split_axis=0, concat_axis=0)
        out = all_gather_heads(out.transpose(1, 0, 2).reshape(tok_own, width), 7)
        out = out.reshape(tok_m, n_model, width_loc).transpose(1, 0, 2).reshape(n_tok, width_loc)
        return out, jnp.stack(keys), jnp.stack(values)

    return jax.shard_map(body, mesh=mesh,
                         in_specs=(P(None, 'model'), P(), P(), col_spec, col_spec, col_spec, row_spec, col_spec, col_spec, row_spec, P(None, None, 'model'), P()),
                         out_specs=(P(None, 'model'), cache_spec, cache_spec),
                         check_vma=False)
```

time: 1350 us -> 623 us (0.46)
  waiting for transfers between devices: 1070 us -> 45.1 us
  Pallas kernels: 0 us -> 412 us
  matrix products: 145 us -> 67.6 us
  local copies, waits for them, and re-layouts: 57.2 us -> 33.5 us
    all_gather x23 -> x8, waiting for transfers between devices: 743 us -> 43.1 us  [the longest x2 43 us: body(): down_w.append(lax.all_gather(w_down[l], 'model', axis=0))]
    pallas_call x0 -> x8, Pallas kernels: none -> 412 us  [the longest x4 281 us: project(): pl.pallas_call(kernel, out_shape=out_shape, in_specs=[vmem] * 5, out_spec...]
    reduce_scatter x4 -> x0, waiting for transfers between devices: 324 us -> none  [the longest x2 164 us: body(): lax.psum_scatter(dot_cols(mid, wd), 'heads', scatter_dimension=0, tiled=T...]
    dot_general x42 -> x6, matrix products: 124 us -> 53.1 us  [the longest x2 21.6 us: body(): jnp.dot(h2, gate_w[l], preferred_element_type=jnp.float32)]
    unnamed x41 -> x49, local copies, waits for them, and re-layouts: 41 us -> 6.84 us
  transfers between devices with their start and end apart: 28 -> 10, of which waited for: 27 -> 1; matrix products, arithmetic and copies ran while one was open for 9% -> 17% of each run, Pallas kernels for 0% -> 54%
where the time goes in v2:
time: 623 us; the launch traced here: 617 us
  Pallas kernels  412 us (66%)
  matrix products  67.6 us (11%)
  waiting for transfers between devices  45.1 us (7%)
  local copies, waits for them, and re-layouts  33.5 us (5%)
  other arithmetic  22.1 us (4%)
  between operations  14.8 us (2%)
  blocking collectives  14 us (2%)
  starting transfers between devices  8.64 us (1%)
    pallas_call x4, Pallas kernels, project(): pl.pallas_call(kernel, out_shape=out_shape, in_specs=[vmem] * 5, out_spec...  281 us
    pallas_call x2, Pallas kernels, exchange(): pl.pallas_call(functools.partial(exchange_kernel, n_model // 2), out_shap...  68.7 us
    pallas_call x2, Pallas kernels, all_gather_heads(): pl.pallas_call(gather_kernel, out_shape=jax.ShapeDtypeStruct((rows * SIDE...  61.5 us
    all_gather x2, waiting for transfers between devices, body(): down_w.append(lax.all_gather(w_down[l], 'model', axis=0))  43 us
    dot_general x2, matrix products, body(): jnp.dot(h2, gate_w[l], preferred_element_type=jnp.float32)  21.6 us
    dot_general x2, matrix products, body(): jnp.dot(h2, up_w[l], preferred_element_type=jnp.float32)  19.5 us
    all_gather x1, blocking collectives, body(): scales = lax.all_gather(norm_scales, 'model', axis=2, tiled=True)  14 us
  transfers between devices with their start and end apart: 10, of which 1 were waited for; matrix products, arithmetic and copies ran while one was open for 17% of the time, Pallas kernels for 54%

profile of v2, /device:TPU:0, one launch (start us, length us, event | category | flops | bytes accessed | tf_op | source)
XLA Modules:
  0.0 617.3 jit_solution(15490932367754033043)
XLA Ops:
  18.7 3.2 fusion.109
  22.0 3.2 fusion.108
  25.3 3.3 fusion.107
  30.6 4.4 all-to-all-start
  36.9 14.0 %all_gather.27 = f32[2,4,3072]{2,1,0:T(4,128)S(1)} all-gather(f32[2,4,384]{2,1,0:T(4,128)S(1)} %copy-done.7), channel_id=1, replica_groups=mesh['heads'=16,'model'=8] {'model'}, dimensions={2}, use_global_device_ids=true | all-gather | bytes 110592 | tf_op jit(solution)/shard_map/all_gather | solution.py:334
  53.4 32.6 %gather_heads.2 = bf16[512,3072]{1,0:T(8,128)(2,1)} custom-call(bf16[32,3072]{1,0:T(8,128)(2,1)} %multiply_convert_fusion.x_ref), custom_call_target="tpu_custom_call" | custom-call | flops 20000000000 | bytes 4000000 | tf_op jit(solution)/shard_map/gather_heads/pallas_call | solution.py:138
  86.0 5.9 fusion.49
  95.3 27.0 %exchange_kv.2 = (bf16[4096,256]{1,0:T(8,128)(2,1)}, bf16[4096,256]{1,0:T(8,128)(2,1)}) custom-call(bf16[512,256]{1,0:T(8,128)(2,1)} %pad_maximum_fusion.4.k_ref, bf16[512,256]{1,0:T(8,128)(2,1)} %slice.185.v_ref), custom_call_target="tpu_custom_call" | custom-call | flops 20000000000 | bytes 5000000 | tf_op jit(solution)/shard_map/exchange_kv/pallas_call | solution.py:300
  122.4 4.7 fusion.111
  133.9 77.1 %project_reduce.4 = (bf16[32,3072]{1,0:T(8,128)(2,1)}, bf16[512,3072]{1,0:T(8,128)(2,1)}) custom-call(bf16[512,256]{1,0:T(8,128)(2,1)} %fusion.56.a_ref, bf16[3072,256]{1,0:T(8,128)(2,1)} %slice.186.w_ref, bf16[32,3072]{1,0:T(8,128)(2,1)} %bitcast.111, f32[1,3072]{1,0:T(1,128)} %get-tuple-element.61.sa_ref, f32[1,3072]{1,0:T(1,128)} %get-tuple-element.60.sb_ref), custom_call_target="tpu_custom_call" | custom-call | flops 49999998976 | bytes 20000000 | tf_op jit(solution)/shard_map/project_reduce/pallas_call | solution.py:240
  213.9 8.9 %fusion.38 = bf16[512,1536]{1,0:T(8,128)(2,1)} fusion(bf16[512,3072]{1,0:T(8,128)(2,1)S(1)} %copy-done.21, bf16[1,3072,1536]{2,1,0:T(8,128)(2,1)} %all-gather.23.cloned.1.call-done), kind=kOutput, calls=%fused_computation.53 | convolution fusion | flops 4832624640 | bytes 14155776 | tf_op jit(solution)/shard_map/dot_general | solution.py:359
  222.7 11.0 %fusion.25.a_ref = bf16[512,1536]{1,0:T(8,128)(2,1)} fusion(bf16[512,1536]{1,0:T(8,128)(2,1)} %fusion.38, bf16[512,3072]{1,0:T(8,128)(2,1)S(1)} %copy-done.21, bf16[1,3072,1536]{2,1,0:T(8,128)(2,1)} %all-gather.21.cloned.1.call-done), kind=kOutput, calls=%fused_computation.44 | convolution fusion | flops 4842061824 | bytes 15728640 | tf_op jit(solution)/shard_map/dot_general | solution.py:358
  233.7 43.0 %all-gather.15.cloned.1.call-done.w_ref = bf16[8,1536,384]{2,1,0:T(8,128)(2,1)} async-done(((bf16[1,1536,384]{2,1,0:T(8,128)(2,1)}), bf16[8,1536,384]{2,1,0:T(8,128)(2,1)}) %all-gather.15.cloned.1.call-update) | async-done | bytes 9437200 | tf_op jit(solution)/shard_map/all_gather | solution.py:332
  276.8 80.1 %project_reduce.5 = (bf16[32,3072]{1,0:T(8,128)(2,1)}, bf16[512,3072]{1,0:T(8,128)(2,1)}) custom-call(bf16[512,1536]{1,0:T(8,128)(2,1)} %fusion.25.a_ref, bf16[8,1536,384]{2,1,0:T(8,128)(2,1)} %all-gather.15.cloned.1.call-done.w_ref, bf16[32,3072]{1,0:T(8,128)(2,1)} %get-tuple-element.16.res_ref, f32[1,3072]{1,0:T(1,128)} %get-tuple-element.59.sa_ref, ...), custom_call_target="tpu_custom_call" | custom-call | flops 49999998976 | bytes 20000000 | tf_op jit(solution)/shard_map/project_reduce/pallas_call | solution.py:240
  357.0 6.1 fusion.52
  366.3 41.7 %exchange_kv.3 = (bf16[4096,256]{1,0:T(8,128)(2,1)}, bf16[4096,256]{1,0:T(8,128)(2,1)}) custom-call(bf16[512,256]{1,0:T(8,128)(2,1)} %pad_maximum_fusion.5.k_ref, bf16[512,256]{1,0:T(8,128)(2,1)} %slice.198.v_ref), custom_call_target="tpu_custom_call" | custom-call | flops 20000000000 | bytes 5000000 | tf_op jit(solution)/shard_map/exchange_kv/pallas_call | solution.py:300
  408.0 4.7 fusion.112
  416.9 75.4 %project_reduce.6 = (bf16[32,3072]{1,0:T(8,128)(2,1)}, bf16[512,3072]{1,0:T(8,128)(2,1)}) custom-call(bf16[512,256]{1,0:T(8,128)(2,1)} %fusion.55.a_ref, bf16[3072,256]{1,0:T(8,128)(2,1)} %slice.199.w_ref, bf16[32,3072]{1,0:T(8,128)(2,1)} %get-tuple-element.20.res_ref, f32[1,3072]{1,0:T(1,128)} %get-tuple-element.57.sa_ref, f32[1,3072]{1,0:T(1,128)} %get-tuple-element.56.sb_ref), custom_call_target="tpu_custom_call" | custom-call | flops 49999998976 | bytes 20000000 | tf_op jit(solution)/shard_map/project_reduce/pallas_call | solution.py:240
  492.3 10.6 %fusion.46 = bf16[512,1536]{1,0:T(8,128)(2,1)} fusion(bf16[512,3072]{1,0:T(8,128)(2,1)} %get-tuple-element.21, bf16[1,3072,1536]{2,1,0:T(8,128)(2,1)} %all-gather.27.cloned.1.call-done), kind=kOutput, calls=%fused_computation.55 | convolution fusion | flops 4832624640 | bytes 14155776 | tf_op jit(solution)/shard_map/dot_general | solution.py:359
  502.9 10.6 %fusion.32.a_ref = bf16[512,1536]{1,0:T(8,128)(2,1)} fusion(bf16[512,1536]{1,0:T(8,128)(2,1)} %fusion.46, bf16[512,3072]{1,0:T(8,128)(2,1)S(1)} %copy-done.22, bf16[1,3072,1536]{2,1,0:T(8,128)(2,1)} %all-gather.25.cloned.1.call-done), kind=kOutput, calls=%fused_computation.51 | convolution fusion | flops 4842061824 | bytes 15728640 | tf_op jit(solution)/shard_map/dot_general | solution.py:358
  513.6 48.7 %project_reduce.7 = bf16[32,3072]{1,0:T(8,128)(2,1)} custom-call(bf16[512,1536]{1,0:T(8,128)(2,1)} %fusion.32.a_ref, bf16[8,1536,384]{2,1,0:T(8,128)(2,1)} %all-gather.19.cloned.1.call-done.w_ref, bf16[32,3072]{1,0:T(8,128)(2,1)} %get-tuple-element.22.res_ref, f32[1,3072]{1,0:T(1,128)} %get-tuple-element.55.sa_ref.sb_ref, ...), custom_call_target="tpu_custom_call" | custom-call | flops 49999998976 | bytes 20000000 | tf_op jit(solution)/shard_map/project_reduce/pallas_call | solution.py:240
  563.9 3.9 all-to-all-start.1
  567.8 4.8 pad_maximum_fusion
  575.7 28.9 %gather_heads.3 = bf16[512,3072]{1,0:T(8,128)(2,1)} custom-call(bf16[32,3072]{1,0:T(8,128)(2,1)} %bitcast.114), custom_call_target="tpu_custom_call" | custom-call | flops 20000000000 | bytes 4000000 | tf_op jit(solution)/shard_map/gather_heads/pallas_call | solution.py:138
  (115 shorter events, 48.7 us)
Async XLA Ops:
  7.2 22.8 %copy-start = (bf16[4096,384]{1,0:T(8,128)(2,1)S(1)}, bf16[4096,384]{1,0:T(8,128)(2,1)}, u32[]{:S(2)}) copy-start(bf16[4096,384]{1,0:T(8,128)(2,1)} %param.12) | copy-start | bytes 9437188
  7.2 78.8 %all-gather.13.cloned.1.call-start = ((), (), s32[]{:S(2)}) async-start(), calls=%async_computation.2 | async-start | bytes 7077888 | tf_op jit(solution)/shard_map/all_gather | solution.py:329
  14.9 196.2 %all-gather.17.cloned.1.call-start = ((), (), s32[]{:S(2)}) async-start(), calls=%async_computation.4 | async-start | bytes 7077888 | tf_op jit(solution)/shard_map/all_gather | solution.py:329
  18.7 195.2 %all-gather.23.cloned.1.call-start = ((), (), s32[]{:S(2)}) async-start(), calls=%async_computation.7 | async-start | bytes 10616832 | tf_op jit(solution)/shard_map/all_gather | solution.py:331
  21.9 200.8 %all-gather.21.cloned.1.call-start = ((), (), s32[]{:S(2)}) async-start(), calls=%async_computation.6 | async-start | bytes 10616832 | tf_op jit(solution)/shard_map/all_gather | solution.py:330
  25.2 251.6 %all-gather.15.cloned.1.call-start = ((), (), s32[]{:S(2)}) async-start(), calls=%async_computation.3 | async-start | bytes 10616832 | tf_op jit(solution)/shard_map/all_gather | solution.py:332
  28.6 7.8 %copy-start.13 = (f32[2,2,256]{2,1,0:T(2,128)S(1)}, f32[2,2,256]{2,1,0:T(2,128)}, u32[]{:S(2)}) copy-start(f32[2,2,256]{2,1,0:T(2,128)} %param.23) | copy-start | bytes 12292
  28.6 8.4 %copy-start.7 = (f32[2,4,384]{2,1,0:T(4,128)S(1)}, f32[2,4,384]{2,1,0:T(4,128)}, u32[]{:S(2)}) copy-start(f32[2,4,384]{2,1,0:T(4,128)} %param.22) | copy-start | bytes 36868
  28.6 23.1 %copy-start.17 = (s32[4096]{0:T(1024)S(1)}, s32[4096]{0:T(1024)}, u32[]{:S(2)}) copy-start(s32[4096]{0:T(1024)} %param.14) | copy-start | bytes 49156
  28.6 23.7 %copy-start.19 = (s32[4096]{0:T(1024)S(1)}, s32[4096]{0:T(1024)}, u32[]{:S(2)}) copy-start(s32[4096]{0:T(1024)} %param.13) | copy-start | bytes 49156
  28.6 463.7 %all-gather.27.cloned.1.call-start = ((), (), s32[]{:S(2)}) async-start(), calls=%async_computation.9 | async-start | bytes 10616832 | tf_op jit(solution)/shard_map/all_gather | solution.py:331
  29.2 473.7 %all-gather.25.cloned.1.call-start = ((), (), s32[]{:S(2)}) async-start(), calls=%async_computation.8 | async-start | bytes 10616832 | tf_op jit(solution)/shard_map/all_gather | solution.py:330
  30.6 21.7 %all-to-all-start = ((bf16[8,32,384]{2,1,0:T(8,128)(2,1)}), bf16[8,32,384]{2,1,0:T(8,128)(2,1)S(1)}, u32[]{:S(2)}, u32[]{:S(2)}) async-start(bf16[8,32,384]{2,1,0:T(8,128)(2,1)} %dynamic-slice_bitcast_fusion), calls=%async_computation | async-start | bytes 393216 | tf_op jit(solution)/shard_map/all_to_all | solution.py:336
  35.1 478.5 %all-gather.19.cloned.1.call-start = ((), (), s32[]{:S(2)}) async-start(), calls=%async_computation.5 | async-start | bytes 10616832 | tf_op jit(solution)/shard_map/all_gather | solution.py:332
  52.3 70.0 %copy-start.9 = (s32[512]{0:T(512)}, s32[512]{0:T(512)S(1)}, u32[]{:S(2)}) copy-start(s32[512]{0:T(512)S(1)} %get-tuple-element.28) | copy-start | bytes 6148
  52.4 70.0 %copy-start.14 = (s32[512]{0:T(512)}, s32[512]{0:T(512)S(1)}, u32[]{:S(2)}) copy-start(s32[512]{0:T(512)S(1)} %dynamic_slice.10) | copy-start | bytes 6148
  52.4 33.6 %copy-start.6 = (bf16[8,4,8,384]{3,2,0,1:T(8,128)(2,1)}, bf16[8,4,8,384]{3,2,0,1:T(8,128)(2,1)S(1)}, u32[]{:S(2)}) copy-start(bf16[8,4,8,384]{3,2,0,1:T(8,128)(2,1)S(1)} %copy.30) | copy-start | bytes 589828
  356.9 7.3 %copy-start.8 = (f32[512]{0:T(512)S(1)}, f32[512]{0:T(512)}, u32[]{:S(2)}) copy-start(f32[512]{0:T(512)} %get-tuple-element.27) | copy-start | bytes 6148
  366.3 41.7 %copy-start.10 = (s32[512]{0:T(512)S(1)}, s32[512]{0:T(512)}, u32[]{:S(2)}) copy-start(s32[512]{0:T(512)} %copy-done.9) | copy-start | bytes 6148
  366.3 41.7 %copy-start.15 = (s32[512]{0:T(512)S(1)}, s32[512]{0:T(512)}, u32[]{:S(2)}) copy-start(s32[512]{0:T(512)} %copy-done.14) | copy-start | bytes 6148
  366.3 41.7 %copy-start.18 = (s32[4096]{0:T(1024)S(1)}, s32[4096]{0:T(1024)}, u32[]{:S(2)}) copy-start(s32[4096]{0:T(1024)} %param.14) | copy-start | bytes 49156
  366.3 41.7 %copy-start.20 = (s32[4096]{0:T(1024)S(1)}, s32[4096]{0:T(1024)}, u32[]{:S(2)}) copy-start(s32[4096]{0:T(1024)} %param.13) | copy-start | bytes 49156
  492.3 10.6 %copy-start.22 = (bf16[512,3072]{1,0:T(8,128)(2,1)S(1)}, bf16[512,3072]{1,0:T(8,128)(2,1)}, u32[]{:S(2)}) copy-start(bf16[512,3072]{1,0:T(8,128)(2,1)} %get-tuple-element.21) | copy-start | bytes 9437188
  563.9 11.1 %all-to-all-start.1 = ((bf16[8,32,384]{2,1,0:T(8,128)(2,1)}), bf16[8,32,384]{2,1,0:T(8,128)(2,1)S(1)}, u32[]{:S(2)}, u32[]{:S(2)}) async-start(bf16[8,32,384]{2,1,0:T(8,128)(2,1)} %bitcast.98), calls=%async_computation.1 | async-start | bytes 393216 | tf_op jit(solution)/shard_map/all_to_all | solution.py:366
  (9 other events, 40.2 us)
Sparse Core Ops, SparseCore 0:
  15.0 45.6 all-gather.12
  63.0 42.7 all-gather.16
  107.5 57.6 all-gather.22
  166.7 54.2 all-gather.20
  222.5 54.2 all-gather.14
  278.9 54.2 all-gather.26
  334.8 71.1 all-gather.24
  407.7 54.1 all-gather.18

commit v3 on v1

v3 whole, which is shorter than its diff:
```python
import functools

import jax
import jax.numpy as jnp
from jax import lax
from jax.experimental import pallas as pl
from jax.experimental.pallas import tpu as pltpu
from jax.sharding import PartitionSpec as P

NORM_EPS = 1e-6
WINDOW = 1024
GLOBAL_BASE = 1000000.0
GLOBAL_FACTOR = 8.0
LOCAL_BASE = 10000.0
MESH = pl.DeviceIdType.MESH
SIDE = 4
VMEM_LIMIT = 60 * 1024 * 1024


def norm(values, scale_row):
    mean_sq = jnp.mean(values * values, axis=-1, keepdims=True)
    return values * lax.rsqrt(mean_sq + NORM_EPS) * (1.0 + scale_row)


def rope_tables(positions, head_dim, rope_base, pos_factor):
    exponents = jnp.arange(0, head_dim, 2).astype(jnp.float32) / head_dim
    inv_freq = rope_base ** (-exponents)
    angles = (positions.astype(jnp.float32) / pos_factor)[:, None] * inv_freq[None, :]
    return jnp.cos(angles), jnp.sin(angles)


def apply_rope(values, cos_tab, sin_tab):
    half_dim = values.shape[-1] // 2
    first_half = values[..., :half_dim]
    second_half = values[..., half_dim:]
    return jnp.concatenate([first_half * cos_tab - second_half * sin_tab, second_half * cos_tab + first_half * sin_tab], axis=-1)


def attend(q, k, v, seg_q, pos_q, seg_ids, positions, window):
    scores = jnp.dot(q, k.T, preferred_element_type=jnp.float32) * (q.shape[-1] ** -0.5)
    gap = pos_q[:, None] - positions[None, :]
    allowed = (seg_q[:, None] == seg_ids[None, :]) & (gap >= 0) & (gap < window)
    scores = jnp.where(allowed, scores, -1e30)
    row_max = jnp.max(scores, axis=-1, keepdims=True)
    e = jnp.exp(scores - row_max)
    p = (e / jnp.sum(e, axis=-1, keepdims=True)).astype(jnp.bfloat16)
    return jnp.dot(p, v, preferred_element_type=jnp.float32).astype(jnp.bfloat16)


def wrap(i):
    return lax.rem(i + 2 * SIDE, SIDE)


def remote(src, dst, send, recv, to):
    return pltpu.make_async_remote_copy(src, dst, send, recv, device_id=to, device_id_type=MESH)


def row_block(ref, start, size, align):
    return ref.at[pl.ds(pl.multiple_of(start, align), size), :]


class Torus:
    def __init__(self):
        me = lax.axis_index('heads')
        self.own = (lax.rem(me, SIDE), me // SIDE)

    def block(self, axis, along, across):
        return across * SIDE + along if axis == 0 else along * SIDE + across

    def at(self, axis, da, db):
        return self.block(axis, wrap(self.own[axis] + da), wrap(self.own[1 - axis] + db))

    def peer(self, axis, step):
        return {'heads': self.at(axis, step, 0)}


class Line:
    def __init__(self, n_model):
        self.n = n_model
        self.me = lax.axis_index('model')
        chips = n_model // 2
        chip, core = self.me // 2, lax.rem(self.me, 2)
        self.right = lax.rem(chip + 1, chips) * 2 + core
        self.left = lax.rem(chip + chips - 1, chips) * 2 + core
        self.far = lax.rem(chip + 2, chips) * 2 + core
        self.mate = chip * 2 + 1 - core


def meet(torus, models):
    barrier = pltpu.get_barrier_semaphore()
    count = len(models)
    for other in models:
        pl.semaphore_signal(barrier, inc=1, device_id={'model': other}, device_id_type=MESH)
    if torus is not None:
        for axis in (0, 1):
            for step in (1, -1):
                pl.semaphore_signal(barrier, inc=1, device_id=torus.peer(axis, step), device_id_type=MESH)
                count += 1
    pl.semaphore_wait(barrier, count)


def gather_blocks(torus, h_ref, send, recv):
    rows = h_ref.shape[0] // (SIDE * SIDE)
    cols = h_ref.shape[1] // 2
    half = rows // 2

    def view(q, da, db, part):
        start = torus.at(q, da, db) * rows + (half if part == 2 else 0)
        return h_ref.at[pl.ds(pl.multiple_of(start, half), rows if part == 0 else half), pl.ds(q * cols, cols)]

    def ring(q, axis, base, slot, offsets):
        def make(k, da, db, part, step):
            v = view(q, da, db, part)
            return remote(v, v, send.at[q, base, k], recv.at[q, base, k], torus.peer(axis, step))
        along = (lambda off: (off, offsets)) if axis == q else (lambda off: (offsets, off))
        return (make(0, *along(0), 0, 1), make(1, *along(0), 0, -1), make(2, *along(-1), 1, 1), make(3, *along(1), 2, -1))

    first = [ring(q, 1 - q, 0, 0, 0) for q in (0, 1)]
    second = [[ring(q, q, 1 + n, 0, off) for n, off in enumerate((0, -1, 1, 2))] for q in (0, 1)]

    def begin(copies):
        copies[0].start()
        copies[1].start()

    def onward(copies):
        copies[0].wait_recv()
        copies[2].start()
        copies[1].wait_recv()
        copies[3].start()

    for q in (0, 1):
        begin(first[q])
    for q in (0, 1):
        begin(second[q][0])
    for q in (0, 1):
        first[q][0].wait_recv()
        first[q][2].start()
        begin(second[q][1])
        first[q][1].wait_recv()
        first[q][3].start()
        begin(second[q][2])
    for q in (0, 1):
        onward(second[q][0])
    for q in (0, 1):
        first[q][2].wait_recv()
        first[q][3].wait_recv()
        begin(second[q][3])
    for n in (1, 2, 3):
        for q in (0, 1):
            onward(second[q][n])
    for q in (0, 1):
        for n in range(SIDE):
            second[q][n][2].wait_recv()
            second[q][n][3].wait_recv()
    for q in (0, 1):
        for copies in [first[q]] + second[q]:
            for c in copies:
                c.wait_send()


GATHER_SEMS = [pltpu.SemaphoreType.DMA((2, 1 + SIDE, 4)), pltpu.SemaphoreType.DMA((2, 1 + SIDE, 4))]


class Exchange:
    def __init__(self, line, refs, send, recv):
        self.refs = refs
        self.copies = []
        plan = [(line.me, line.right, 0), (line.me, line.left, 0), (line.me, line.mate, 0), (line.left, line.right, 1),
                (line.right, line.left, 2), (line.left, line.mate, 0), (line.right, line.mate, 0),
                (line.far, line.mate, 1), (line.far, line.mate, 2)]
        for a, ref in enumerate(refs):
            rows = ref.shape[0] // line.n
            half = rows // 2
            group = []
            for slot, (owner, to, part) in enumerate(plan):
                start = owner * rows + (half if part == 2 else 0)
                v = row_block(ref, start, rows if part == 0 else half, half)
                group.append(remote(v, v, send.at[a, slot], recv.at[a, slot], {'model': to}))
            self.copies.append(group)

    def begin(self):
        for c in self.copies:
            c[0].start()
            c[1].start()
            c[2].start()

    def onward(self):
        for c in self.copies:
            c[0].wait_recv()
            c[3].start()
            c[1].wait_recv()
            c[4].start()
            c[5].start()
            c[6].start()

    def finish(self):
        for c in self.copies:
            c[3].wait_recv()
            c[7].start()
            c[4].wait_recv()
            c[8].start()
        for c in self.copies:
            for slot in (2, 5, 6, 7, 8):
                c[slot].wait_recv()
            for one in c:
                one.wait_send()


def exchange_sems(count):
    return [pltpu.SemaphoreType.DMA((count, 9)), pltpu.SemaphoreType.DMA((count, 9))]


def exchange_kernel(n_model, k_ref, v_ref, ka_ref, va_ref, send, recv):
    line = Line(n_model)
    rows = k_ref.shape[0]
    meet(None, (line.right, line.left, line.mate))
    here = pl.ds(pl.multiple_of(line.me * rows, rows), rows)
    ka_ref[here, :] = k_ref[...]
    va_ref[here, :] = v_ref[...]
    ex = Exchange(line, (ka_ref, va_ref), send, recv)
    ex.begin()
    ex.onward()
    ex.finish()


VMEM = pl.BlockSpec(memory_space=pltpu.VMEM)


def params(cid):
    return pltpu.CompilerParams(collective_id=cid, has_side_effects=True, vmem_limit_bytes=VMEM_LIMIT)


def cost(flops):
    return pl.CostEstimate(flops=flops, bytes_accessed=10_000_000, transcendentals=0)


def exchange(k, v, n_model, cid):
    rows, dim = k.shape
    full = jax.ShapeDtypeStruct((rows * n_model, dim), k.dtype)
    return pl.pallas_call(
        functools.partial(exchange_kernel, n_model),
        out_shape=(full, full), in_specs=[VMEM] * 2, out_specs=(VMEM, VMEM),
        scratch_shapes=exchange_sems(2), compiler_params=params(cid), cost_estimate=cost(20_000_000_000), name='exchange_kv',
    )(k, v)


def load_attn_weights(line, layer, wq_ref, wk_ref, wv_ref, wo_ref, wqkv_ref, woa_ref):
    rows, dim = wq_ref.shape[1:]
    here = pl.ds(pl.multiple_of(line.me * rows, rows), rows)
    for at, ref in enumerate((wq_ref, wk_ref, wv_ref)):
        wqkv_ref[here, at * dim:(at + 1) * dim] = ref[layer]
    o_rows = wo_ref.shape[1]
    woa_ref[pl.ds(pl.multiple_of(line.me * o_rows, o_rows), o_rows), :] = wo_ref[layer]


def to_all(line, make):
    copies = []
    for step in range(1, line.n):
        peer = lax.rem(line.me + step, line.n)
        copies.append(make(step, peer))
    for c in copies:
        c.start()
    return copies


def others(line):
    return [lax.rem(line.me + step, line.n) for step in range(1, line.n)]


def start_kernel(n_model, hid_ref, sc_ref, wq_ref, wk_ref, wv_ref, wo_ref, x_ref, h_ref, sca_ref, wqkv_ref, woa_ref,
                 xin, scin, xs, xr, ss, sr, hs, hr, es, er):
    torus, line = Torus(), Line(n_model)
    rows = x_ref.shape[0]
    meet(torus, others(line))
    xin[line.me] = hid_ref[line.me]
    scin[line.me] = sc_ref[...]
    xc = to_all(line, lambda step, peer: remote(hid_ref.at[peer], xin.at[line.me], xs.at[step], xr.at[step], {'model': peer}))
    sc = to_all(line, lambda step, peer: remote(sc_ref, scin.at[line.me], ss.at[step], sr.at[step], {'model': peer}))
    load_attn_weights(line, 0, wq_ref, wk_ref, wv_ref, wo_ref, wqkv_ref, woa_ref)
    ex = Exchange(line, (wqkv_ref, woa_ref), es, er)
    ex.begin()
    for c in xc + sc:
        c.wait_recv()
    sca_ref[...] = jnp.concatenate([scin[m] for m in range(n_model)], axis=1)
    x = jnp.concatenate([xin[m] for m in range(n_model)], axis=1)
    x_ref[...] = x
    mine = torus.at(0, 0, 0)
    h_ref[pl.ds(pl.multiple_of(mine * rows, rows), rows), :] = norm(x.astype(jnp.float32), sca_ref[0:1]).astype(jnp.bfloat16)
    gather_blocks(torus, h_ref, hs, hr)
    ex.onward()
    ex.finish()
    for c in xc + sc:
        c.wait_send()


def attn_weight_shapes(wq, wo, n_model):
    _, rows, dim = wq.shape
    _, o_rows, o_cols = wo.shape
    return (jax.ShapeDtypeStruct((rows * n_model, 3 * dim), wq.dtype), jax.ShapeDtypeStruct((o_rows * n_model, o_cols), wo.dtype))


def start(hidden_mine, scales, wq, wk, wv, wo, cid):
    n_model, rows, width_loc = hidden_mine.shape
    width = n_model * width_loc
    peer_sems = [pltpu.SemaphoreType.DMA((n_model,))] * 4
    return pl.pallas_call(
        functools.partial(start_kernel, n_model),
        out_shape=(jax.ShapeDtypeStruct((rows, width), hidden_mine.dtype),
                   jax.ShapeDtypeStruct((rows * SIDE * SIDE, width), hidden_mine.dtype),
                   jax.ShapeDtypeStruct((scales.shape[0], width), scales.dtype)) + attn_weight_shapes(wq, wo, n_model),
        in_specs=[VMEM] * 6, out_specs=(VMEM,) * 5,
        scratch_shapes=[pltpu.VMEM(hidden_mine.shape, hidden_mine.dtype), pltpu.VMEM((n_model,) + scales.shape, scales.dtype)]
        + peer_sems + GATHER_SEMS + exchange_sems(2),
        compiler_params=params(cid), cost_estimate=cost(30_000_000_000), name='start',
    )(hidden_mine, scales, wq, wk, wv, wo)


def project_kernel(n_model, final, prefetch, a_ref, w_ref, res_ref, sa_ref, sb_ref, *rest):
    rest = list(rest)
    if prefetch:
        wq_ref, wk_ref, wv_ref, wo_ref = rest[:4]
        rest = rest[4:]
    if not final:
        x_ref = rest.pop(0)
    h_ref = rest.pop(0)
    if prefetch:
        wqkv_ref, woa_ref = rest[:2]
        rest = rest[2:]
    far, right, left, own, from_l1, from_r1, from_l, from_r, q_l1, q_r1, q_l, q_r, s1, r1, s2, r2, hs, hr = rest[:18]
    rest = rest[18:]
    torus, line = Torus(), Line(n_model)
    rows, width = res_ref.shape
    half = rows // 2
    cols = width // 2
    if final:
        meet(torus, others(line))
    elif prefetch:
        meet(torus, (line.right, line.left, line.mate))
    else:
        meet(torus, ())
    order = (2, 1, -1, 0)

    def product(q, off, dst):
        lhs = jnp.concatenate([a_ref[pl.ds(pl.multiple_of(torus.at(q, off, o) * rows, rows), rows), :] for o in order], axis=0)
        piece = w_ref.shape[2]
        per = cols // piece
        for p in range(per):
            res = jnp.dot(lhs, w_ref[q * per + p], preferred_element_type=jnp.float32)
            for n in range(SIDE):
                dst[q, n, :, p * piece:(p + 1) * piece] = res[n * rows:(n + 1) * rows]

    def ring1(q, n, k):
        src, dst, step = ((far.at[q, n, pl.ds(0, half)], from_l1.at[q, n], 1), (far.at[q, n, pl.ds(half, half)], from_r1.at[q, n], -1),
                          (right.at[q, n], from_l.at[q, n], 1), (left.at[q, n], from_r.at[q, n], -1))[k]
        return remote(src, dst, s1.at[q, n, k], r1.at[q, n, k], torus.peer(q, step))

    def ring2(q, k):
        src, dst, step = ((own.at[q, 0, pl.ds(0, half)], q_l1.at[q], 1), (own.at[q, 0, pl.ds(half, half)], q_r1.at[q], -1),
                          (own.at[q, 1], q_l.at[q], 1), (own.at[q, 2], q_r.at[q], -1))[k]
        return remote(src, dst, s2.at[q, k], r2.at[q, k], torus.peer(1 - q, step))

    for q in (0, 1):
        product(q, 2, far)
        for n in range(SIDE):
            ring1(q, n, 0).start()
            ring1(q, n, 1).start()
    if prefetch:
        load_attn_weights(line, 1, wq_ref, wk_ref, wv_ref, wo_ref, wqkv_ref, woa_ref)
        ex = Exchange(line, (wqkv_ref, woa_ref), rest[0], rest[1])
        ex.begin()
    for q in (0, 1):
        product(q, 1, right)
        product(q, -1, left)
        for n in range(SIDE):
            ring1(q, n, 0).wait_recv()
            right[q, n, 0:half] += from_l1[q, n]
            ring1(q, n, 2).start()
            ring1(q, n, 1).wait_recv()
            left[q, n, half:rows] += from_r1[q, n]
            ring1(q, n, 3).start()
    for q in (0, 1):
        product(q, 0, own)
    for n in range(SIDE):
        for q in (0, 1):
            ring1(q, n, 2).wait_recv()
            ring1(q, n, 3).wait_recv()
            own[q, n] += from_l[q, n] + from_r[q, n]
            if n == 0:
                ring2(q, 0).start()
                ring2(q, 1).start()
            if n == 1:
                ring2(q, 0).wait_recv()
                own[q, 1, 0:half] += q_l1[q]
                ring2(q, 2).start()
            if n == 2:
                ring2(q, 1).wait_recv()
                own[q, 2, half:rows] += q_r1[q]
                ring2(q, 3).start()
    if prefetch:
        ex.onward()
    total = []
    for q in (0, 1):
        ring2(q, 2).wait_recv()
        ring2(q, 3).wait_recv()
        total.append(own[q, 3] + q_l[q] + q_r[q])
    out = jnp.concatenate(total, axis=1).astype(jnp.bfloat16).astype(jnp.float32)
    x_new = (res_ref[...].astype(jnp.float32) + norm(out, sa_ref[...])).astype(jnp.bfloat16)
    here = pl.ds(pl.multiple_of(torus.at(0, 0, 0) * rows, rows), rows)
    if final:
        outgo, income, cs, cr = rest
        part = width // n_model
        for m in range(n_model):
            outgo[m] = x_new[:, m * part:(m + 1) * part]
        income[line.me] = outgo[line.me]
        copies = to_all(line, lambda step, peer: remote(outgo.at[peer], income.at[line.me], cs.at[step], cr.at[step], {'model': peer}))
        for c in copies:
            c.wait_recv()
        h_ref[here, :] = jnp.concatenate([income[m] for m in range(n_model)], axis=1)
    else:
        x_ref[...] = x_new
        h_ref[here, :] = norm(x_new.astype(jnp.float32), sb_ref[...]).astype(jnp.bfloat16)
    gather_blocks(torus, h_ref, hs, hr)
    if prefetch:
        ex.finish()
    if final:
        for c in copies:
            c.wait_send()
    for q in (0, 1):
        for k in range(4):
            ring2(q, k).wait_send()
            for n in range(SIDE):
                ring1(q, n, k).wait_send()


def project(a, w, resid, scale_a, scale_b, n_model, cid, final=False, prefetch=None):
    rows, width = resid.shape
    cols = width // 2
    half = rows // 2

    def f32(*shape):
        return pltpu.VMEM((2,) + shape + (cols,), jnp.float32)

    scratch = [f32(SIDE, rows)] * 4 + [f32(SIDE, half)] * 2 + [f32(SIDE, rows)] * 2 + [f32(half)] * 2 + [f32(rows)] * 2
    scratch += [pltpu.SemaphoreType.DMA((2, SIDE, 4))] * 2 + [pltpu.SemaphoreType.DMA((2, 4))] * 2 + GATHER_SEMS
    h_shape = jax.ShapeDtypeStruct((rows * SIDE * SIDE, width), jnp.bfloat16)
    out_shape = (h_shape,) if final else (jax.ShapeDtypeStruct((rows, width), jnp.bfloat16), h_shape)
    args = (a, w, resid, scale_a, scale_b)
    if prefetch is not None:
        args += tuple(prefetch)
        out_shape += attn_weight_shapes(prefetch[0], prefetch[3], n_model)
        scratch += exchange_sems(2)
    if final:
        part = (n_model, rows, width // n_model)
        scratch += [pltpu.VMEM(part, jnp.bfloat16)] * 2 + [pltpu.SemaphoreType.DMA((n_model,))] * 2
    return pl.pallas_call(
        functools.partial(project_kernel, n_model, final, prefetch is not None),
        out_shape=out_shape, in_specs=[VMEM] * len(args), out_specs=(VMEM,) * len(out_shape), scratch_shapes=scratch,
        compiler_params=params(cid), cost_estimate=cost(50_000_000_000), name='project_reduce',
    )(*args)


def solution(mesh):
    n_model = mesh.shape['model']
    n_heads = mesh.shape['heads']
    col_spec = P(None, 'model', 'heads')
    row_spec = P(None, 'heads', 'model')
    cache_spec = P(None, None, 'heads', None)

    def body(hidden_in, seg_ids, positions, w_query, w_key, w_value, w_out, w_gate, w_up, w_down, norm_scales, qk_scales):
        n_tok, width_loc = hidden_in.shape
        width = width_loc * n_model
        head_dim = qk_scales.shape[-1]
        tok_m = n_tok // n_model
        tok_own = tok_m // n_heads
        hd = lax.axis_index('heads')
        md = lax.axis_index('model')

        gate_w, up_w, down_w = [], [], []
        for l in range(2):
            gate_w.append(lax.all_gather(w_gate[l], 'model', axis=0, tiled=True))
            up_w.append(lax.all_gather(w_up[l], 'model', axis=0, tiled=True))
            down_w.append(lax.all_gather(w_down[l], 'model', axis=0))

        attn_shards = (w_query, w_key, w_value, w_out)
        mine = lax.dynamic_index_in_dim(hidden_in.reshape(n_model, n_heads, tok_own, width_loc), hd, 1, keepdims=False)
        resid, h, scales, wqkv, wo = start(mine, norm_scales.reshape(-1, width_loc), *attn_shards, 0)

        pos_m = lax.dynamic_slice_in_dim(positions, md * tok_m, tok_m)
        seg_m = lax.dynamic_slice_in_dim(seg_ids, md * tok_m, tok_m)

        settings = ((GLOBAL_BASE, GLOBAL_FACTOR, n_tok), (LOCAL_BASE, 1.0, WINDOW))
        keys, values = [], []
        for l in range(2):
            rope_base, pos_factor, window = settings[l]
            qkv = jnp.dot(h, wqkv, preferred_element_type=jnp.float32).astype(jnp.bfloat16)
            q, k, v = qkv[:, :head_dim], qkv[:, head_dim:2 * head_dim], qkv[:, 2 * head_dim:]
            cos_tab, sin_tab = rope_tables(pos_m, head_dim, rope_base, pos_factor)
            q = apply_rope(norm(q.astype(jnp.float32), qk_scales[l, 0]), cos_tab, sin_tab).astype(jnp.bfloat16)
            k = apply_rope(norm(k.astype(jnp.float32), qk_scales[l, 1]), cos_tab, sin_tab).astype(jnp.bfloat16)
            k_all, v_all = exchange(k, v, n_model, 1 + 3 * l)
            keys.append(k_all[:, None, :])
            values.append(v_all[:, None, :])
            o = attend(q, k_all, v_all, seg_m, pos_m, seg_ids, positions, window)
            wo = wo.reshape(n_model, head_dim, width_loc)
            row = 4 * l
            if l == 0:
                resid, h, wqkv, wo_next = project(o, wo, resid, scales[row + 1:row + 2], scales[row + 2:row + 3], n_model, 2, prefetch=attn_shards)
                wo = wo_next
            else:
                resid, h = project(o, wo, resid, scales[row + 1:row + 2], scales[row + 2:row + 3], n_model, 5)
            g = jnp.dot(h, gate_w[l], preferred_element_type=jnp.float32).astype(jnp.bfloat16)
            u = jnp.dot(h, up_w[l], preferred_element_type=jnp.float32).astype(jnp.bfloat16)
            mid = (jax.nn.gelu(g.astype(jnp.float32), approximate=True) * u.astype(jnp.float32)).astype(jnp.bfloat16)
            if l == 0:
                resid, h = project(mid, down_w[0], resid, scales[3:4], scales[4:5], n_model, 3)
            else:
                out, = project(mid, down_w[1], resid, scales[7:8], scales[7:8], n_model, 6, final=True)
        out = out.reshape(tok_m, n_model, width_loc).transpose(1, 0, 2).reshape(n_tok, width_loc)
        return out, jnp.stack(keys), jnp.stack(values)

    return jax.shard_map(body, mesh=mesh,
                         in_specs=(P(None, 'model'), P(), P(), col_spec, col_spec, col_spec, row_spec, col_spec, col_spec, row_spec, P(None, None, 'model'), P()),
                         out_specs=(P(None, 'model'), cache_spec, cache_spec),
                         check_vma=False)
```

time: 1350 us -> 562 us (0.42)
  waiting for transfers between devices: 1070 us -> 1.71 us
  Pallas kernels: 0 us -> 436 us
  matrix products: 145 us -> 68.9 us
  local copies, waits for them, and re-layouts: 57.2 us -> 21.3 us
  blocking collectives: 24.9 us -> 0 us
  other arithmetic: 29.3 us -> 14.4 us
    all_gather x23 -> x6, waiting for transfers between devices: 743 us -> 0.09 us  [the longest x2 0.04 us: body(): up_w.append(lax.all_gather(w_up[l], 'model', axis=0, tiled=True))]
    pallas_call x0 -> x7, Pallas kernels: none -> 436 us  [the longest x4 287 us: project(): pl.pallas_call(functools.partial(project_kernel, n_model, final, prefetch...]
    reduce_scatter x4 -> x0, waiting for transfers between devices: 324 us -> none  [the longest x2 164 us: body(): lax.psum_scatter(dot_cols(mid, wd), 'heads', scatter_dimension=0, tiled=T...]
    dot_general x42 -> x6, matrix products: 124 us -> 54.5 us  [the longest x2 21.8 us: body(): jnp.dot(h, gate_w[l], preferred_element_type=jnp.float32)]
    unnamed x41 -> x51, local copies, waits for them, and re-layouts: 41 us -> 5.84 us
    all_gather x1 -> x0, blocking collectives: 14 us -> none  [body(): scales = lax.all_gather(norm_scales, 'model', axis=2, tiled=True)]
  transfers between devices with their start and end apart: 28 -> 6, of which waited for: 27 -> 0; matrix products, arithmetic and copies ran while one was open for 9% -> 16% of each run, Pallas kernels for 0% -> 64%
where the time goes in v3:
time: 562 us; the launch traced here: 558 us
  Pallas kernels  436 us (78%)
  matrix products  68.9 us (12%)
  local copies, waits for them, and re-layouts  21.3 us (4%)
  between operations  14.7 us (3%)
  other arithmetic  14.4 us (3%)
    pallas_call x4, Pallas kernels, project(): pl.pallas_call(functools.partial(project_kernel, n_model, final, prefetch...  287 us
    pallas_call x2, Pallas kernels, exchange(): pl.pallas_call(functools.partial(exchange_kernel, n_model), out_shape=(fu...  78.6 us
    pallas_call x1, Pallas kernels, start(): pl.pallas_call(functools.partial(start_kernel, n_model), out_shape=(jax.S...  71.2 us
    dot_general x2, matrix products, body(): jnp.dot(h, gate_w[l], preferred_element_type=jnp.float32)  21.8 us
    dot_general x2, matrix products, body(): jnp.dot(h, up_w[l], preferred_element_type=jnp.float32).astype(jnp.bfloat16)  20.8 us
    dot_general x2, matrix products, body(): jnp.dot(h, wqkv, preferred_element_type=jnp.float32).astype(jnp.bfloat16)  11.8 us
  transfers between devices with their start and end apart: 6, of which 0 were waited for; matrix products, arithmetic and copies ran while one was open for 16% of the time, Pallas kernels for 64%

profile of v3, /device:TPU:0, one launch (start us, length us, event | category | flops | bytes accessed | tf_op | source)
XLA Modules:
  0.0 557.7 jit_solution(14866466688609324919)
XLA Ops:
  7.2 3.3 fusion.99
  10.6 3.3 fusion.98
  14.0 3.3 fusion.97
  20.3 71.2 %start.1 = (bf16[32,3072]{1,0:T(8,128)(2,1)}, bf16[512,3072]{1,0:T(8,128)(2,1)}, f32[8,3072]{1,0:T(8,128)}, bf16[3072,768]{1,0:T(8,128)(2,1)}, bf16[2048,384]{1,0:T(8,128)(2,1)}) custom-call(bf16[8,32,384]{2,1,0:T(8,128)(2,1)} %dynamic-slice_bitcast_fusion.hid_ref, f32[8,384]{1,0:T(8,128)} %reshape.106.sc_ref, bf16[2,384,256]{2,1,0:T(8,128)(2,1)} %rest_0_.1, ...), custom_call_target="tpu_custom_call" | custom-call | flops 30000001024 | bytes 10000000 | tf_op jit(solution)/shard_map/start/pallas_call | solution.py:306
  91.6 5.9 %convolution_convert_fusion.1 = bf16[512,768]{1,0:T(8,128)(2,1)S(1)} fusion(bf16[512,3072]{1,0:T(8,128)(2,1)} %get-tuple-element.20, bf16[3072,768]{1,0:T(8,128)(2,1)} %get-tuple-element.21), kind=kOutput, calls=%fused_computation.53 | convolution fusion | flops 2416312320 | bytes 8650752 | tf_op jit(solution)/shard_map/dot_general | solution.py:495
  103.4 39.8 %exchange_kv.2 = (bf16[4096,256]{1,0:T(8,128)(2,1)}, bf16[4096,256]{1,0:T(8,128)(2,1)}) custom-call(bf16[512,256]{1,0:T(8,128)(2,1)} %pad_maximum_fusion.2.k_ref, bf16[512,256]{1,0:T(8,128)(2,1)} %slice.131.v_ref), custom_call_target="tpu_custom_call" | custom-call | flops 20000000000 | bytes 10000000 | tf_op jit(solution)/shard_map/exchange_kv/pallas_call | solution.py:240
  143.3 4.7 fusion.101
  149.6 2.6 fusion.46.a_ref
  152.2 72.9 %project_reduce.4 = (bf16[32,3072]{1,0:T(8,128)(2,1)}, bf16[512,3072]{1,0:T(8,128)(2,1)}, bf16[3072,768]{1,0:T(8,128)(2,1)}, bf16[2048,384]{1,0:T(8,128)(2,1)}) custom-call(bf16[512,256]{1,0:T(8,128)(2,1)} %fusion.46.a_ref, bf16[8,256,384]{2,1,0:T(8,128)(2,1)} %bitcast.68, bf16[32,3072]{1,0:T(8,128)(2,1)} %get-tuple-element.25.res_ref, ...), custom_call_target="tpu_custom_call" | custom-call | flops 49999998976 | bytes 10000000 | tf_op jit(solution)/shard_map/project_reduce/pallas_call | solution.py:455
  225.1 10.4 %fusion.34 = bf16[512,1536]{1,0:T(8,128)(2,1)} fusion(bf16[512,3072]{1,0:T(8,128)(2,1)} %get-tuple-element.27, bf16[1,3072,1536]{2,1,0:T(8,128)(2,1)} %all-gather.17.cloned.1.call-done), kind=kOutput, calls=%fused_computation.49 | convolution fusion | flops 4832624640 | bytes 14155776 | tf_op jit(solution)/shard_map/dot_general | solution.py:512
  235.5 11.0 %fusion.21.a_ref = bf16[512,1536]{1,0:T(8,128)(2,1)} fusion(bf16[512,1536]{1,0:T(8,128)(2,1)} %fusion.34, bf16[512,3072]{1,0:T(8,128)(2,1)S(1)} %copy-done.23, bf16[1,3072,1536]{2,1,0:T(8,128)(2,1)} %all-gather.15.cloned.1.call-done), kind=kOutput, calls=%fused_computation.40 | convolution fusion | flops 4842061824 | bytes 15728640 | tf_op jit(solution)/shard_map/dot_general | solution.py:511
  246.6 69.8 %project_reduce.5 = (bf16[32,3072]{1,0:T(8,128)(2,1)}, bf16[512,3072]{1,0:T(8,128)(2,1)}) custom-call(bf16[512,1536]{1,0:T(8,128)(2,1)} %fusion.21.a_ref, bf16[8,1536,384]{2,1,0:T(8,128)(2,1)} %all-gather.11.cloned.1.call-done.w_ref, bf16[32,3072]{1,0:T(8,128)(2,1)} %get-tuple-element.28.res_ref, f32[1,3072]{1,0:T(1,128)} %get-tuple-element.65.sa_ref, ...), custom_call_target="tpu_custom_call" | custom-call | flops 49999998976 | bytes 10000000 | tf_op jit(solution)/shard_map/project_reduce/pallas_call | solution.py:455
  316.4 5.9 %convolution_convert_fusion = bf16[512,768]{1,0:T(8,128)(2,1)S(1)} fusion(bf16[512,3072]{1,0:T(8,128)(2,1)} %get-tuple-element.29, bf16[3072,768]{1,0:T(8,128)(2,1)} %get-tuple-element.30), kind=kOutput, calls=%fused_computation.52 | convolution fusion | flops 2416312320 | bytes 8650752 | tf_op jit(solution)/shard_map/dot_general | solution.py:495
  325.7 38.8 %exchange_kv.3 = (bf16[4096,256]{1,0:T(8,128)(2,1)}, bf16[4096,256]{1,0:T(8,128)(2,1)}) custom-call(bf16[512,256]{1,0:T(8,128)(2,1)} %pad_maximum_fusion.3.k_ref, bf16[512,256]{1,0:T(8,128)(2,1)} %slice.138.v_ref), custom_call_target="tpu_custom_call" | custom-call | flops 20000000000 | bytes 10000000 | tf_op jit(solution)/shard_map/exchange_kv/pallas_call | solution.py:240
  364.5 4.7 fusion.102
  370.8 2.5 fusion.45.a_ref
  373.3 66.3 %project_reduce.6 = (bf16[32,3072]{1,0:T(8,128)(2,1)}, bf16[512,3072]{1,0:T(8,128)(2,1)}) custom-call(bf16[512,256]{1,0:T(8,128)(2,1)} %fusion.45.a_ref, bf16[8,256,384]{2,1,0:T(8,128)(2,1)} %bitcast.69, bf16[32,3072]{1,0:T(8,128)(2,1)} %get-tuple-element.34.res_ref, f32[1,3072]{1,0:T(1,128)} %get-tuple-element.63.sa_ref, f32[1,3072]{1,0:T(1,128)} %get-tuple-element.62.sb_ref), custom_call_target="tpu_custom_call" | custom-call | flops 49999998976 | bytes 10000000 | tf_op jit(solution)/shard_map/project_reduce/pallas_call | solution.py:455
  439.7 10.4 %fusion.42 = bf16[512,1536]{1,0:T(8,128)(2,1)} fusion(bf16[512,3072]{1,0:T(8,128)(2,1)} %get-tuple-element.35, bf16[1,3072,1536]{2,1,0:T(8,128)(2,1)} %all-gather.21.cloned.1.call-done), kind=kOutput, calls=%fused_computation.51 | convolution fusion | flops 4832624640 | bytes 14155776 | tf_op jit(solution)/shard_map/dot_general | solution.py:512
  450.1 10.8 %fusion.28.a_ref = bf16[512,1536]{1,0:T(8,128)(2,1)} fusion(bf16[512,1536]{1,0:T(8,128)(2,1)} %fusion.42, bf16[512,3072]{1,0:T(8,128)(2,1)S(1)} %copy-done.24, bf16[1,3072,1536]{2,1,0:T(8,128)(2,1)} %all-gather.19.cloned.1.call-done), kind=kOutput, calls=%fused_computation.47 | convolution fusion | flops 4842061824 | bytes 15728640 | tf_op jit(solution)/shard_map/dot_general | solution.py:511
  460.9 77.6 %project_reduce.7 = bf16[512,3072]{1,0:T(8,128)(2,1)} custom-call(bf16[512,1536]{1,0:T(8,128)(2,1)} %fusion.28.a_ref, bf16[8,1536,384]{2,1,0:T(8,128)(2,1)} %all-gather.13.cloned.1.call-done.w_ref, bf16[32,3072]{1,0:T(8,128)(2,1)} %get-tuple-element.36.res_ref, f32[1,3072]{1,0:T(1,128)} %get-tuple-element.61.sa_ref.sb_ref, ...), custom_call_target="tpu_custom_call" | custom-call | flops 49999998976 | bytes 10000000 | tf_op jit(solution)/shard_map/project_reduce/pallas_call | solution.py:455
  538.5 2.6 copy.20
  541.2 2.1 copy.18
  544.5 2.5 pad_maximum_fusion
  548.3 2.4 pad_maximum_fusion.1
  (92 shorter events, 18.2 us)
Async XLA Ops:
  7.2 12.5 %copy-start = (bf16[4096,384]{1,0:T(8,128)(2,1)S(1)}, bf16[4096,384]{1,0:T(8,128)(2,1)}, u32[]{:S(2)}) copy-start(bf16[4096,384]{1,0:T(8,128)(2,1)} %param.12) | copy-start | bytes 9437188
  7.2 217.9 %all-gather.17.cloned.1.call-start = ((), (), s32[]{:S(2)}) async-start(), calls=%async_computation.3 | async-start | bytes 10616832 | tf_op jit(solution)/shard_map/all_gather | solution.py:481
  10.6 224.9 %all-gather.15.cloned.1.call-start = ((), (), s32[]{:S(2)}) async-start(), calls=%async_computation.2 | async-start | bytes 10616832 | tf_op jit(solution)/shard_map/all_gather | solution.py:480
  13.9 232.6 %all-gather.11.cloned.1.call-start = ((), (), s32[]{:S(2)}) async-start(), calls=%async_computation | async-start | bytes 10616832 | tf_op jit(solution)/shard_map/all_gather | solution.py:482
  17.3 422.4 %all-gather.21.cloned.1.call-start = ((), (), s32[]{:S(2)}) async-start(), calls=%async_computation.5 | async-start | bytes 10616832 | tf_op jit(solution)/shard_map/all_gather | solution.py:481
  17.8 432.2 %all-gather.19.cloned.1.call-start = ((), (), s32[]{:S(2)}) async-start(), calls=%async_computation.4 | async-start | bytes 10616832 | tf_op jit(solution)/shard_map/all_gather | solution.py:480
  18.4 442.5 %all-gather.13.cloned.1.call-start = ((), (), s32[]{:S(2)}) async-start(), calls=%async_computation.1 | async-start | bytes 10616832 | tf_op jit(solution)/shard_map/all_gather | solution.py:482
  91.6 7.5 %copy-start.15 = (f32[2,2,256]{2,1,0:T(2,128)S(1)}, f32[2,2,256]{2,1,0:T(2,128)}, u32[]{:S(2)}) copy-start(f32[2,2,256]{2,1,0:T(2,128)} %param.23) | copy-start | bytes 12292
  91.6 8.0 %copy-start.19 = (s32[4096]{0:T(1024)S(1)}, s32[4096]{0:T(1024)}, u32[]{:S(2)}) copy-start(s32[4096]{0:T(1024)} %param.14) | copy-start | bytes 49156
  91.6 8.7 %copy-start.21 = (s32[4096]{0:T(1024)S(1)}, s32[4096]{0:T(1024)}, u32[]{:S(2)}) copy-start(s32[4096]{0:T(1024)} %param.13) | copy-start | bytes 49156
  91.6 8.8 %copy-start.8 = (f32[8,3072]{1,0:T(8,128)S(1)}, f32[8,3072]{1,0:T(8,128)}, u32[]{:S(2)}) copy-start(f32[8,3072]{1,0:T(8,128)} %get-tuple-element.26) | copy-start | bytes 294916
  100.3 43.0 %copy-start.11 = (s32[512]{0:T(512)}, s32[512]{0:T(512)S(1)}, u32[]{:S(2)}) copy-start(s32[512]{0:T(512)S(1)} %get-tuple-element.42) | copy-start | bytes 6148
  100.4 43.0 %copy-start.16 = (s32[512]{0:T(512)}, s32[512]{0:T(512)S(1)}, u32[]{:S(2)}) copy-start(s32[512]{0:T(512)S(1)} %dynamic_slice.10) | copy-start | bytes 6148
  225.1 10.4 %copy-start.23 = (bf16[512,3072]{1,0:T(8,128)(2,1)S(1)}, bf16[512,3072]{1,0:T(8,128)(2,1)}, u32[]{:S(2)}) copy-start(bf16[512,3072]{1,0:T(8,128)(2,1)} %get-tuple-element.27) | copy-start | bytes 9437188
  316.4 6.9 %copy-start.13 = (f32[1,1,256]{2,1,0:T(1,128)S(1)}, f32[1,1,256]{2,1,0:T(1,128)}, u32[]{:S(2)}) copy-start(f32[1,1,256]{2,1,0:T(1,128)} %get-tuple-element.68) | copy-start | bytes 3076
  316.4 6.9 %copy-start.14 = (f32[1,1,256]{2,1,0:T(1,128)S(1)}, f32[1,1,256]{2,1,0:T(1,128)}, u32[]{:S(2)}) copy-start(f32[1,1,256]{2,1,0:T(1,128)} %get-tuple-element.71) | copy-start | bytes 3076
  316.4 7.1 %copy-start.10 = (f32[512]{0:T(512)S(1)}, f32[512]{0:T(512)}, u32[]{:S(2)}) copy-start(f32[512]{0:T(512)} %get-tuple-element.41) | copy-start | bytes 6148
  316.4 7.1 %copy-start.18 = (f32[128]{0:T(128)S(1)}, f32[128]{0:T(128)}, u32[]{:S(2)}) copy-start(f32[128]{0:T(128)} %broadcast_power_fusion) | copy-start | bytes 1540
  325.7 38.8 %copy-start.12 = (s32[512]{0:T(512)S(1)}, s32[512]{0:T(512)}, u32[]{:S(2)}) copy-start(s32[512]{0:T(512)} %copy-done.11) | copy-start | bytes 6148
  325.7 38.8 %copy-start.17 = (s32[512]{0:T(512)S(1)}, s32[512]{0:T(512)}, u32[]{:S(2)}) copy-start(s32[512]{0:T(512)} %copy-done.16) | copy-start | bytes 6148
  325.7 38.8 %copy-start.20 = (s32[4096]{0:T(1024)S(1)}, s32[4096]{0:T(1024)}, u32[]{:S(2)}) copy-start(s32[4096]{0:T(1024)} %param.14) | copy-start | bytes 49156
  325.7 38.8 %copy-start.22 = (s32[4096]{0:T(1024)S(1)}, s32[4096]{0:T(1024)}, u32[]{:S(2)}) copy-start(s32[4096]{0:T(1024)} %param.13) | copy-start | bytes 49156
  439.6 10.4 %copy-start.24 = (bf16[512,3072]{1,0:T(8,128)(2,1)S(1)}, bf16[512,3072]{1,0:T(8,128)(2,1)}, u32[]{:S(2)}) copy-start(bf16[512,3072]{1,0:T(8,128)(2,1)} %get-tuple-element.35) | copy-start | bytes 9437188
  544.5 3.7 copy-start.6
  (7 other events, 16.5 us)
Sparse Core Ops, SparseCore 0:
  10.7 84.8 all-gather.16
  97.3 69.4 all-gather.14
  168.5 64.5 all-gather.10
  235.2 54.2 all-gather.20
  291.6 68.2 all-gather.18
  361.4 56.9 all-gather.12

commit v4 on v3

--- a/solution.py
+++ b/solution.py
@@ -99,7 +99,7 @@
     pl.semaphore_wait(barrier, count)
 
 
-def gather_blocks(torus, h_ref, send, recv):
+def gather_blocks(torus, h_ref, send, recv, between=lambda: None):
     rows = h_ref.shape[0] // (SIDE * SIDE)
     cols = h_ref.shape[1] // 2
     half = rows // 2
@@ -145,6 +145,7 @@
         first[q][2].wait_recv()
         first[q][3].wait_recv()
         begin(second[q][3])
+    between()
     for n in (1, 2, 3):
         for q in (0, 1):
             onward(second[q][n])
@@ -162,20 +163,18 @@
 
 
 class Exchange:
-    def __init__(self, line, refs, send, recv):
-        self.refs = refs
+    def __init__(self, line, items, send, recv):
         self.copies = []
         plan = [(line.me, line.right, 0), (line.me, line.left, 0), (line.me, line.mate, 0), (line.left, line.right, 1),
                 (line.right, line.left, 2), (line.left, line.mate, 0), (line.right, line.mate, 0),
                 (line.far, line.mate, 1), (line.far, line.mate, 2)]
-        for a, ref in enumerate(refs):
-            rows = ref.shape[0] // line.n
+        for a, (ref, stride, row, rows, src) in enumerate(items):
             half = rows // 2
             group = []
             for slot, (owner, to, part) in enumerate(plan):
-                start = owner * rows + (half if part == 2 else 0)
-                v = row_block(ref, start, rows if part == 0 else half, half)
-                group.append(remote(v, v, send.at[a, slot], recv.at[a, slot], {'model': to}))
+                first = owner * stride + (row + (half if part == 2 else 0))
+                v = row_block(ref, first, rows if part == 0 else half, half)
+                group.append(remote(src if src is not None and slot < 3 else v, v, send.at[a, slot], recv.at[a, slot], {'model': to}))
             self.copies.append(group)
 
     def begin(self):
@@ -184,8 +183,8 @@
             c[1].start()
             c[2].start()
 
-    def onward(self):
-        for c in self.copies:
+    def onward(self, lo=0, hi=None):
+        for c in self.copies[lo:hi]:
             c[0].wait_recv()
             c[3].start()
             c[1].wait_recv()
@@ -217,13 +216,15 @@
     here = pl.ds(pl.multiple_of(line.me * rows, rows), rows)
     ka_ref[here, :] = k_ref[...]
     va_ref[here, :] = v_ref[...]
-    ex = Exchange(line, (ka_ref, va_ref), send, recv)
+    ex = Exchange(line, [(ka_ref, rows, 0, rows, None), (va_ref, rows, 0, rows, None)], send, recv)
     ex.begin()
     ex.onward()
     ex.finish()
 
 
 VMEM = pl.BlockSpec(memory_space=pltpu.VMEM)
+ANY = pl.BlockSpec(memory_space=pl.ANY)
+PIECES = 4
 
 
 def params(cid):
@@ -251,6 +252,7 @@
         wqkv_ref[here, at * dim:(at + 1) * dim] = ref[layer]
     o_rows = wo_ref.shape[1]
     woa_ref[pl.ds(pl.multiple_of(line.me * o_rows, o_rows), o_rows), :] = wo_ref[layer]
+    return [(wqkv_ref, rows, 0, rows, None), (woa_ref, o_rows, 0, o_rows, None)]
 
 
 def to_all(line, make):
@@ -267,18 +269,26 @@
     return [lax.rem(line.me + step, line.n) for step in range(1, line.n)]
 
 
-def start_kernel(n_model, hid_ref, sc_ref, wq_ref, wk_ref, wv_ref, wo_ref, x_ref, h_ref, sca_ref, wqkv_ref, woa_ref,
-                 xin, scin, xs, xr, ss, sr, hs, hr, es, er):
+def start_kernel(n_model, hid_ref, sc_ref, wq_ref, wk_ref, wv_ref, wo_ref, wg_ref, wu_ref,
+                 x_ref, h_ref, sca_ref, wqkv_ref, woa_ref, g0_ref, u0_ref, g1_ref, u1_ref,
+                 xin, scin, stage, xs, xr, ss, sr, ls, hs, hr, es, er):
     torus, line = Torus(), Line(n_model)
     rows = x_ref.shape[0]
+    shards = ((wg_ref, 0, g0_ref), (wu_ref, 0, u0_ref), (wg_ref, 1, g1_ref), (wu_ref, 1, u1_ref))
+    loads = [pltpu.make_async_copy(ref.at[layer], stage.at[k], ls.at[k]) for k, (ref, layer, _) in enumerate(shards)]
+    stores = [pltpu.make_async_copy(stage.at[k], dst, ls.at[k]) for k, (_, _, dst) in enumerate(shards)]
+    for c in loads:
+        c.start()
     meet(torus, others(line))
     xin[line.me] = hid_ref[line.me]
     scin[line.me] = sc_ref[...]
     xc = to_all(line, lambda step, peer: remote(hid_ref.at[peer], xin.at[line.me], xs.at[step], xr.at[step], {'model': peer}))
     sc = to_all(line, lambda step, peer: remote(sc_ref, scin.at[line.me], ss.at[step], sr.at[step], {'model': peer}))
-    load_attn_weights(line, 0, wq_ref, wk_ref, wv_ref, wo_ref, wqkv_ref, woa_ref)
-    ex = Exchange(line, (wqkv_ref, woa_ref), es, er)
+    ex = Exchange(line, load_attn_weights(line, 0, wq_ref, wk_ref, wv_ref, wo_ref, wqkv_ref, woa_ref), es, er)
     ex.begin()
+    for load, store in zip(loads, stores):
+        load.wait()
+        store.start()
     for c in xc + sc:
         c.wait_recv()
     sca_ref[...] = jnp.concatenate([scin[m] for m in range(n_model)], axis=1)
@@ -286,9 +296,10 @@
     x_ref[...] = x
     mine = torus.at(0, 0, 0)
     h_ref[pl.ds(pl.multiple_of(mine * rows, rows), rows), :] = norm(x.astype(jnp.float32), sca_ref[0:1]).astype(jnp.bfloat16)
-    gather_blocks(torus, h_ref, hs, hr)
-    ex.onward()
+    gather_blocks(torus, h_ref, hs, hr, ex.onward)
     ex.finish()
+    for c in stores:
+        c.wait()
     for c in xc + sc:
         c.wait_send()
 
@@ -299,7 +310,7 @@
     return (jax.ShapeDtypeStruct((rows * n_model, 3 * dim), wq.dtype), jax.ShapeDtypeStruct((o_rows * n_model, o_cols), wo.dtype))
 
 
-def start(hidden_mine, scales, wq, wk, wv, wo, cid):
+def start(hidden_mine, scales, wq, wk, wv, wo, wg, wu, cid):
     n_model, rows, width_loc = hidden_mine.shape
     width = n_model * width_loc
     peer_sems = [pltpu.SemaphoreType.DMA((n_model,))] * 4
@@ -307,25 +318,32 @@
         functools.partial(start_kernel, n_model),
         out_shape=(jax.ShapeDtypeStruct((rows, width), hidden_mine.dtype),
                    jax.ShapeDtypeStruct((rows * SIDE * SIDE, width), hidden_mine.dtype),
-                   jax.ShapeDtypeStruct((scales.shape[0], width), scales.dtype)) + attn_weight_shapes(wq, wo, n_model),
-        in_specs=[VMEM] * 6, out_specs=(VMEM,) * 5,
-        scratch_shapes=[pltpu.VMEM(hidden_mine.shape, hidden_mine.dtype), pltpu.VMEM((n_model,) + scales.shape, scales.dtype)]
-        + peer_sems + GATHER_SEMS + exchange_sems(2),
+                   jax.ShapeDtypeStruct((scales.shape[0], width), scales.dtype)) + attn_weight_shapes(wq, wo, n_model)
+        + (jax.ShapeDtypeStruct(wg.shape[1:], wg.dtype),) * 4,
+        in_specs=[VMEM] * 6 + [ANY] * 2, out_specs=(VMEM,) * 5 + (ANY,) * 4,
+        scratch_shapes=[pltpu.VMEM(hidden_mine.shape, hidden_mine.dtype), pltpu.VMEM((n_model,) + scales.shape, scales.dtype),
+                        pltpu.VMEM((4,) + wg.shape[1:], wg.dtype)]
+        + peer_sems + [pltpu.SemaphoreType.DMA((4,))] + GATHER_SEMS + exchange_sems(2),
         compiler_params=params(cid), cost_estimate=cost(30_000_000_000), name='start',
-    )(hidden_mine, scales, wq, wk, wv, wo)
-
-
-def project_kernel(n_model, final, prefetch, a_ref, w_ref, res_ref, sa_ref, sb_ref, *rest):
+    )(hidden_mine, scales, wq, wk, wv, wo, wg, wu)
+
+
+def project_kernel(n_model, final, attn, down, a_ref, w_ref, res_ref, sa_ref, sb_ref, *rest):
     rest = list(rest)
-    if prefetch:
+    fetch = attn or down is not None
+    if attn:
         wq_ref, wk_ref, wv_ref, wo_ref = rest[:4]
         rest = rest[4:]
+    if down is not None:
+        wd_ref = rest.pop(0)
     if not final:
         x_ref = rest.pop(0)
     h_ref = rest.pop(0)
-    if prefetch:
+    if attn:
         wqkv_ref, woa_ref = rest[:2]
         rest = rest[2:]
+    if down is not None:
+        wda_ref = rest.pop(0)
     far, right, left, own, from_l1, from_r1, from_l, from_r, q_l1, q_r1, q_l, q_r, s1, r1, s2, r2, hs, hr = rest[:18]
     rest = rest[18:]
     torus, line = Torus(), Line(n_model)
@@ -334,7 +352,7 @@
     cols = width // 2
     if final:
         meet(torus, others(line))
-    elif prefetch:
+    elif fetch:
         meet(torus, (line.right, line.left, line.mate))
     else:
         meet(torus, ())
@@ -359,14 +377,25 @@
                           (own.at[q, 1], q_l.at[q], 1), (own.at[q, 2], q_r.at[q], -1))[k]
         return remote(src, dst, s2.at[q, k], r2.at[q, k], torus.peer(1 - q, step))
 
+    if down is not None:
+        mine, ls = rest[2:]
+        load = pltpu.make_async_copy(wd_ref.at[down], mine, ls.at[0])
+        load.start()
     for q in (0, 1):
         product(q, 2, far)
         for n in range(SIDE):
             ring1(q, n, 0).start()
             ring1(q, n, 1).start()
-    if prefetch:
-        load_attn_weights(line, 1, wq_ref, wk_ref, wv_ref, wo_ref, wqkv_ref, woa_ref)
-        ex = Exchange(line, (wqkv_ref, woa_ref), rest[0], rest[1])
+    if attn:
+        ex = Exchange(line, load_attn_weights(line, 1, wq_ref, wk_ref, wv_ref, wo_ref, wqkv_ref, woa_ref), rest[0], rest[1])
+        ex.begin()
+    if down is not None:
+        load.wait()
+        stride = mine.shape[0]
+        piece = stride // PIECES
+        keep = pltpu.make_async_copy(mine, row_block(wda_ref, line.me * stride, stride, stride), ls.at[0])
+        keep.start()
+        ex = Exchange(line, [(wda_ref, stride, k * piece, piece, mine.at[pl.ds(k * piece, piece)]) for k in range(PIECES)], rest[0], rest[1])
         ex.begin()
     for q in (0, 1):
         product(q, 1, right)
@@ -380,6 +409,8 @@
             ring1(q, n, 3).start()
     for q in (0, 1):
         product(q, 0, own)
+    if down is not None:
+        ex.onward(0, 2)
     for n in range(SIDE):
         for q in (0, 1):
             ring1(q, n, 2).wait_recv()
@@ -396,8 +427,6 @@
                 ring2(q, 1).wait_recv()
                 own[q, 2, half:rows] += q_r1[q]
                 ring2(q, 3).start()
-    if prefetch:
-        ex.onward()
     total = []
     for q in (0, 1):
         ring2(q, 2).wait_recv()
@@ -419,9 +448,15 @@
     else:
         x_ref[...] = x_new
         h_ref[here, :] = norm(x_new.astype(jnp.float32), sb_ref[...]).astype(jnp.bfloat16)
-    gather_blocks(torus, h_ref, hs, hr)
-    if prefetch:
+    if attn:
+        gather_blocks(torus, h_ref, hs, hr, ex.onward)
         ex.finish()
+    elif down is not None:
+        gather_blocks(torus, h_ref, hs, hr, lambda: ex.onward(2))
+        ex.finish()
+        keep.wait()
+    else:
+        gather_blocks(torus, h_ref, hs, hr)
     if final:
         for c in copies:
             c.wait_send()
@@ -432,7 +467,7 @@
                 ring1(q, n, k).wait_send()
 
 
-def project(a, w, resid, scale_a, scale_b, n_model, cid, final=False, prefetch=None):
+def project(a, w, resid, scale_a, scale_b, n_model, cid, final=False, attn=None, down=None, layer=None):
     rows, width = resid.shape
     cols = width // 2
     half = rows // 2
@@ -445,16 +480,26 @@
     h_shape = jax.ShapeDtypeStruct((rows * SIDE * SIDE, width), jnp.bfloat16)
     out_shape = (h_shape,) if final else (jax.ShapeDtypeStruct((rows, width), jnp.bfloat16), h_shape)
     args = (a, w, resid, scale_a, scale_b)
-    if prefetch is not None:
-        args += tuple(prefetch)
-        out_shape += attn_weight_shapes(prefetch[0], prefetch[3], n_model)
+    in_specs, out_specs = [VMEM] * 5, (VMEM,) * len(out_shape)
+    if attn is not None:
+        args += tuple(attn)
+        in_specs += [VMEM] * 4
+        out_shape += attn_weight_shapes(attn[0], attn[3], n_model)
+        out_specs += (VMEM,) * 2
         scratch += exchange_sems(2)
+    if down is not None:
+        args += (down,)
+        in_specs += [ANY]
+        _, d_rows, d_cols = down.shape
+        out_shape += (jax.ShapeDtypeStruct((d_rows * n_model, d_cols), down.dtype),)
+        out_specs += (ANY,)
+        scratch += exchange_sems(PIECES) + [pltpu.VMEM((d_rows, d_cols), down.dtype), pltpu.SemaphoreType.DMA((1,))]
     if final:
         part = (n_model, rows, width // n_model)
         scratch += [pltpu.VMEM(part, jnp.bfloat16)] * 2 + [pltpu.SemaphoreType.DMA((n_model,))] * 2
     return pl.pallas_call(
-        functools.partial(project_kernel, n_model, final, prefetch is not None),
-        out_shape=out_shape, in_specs=[VMEM] * len(args), out_specs=(VMEM,) * len(out_shape), scratch_shapes=scratch,
+        functools.partial(project_kernel, n_model, final, attn is not None, layer),
+        out_shape=out_shape, in_specs=in_specs, out_specs=out_specs, scratch_shapes=scratch,
         compiler_params=params(cid), cost_estimate=cost(50_000_000_000), name='project_reduce',
     )(*args)
 
@@ -475,15 +520,10 @@
         hd = lax.axis_index('heads')
         md = lax.axis_index('model')
 
-        gate_w, up_w, down_w = [], [], []
-        for l in range(2):
-            gate_w.append(lax.all_gather(w_gate[l], 'model', axis=0, tiled=True))
-            up_w.append(lax.all_gather(w_up[l], 'model', axis=0, tiled=True))
-            down_w.append(lax.all_gather(w_down[l], 'model', axis=0))
-
         attn_shards = (w_query, w_key, w_value, w_out)
         mine = lax.dynamic_index_in_dim(hidden_in.reshape(n_model, n_heads, tok_own, width_loc), hd, 1, keepdims=False)
-        resid, h, scales, wqkv, wo = start(mine, norm_scales.reshape(-1, width_loc), *attn_shards, 0)
+        resid, h, scales, wqkv, wo, *shards = start(mine, norm_scales.reshape(-1, width_loc), *attn_shards, w_gate, w_up, 0)
+        wide = [lax.all_gather(w, 'model', axis=0, tiled=True) for w in shards]
 
         pos_m = lax.dynamic_slice_in_dim(positions, md * tok_m, tok_m)
         seg_m = lax.dynamic_slice_in_dim(seg_ids, md * tok_m, tok_m)
@@ -503,18 +543,15 @@
             o = attend(q, k_all, v_all, seg_m, pos_m, seg_ids, positions, window)
             wo = wo.reshape(n_model, head_dim, width_loc)
             row = 4 * l
-            if l == 0:
-                resid, h, wqkv, wo_next = project(o, wo, resid, scales[row + 1:row + 2], scales[row + 2:row + 3], n_model, 2, prefetch=attn_shards)
-                wo = wo_next
-            else:
-                resid, h = project(o, wo, resid, scales[row + 1:row + 2], scales[row + 2:row + 3], n_model, 5)
-            g = jnp.dot(h, gate_w[l], preferred_element_type=jnp.float32).astype(jnp.bfloat16)
-            u = jnp.dot(h, up_w[l], preferred_element_type=jnp.float32).astype(jnp.bfloat16)
+            resid, h, wd = project(o, wo, resid, scales[row + 1:row + 2], scales[row + 2:row + 3], n_model, 2 + 3 * l, down=w_down, layer=l)
+            wd = wd.reshape(n_model, w_down.shape[1], width_loc)
+            g = jnp.dot(h, wide[2 * l], preferred_element_type=jnp.float32).astype(jnp.bfloat16)
+            u = jnp.dot(h, wide[2 * l + 1], preferred_element_type=jnp.float32).astype(jnp.bfloat16)
             mid = (jax.nn.gelu(g.astype(jnp.float32), approximate=True) * u.astype(jnp.float32)).astype(jnp.bfloat16)
             if l == 0:
-                resid, h = project(mid, down_w[0], resid, scales[3:4], scales[4:5], n_model, 3)
+                resid, h, wqkv, wo = project(mid, wd, resid, scales[3:4], scales[4:5], n_model, 3, attn=attn_shards)
             else:
-                out, = project(mid, down_w[1], resid, scales[7:8], scales[7:8], n_model, 6, final=True)
+                out, = project(mid, wd, resid, scales[7:8], scales[7:8], n_model, 6, final=True)
         out = out.reshape(tok_m, n_model, width_loc).transpose(1, 0, 2).reshape(n_tok, width_loc)
         return out, jnp.stack(keys), jnp.stack(values)
 

time: 562 us -> 542 us (0.964)
  Pallas kernels: 436 us -> 426 us
  local copies, waits for them, and re-layouts: 21.3 us -> 12.7 us
    pallas_call x1, Pallas kernels: 71.2 us -> 43.3 us  [start(): pl.pallas_call(functools.partial(start_kernel, n_model), out_shape=(jax.S...]
    pallas_call x4, Pallas kernels: 287 us -> 297 us  [project(): pl.pallas_call(functools.partial(project_kernel, n_model, final, attn is...]
    slice x3 -> x0, local copies, waits for them, and re-layouts: 9.85 us -> none  [the longest x1 3.33 us: body(): up_w.append(lax.all_gather(w_up[l], 'model', axis=0, tiled=True))]
    pallas_call x2, Pallas kernels: 78.6 us -> 85.6 us  [exchange(): pl.pallas_call(functools.partial(exchange_kernel, n_model), out_shape=(fu...]
  transfers between devices with their start and end apart: 6 -> 4, of which waited for: 0 -> 0; matrix products, arithmetic and copies ran while one was open for 16% -> 13% of each run, Pallas kernels for 64% -> 57%
where the time goes in v4:
time: 542 us; the launch traced here: 538 us
  Pallas kernels  426 us (79%)
  matrix products  67.8 us (13%)
  other arithmetic  14.8 us (3%)
  between operations  14.6 us (3%)
  local copies, waits for them, and re-layouts  12.7 us (2%)
    pallas_call x4, Pallas kernels, project(): pl.pallas_call(functools.partial(project_kernel, n_model, final, attn is...  297 us
    pallas_call x2, Pallas kernels, exchange(): pl.pallas_call(functools.partial(exchange_kernel, n_model), out_shape=(fu...  85.6 us
    pallas_call x1, Pallas kernels, start(): pl.pallas_call(functools.partial(start_kernel, n_model), out_shape=(jax.S...  43.3 us
    dot_general x2, matrix products, body(): jnp.dot(h, wide[2 * l], preferred_element_type=jnp.float32)  20.8 us
    dot_general x2, matrix products, body(): jnp.dot(h, wide[2 * l + 1], preferred_element_type=jnp.float32)  20.8 us
    dot_general x2, matrix products, body(): jnp.dot(h, wqkv, preferred_element_type=jnp.float32).astype(jnp.bfloat16)  11.8 us
  transfers between devices with their start and end apart: 4, of which 0 were waited for; matrix products, arithmetic and copies ran while one was open for 13% of the time, Pallas kernels for 57%

profile of v4, /device:TPU:0, one launch (start us, length us, event | category | flops | bytes accessed | tf_op | source)
XLA Modules:
  0.0 538.3 jit_solution(15126514543150931035)
XLA Ops:
  7.2 1.5 reshape.112.sc_ref
  9.8 43.3 %start.1 = (bf16[32,3072]{1,0:T(8,128)(2,1)}, bf16[512,3072]{1,0:T(8,128)(2,1)}, f32[8,3072]{1,0:T(8,128)}, bf16[3072,768]{1,0:T(8,128)(2,1)}, bf16[2048,384]{1,...) custom-call(bf16[8,32,384]{2,1,0:T(8,128)(2,1)} %dynamic-slice_bitca, ...), custom_call_target="tpu_custom_call" | custom-call | flops 30000001024 | bytes 10000000 | tf_op jit(solution)/shard_map/start/pallas_call | solution.py:317
  55.3 5.9 %convolution_convert_fusion.5 = bf16[512,768]{1,0:T(8,128)(2,1)S(1)} fusion(bf16[512,3072]{1,0:T(8,128)(2,1)} %get-tuple-element.26, bf16[3072,768]{1,0:T(8,128)(2,1)} %get-tuple-element.27), kind=kOutput, calls=%fused_computation.45 | convolution fusion | flops 2416312320 | bytes 8650752 | tf_op jit(solution)/shard_map/dot_general | solution.py:535
  65.0 1.7 fusion.48
  67.5 42.8 %exchange_kv.2 = (bf16[4096,256]{1,0:T(8,128)(2,1)}, bf16[4096,256]{1,0:T(8,128)(2,1)}) custom-call(bf16[512,256]{1,0:T(8,128)(2,1)} %pad_maximum_fusion.2.k_ref, bf16[512,256]{1,0:T(8,128)(2,1)} %slice.107.v_ref), custom_call_target="tpu_custom_call" | custom-call | flops 20000000000 | bytes 10000000 | tf_op jit(solution)/shard_map/exchange_kv/pallas_call | solution.py:241
  110.3 4.7 fusion.74
  116.6 2.5 fusion.22.a_ref
  119.1 76.6 %project_reduce.4 = (bf16[32,3072]{1,0:T(8,128)(2,1)}, bf16[512,3072]{1,0:T(8,128)(2,1)}, bf16[12288,384]{1,0:T(8,128)(2,1)}) custom-call(bf16[512,256]{1,0:T(8,128)(2,1)} %fusion.22.a_ref, bf16[8,256,384]{2,1,0:T(8,128)(2,1)} %bitcast.52, bf16[32,3072]{1,0:T(8,128)(2,1)} %get-tuple-element.31.res_ref, f32[1,3072]{1,0:T(1,128)} %get-tuple-element.73.sa_ref, ...), custom_call_target="tpu_custom_call" | custom-call | flops 49999998976 | bytes 10000000 | tf_op jit(solution)/shard_map/project_reduce/pallas_call | solution.py:500
  195.8 10.4 %convolution_convert_fusion.3 = bf16[512,1536]{1,0:T(8,128)(2,1)} fusion(bf16[512,3072]{1,0:T(8,128)(2,1)} %get-tuple-element.33, bf16[3072,1536]{1,0:T(8,128)(2,1)} %all-gather.5.cloned.1.call-done), kind=kOutput, calls=%fused_computation.43 | convolution fusion | flops 4832624640 | bytes 14155776 | tf_op jit(solution)/shard_map/dot_general | solution.py:548
  206.2 10.4 %fusion.13.a_ref = bf16[512,1536]{1,0:T(8,128)(2,1)} fusion(bf16[512,1536]{1,0:T(8,128)(2,1)} %convolution_convert_fusion.3, bf16[512,3072]{1,0:T(8,128)(2,1)S(1)} %copy-done.22, bf16[3072,1536]{1,0:T(8,128)(2,1)} %all-gather.7.cloned.1.call-done), kind=kOutput, calls=%fused_computation.32 | convolution fusion | flops 4842061824 | bytes 15728640 | tf_op jit(solution)/shard_map/dot_general | solution.py:549
  216.6 76.0 %project_reduce.5 = (bf16[32,3072]{1,0:T(8,128)(2,1)}, bf16[512,3072]{1,0:T(8,128)(2,1)}, bf16[3072,768]{1,0:T(8,128)(2,1)}, bf16[2048,384]{1,0:T(8,128)(2,1)}) custom-call(bf16[512,1536]{1,0:T(8,128)(2,1)} %fusion.13.a_ref, bf16[8,1536,384]{2,1,0:T(8,128)(2,1)} %bitcast.50, bf16[32,3072]{1,0:T(8,128)(2,1)} %get-tuple-element.37.res_ref, ...), custom_call_target="tpu_custom_call" | custom-call | flops 49999998976 | bytes 10000000 | tf_op jit(solution)/shard_map/project_reduce/pallas_call | solution.py:500
  292.6 5.9 %convolution_convert_fusion.4 = bf16[512,768]{1,0:T(8,128)(2,1)S(1)} fusion(bf16[512,3072]{1,0:T(8,128)(2,1)} %get-tuple-element.38, bf16[3072,768]{1,0:T(8,128)(2,1)} %get-tuple-element.39), kind=kOutput, calls=%fused_computation.44 | convolution fusion | flops 2416312320 | bytes 8650752 | tf_op jit(solution)/shard_map/dot_general | solution.py:535
  299.7 1.5 fusion.56
  301.9 42.8 %exchange_kv.3 = (bf16[4096,256]{1,0:T(8,128)(2,1)}, bf16[4096,256]{1,0:T(8,128)(2,1)}) custom-call(bf16[512,256]{1,0:T(8,128)(2,1)} %pad_maximum_fusion.3.k_ref, bf16[512,256]{1,0:T(8,128)(2,1)} %slice.114.v_ref), custom_call_target="tpu_custom_call" | custom-call | flops 20000000000 | bytes 10000000 | tf_op jit(solution)/shard_map/exchange_kv/pallas_call | solution.py:241
  344.8 4.7 fusion.75
  351.1 2.5 fusion.21.a_ref
  353.6 68.1 %project_reduce.6 = (bf16[32,3072]{1,0:T(8,128)(2,1)}, bf16[512,3072]{1,0:T(8,128)(2,1)}, bf16[12288,384]{1,0:T(8,128)(2,1)}) custom-call(bf16[512,256]{1,0:T(8,128)(2,1)} %fusion.21.a_ref, bf16[8,256,384]{2,1,0:T(8,128)(2,1)} %bitcast.53, bf16[32,3072]{1,0:T(8,128)(2,1)} %get-tuple-element.43.res_ref, f32[1,3072]{1,0:T(1,128)} %get-tuple-element.69.sa_ref, ...), custom_call_target="tpu_custom_call" | custom-call | flops 49999998976 | bytes 10000000 | tf_op jit(solution)/shard_map/project_reduce/pallas_call | solution.py:500
  421.7 10.4 %convolution_convert_fusion.1 = bf16[512,1536]{1,0:T(8,128)(2,1)} fusion(bf16[512,3072]{1,0:T(8,128)(2,1)} %get-tuple-element.44, bf16[3072,1536]{1,0:T(8,128)(2,1)} %all-gather.9.cloned.1.call-done), kind=kOutput, calls=%fused_computation.41 | convolution fusion | flops 4832624640 | bytes 14155776 | tf_op jit(solution)/shard_map/dot_general | solution.py:548
  432.1 10.4 %fusion.20.a_ref = bf16[512,1536]{1,0:T(8,128)(2,1)} fusion(bf16[512,1536]{1,0:T(8,128)(2,1)} %convolution_convert_fusion.1, bf16[512,3072]{1,0:T(8,128)(2,1)S(1)} %copy-done.23, bf16[3072,1536]{1,0:T(8,128)(2,1)} %all-gather.11.cloned.1.call-done), kind=kOutput, calls=%fused_computation.39 | convolution fusion | flops 4842061824 | bytes 15728640 | tf_op jit(solution)/shard_map/dot_general | solution.py:549
  442.6 76.6 %project_reduce.7 = bf16[512,3072]{1,0:T(8,128)(2,1)} custom-call(bf16[512,1536]{1,0:T(8,128)(2,1)} %fusion.20.a_ref, bf16[8,1536,384]{2,1,0:T(8,128)(2,1)} %bitcast.51, bf16[32,3072]{1,0:T(8,128)(2,1)} %get-tuple-element.48.res_ref, f32[1,3072]{1,0:T(1,128)} %get-tuple-element.67.sa_ref.sb_ref, f32[1,3072]{1,0:T(1,128)} %get-tuple-element.67.sa_ref.sb_ref), custom_call_target="tpu_custom_call" | custom-call | flops 49999998976 | bytes 10000000 | tf_op jit(solution)/shard_map/project_reduce/pallas_call | solution.py:500
  519.2 2.6 copy.18
  521.9 2.1 copy.16
  525.2 2.5 pad_maximum_fusion
  529.0 2.4 pad_maximum_fusion.1
  (81 shorter events, 15.4 us)
Async XLA Ops:
  7.2 188.6 %all-gather.5.cloned.1.call-start = ((), (), s32[]{:S(2)}) async-start(), calls=%async_computation | async-start | bytes 10616832 | tf_op jit(solution)/shard_map/all_gather | solution.py:526
  53.1 153.0 %all-gather.7.cloned.1.call-start = ((), (), s32[]{:S(2)}) async-start(), calls=%async_computation.1 | async-start | bytes 10616832 | tf_op jit(solution)/shard_map/all_gather | solution.py:526
  53.9 367.8 %all-gather.9.cloned.1.call-start = ((), (), s32[]{:S(2)}) async-start(), calls=%async_computation.2 | async-start | bytes 10616832 | tf_op jit(solution)/shard_map/all_gather | solution.py:526
  54.6 377.5 %all-gather.11.cloned.1.call-start = ((), (), s32[]{:S(2)}) async-start(), calls=%async_computation.3 | async-start | bytes 10616832 | tf_op jit(solution)/shard_map/all_gather | solution.py:526
  55.2 7.5 %copy-start.14 = (f32[2,2,256]{2,1,0:T(2,128)S(1)}, f32[2,2,256]{2,1,0:T(2,128)}, u32[]{:S(2)}) copy-start(f32[2,2,256]{2,1,0:T(2,128)} %param.23) | copy-start | bytes 12292
  55.2 8.1 %copy-start.18 = (s32[4096]{0:T(1024)S(1)}, s32[4096]{0:T(1024)}, u32[]{:S(2)}) copy-start(s32[4096]{0:T(1024)} %param.14) | copy-start | bytes 49156
  55.2 8.8 %copy-start.20 = (s32[4096]{0:T(1024)S(1)}, s32[4096]{0:T(1024)}, u32[]{:S(2)}) copy-start(s32[4096]{0:T(1024)} %param.13) | copy-start | bytes 49156
  55.3 8.8 %copy-start.8 = (f32[8,3072]{1,0:T(8,128)S(1)}, f32[8,3072]{1,0:T(8,128)}, u32[]{:S(2)}) copy-start(f32[8,3072]{1,0:T(8,128)} %get-tuple-element.32) | copy-start | bytes 294916
  64.0 46.3 %copy-start.10 = (s32[512]{0:T(512)}, s32[512]{0:T(512)S(1)}, u32[]{:S(2)}) copy-start(s32[512]{0:T(512)S(1)} %get-tuple-element.54) | copy-start | bytes 6148
  64.1 46.2 %copy-start.15 = (s32[512]{0:T(512)}, s32[512]{0:T(512)S(1)}, u32[]{:S(2)}) copy-start(s32[512]{0:T(512)S(1)} %dynamic_slice.10) | copy-start | bytes 6148
  195.8 10.4 %copy-start.22 = (bf16[512,3072]{1,0:T(8,128)(2,1)S(1)}, bf16[512,3072]{1,0:T(8,128)(2,1)}, u32[]{:S(2)}) copy-start(bf16[512,3072]{1,0:T(8,128)(2,1)} %get-tuple-element.33) | copy-start | bytes 9437188
  292.6 6.9 %copy-start.12 = (f32[1,1,256]{2,1,0:T(1,128)S(1)}, f32[1,1,256]{2,1,0:T(1,128)}, u32[]{:S(2)}) copy-start(f32[1,1,256]{2,1,0:T(1,128)} %get-tuple-element.74) | copy-start | bytes 3076
  292.6 6.9 %copy-start.13 = (f32[1,1,256]{2,1,0:T(1,128)S(1)}, f32[1,1,256]{2,1,0:T(1,128)}, u32[]{:S(2)}) copy-start(f32[1,1,256]{2,1,0:T(1,128)} %get-tuple-element.77) | copy-start | bytes 3076
  292.6 7.1 %copy-start.9 = (f32[512]{0:T(512)S(1)}, f32[512]{0:T(512)}, u32[]{:S(2)}) copy-start(f32[512]{0:T(512)} %get-tuple-element.53) | copy-start | bytes 6148
  292.6 7.1 %copy-start.17 = (f32[128]{0:T(128)S(1)}, f32[128]{0:T(128)}, u32[]{:S(2)}) copy-start(f32[128]{0:T(128)} %broadcast_power_fusion) | copy-start | bytes 1540
  301.9 42.8 %copy-start.11 = (s32[512]{0:T(512)S(1)}, s32[512]{0:T(512)}, u32[]{:S(2)}) copy-start(s32[512]{0:T(512)} %copy-done.10) | copy-start | bytes 6148
  301.9 42.8 %copy-start.16 = (s32[512]{0:T(512)S(1)}, s32[512]{0:T(512)}, u32[]{:S(2)}) copy-start(s32[512]{0:T(512)} %copy-done.15) | copy-start | bytes 6148
  301.9 42.8 %copy-start.19 = (s32[4096]{0:T(1024)S(1)}, s32[4096]{0:T(1024)}, u32[]{:S(2)}) copy-start(s32[4096]{0:T(1024)} %param.14) | copy-start | bytes 49156
  301.9 42.9 %copy-start.21 = (s32[4096]{0:T(1024)S(1)}, s32[4096]{0:T(1024)}, u32[]{:S(2)}) copy-start(s32[4096]{0:T(1024)} %param.13) | copy-start | bytes 49156
  421.7 10.4 %copy-start.23 = (bf16[512,3072]{1,0:T(8,128)(2,1)S(1)}, bf16[512,3072]{1,0:T(8,128)(2,1)}, u32[]{:S(2)}) copy-start(bf16[512,3072]{1,0:T(8,128)(2,1)} %get-tuple-element.44) | copy-start | bytes 9437188
  521.9 3.4 copy-start.7
  525.2 2.5 copy-start.3
  525.2 3.7 copy-start.6
  527.7 3.6 copy-start.1
  (4 other events, 7.2 us)
Sparse Core Ops, SparseCore 0:
  53.3 70.0 all-gather.4
  125.0 79.2 all-gather.6
  205.9 69.0 all-gather.8
  276.6 73.0 all-gather.10

commit v5 on v4

--- a/solution.py
+++ b/solution.py
@@ -14,7 +14,7 @@
 LOCAL_BASE = 10000.0
 MESH = pl.DeviceIdType.MESH
 SIDE = 4
-VMEM_LIMIT = 60 * 1024 * 1024
+VMEM_LIMIT = 63 * 1024 * 1024
 
 
 def norm(values, scale_row):
@@ -108,15 +108,16 @@
         start = torus.at(q, da, db) * rows + (half if part == 2 else 0)
         return h_ref.at[pl.ds(pl.multiple_of(start, half), rows if part == 0 else half), pl.ds(q * cols, cols)]
 
-    def ring(q, axis, base, slot, offsets):
+    def ring(q, axis, base, offsets):
         def make(k, da, db, part, step):
             v = view(q, da, db, part)
             return remote(v, v, send.at[q, base, k], recv.at[q, base, k], torus.peer(axis, step))
+
         along = (lambda off: (off, offsets)) if axis == q else (lambda off: (offsets, off))
         return (make(0, *along(0), 0, 1), make(1, *along(0), 0, -1), make(2, *along(-1), 1, 1), make(3, *along(1), 2, -1))
 
-    first = [ring(q, 1 - q, 0, 0, 0) for q in (0, 1)]
-    second = [[ring(q, q, 1 + n, 0, off) for n, off in enumerate((0, -1, 1, 2))] for q in (0, 1)]
+    first = [ring(q, 1 - q, 0, 0) for q in (0, 1)]
+    second = [[ring(q, q, 1 + n, off) for n, off in enumerate((0, -1, 1, 2))] for q in (0, 1)]
 
     def begin(copies):
         copies[0].start()
@@ -225,6 +226,9 @@
 VMEM = pl.BlockSpec(memory_space=pltpu.VMEM)
 ANY = pl.BlockSpec(memory_space=pl.ANY)
 PIECES = 4
+WIDE = 3
+NEED = ((2, 2), (2, 1), (2, -1), (2, 0), (1, 2), (-1, 2), (0, 2), (1, 1),
+        (1, -1), (1, 0), (-1, 1), (-1, -1), (-1, 0), (0, 1), (0, -1), (0, 0))
 
 
 def params(cid):
@@ -241,7 +245,7 @@
     return pl.pallas_call(
         functools.partial(exchange_kernel, n_model),
         out_shape=(full, full), in_specs=[VMEM] * 2, out_specs=(VMEM, VMEM),
-        scratch_shapes=exchange_sems(2), compiler_params=params(cid), cost_estimate=cost(20_000_000_000), name='exchange_kv',
+        scratch_shapes=exchange_sems(2), compiler_params=params(cid), cost_estimate=cost(100_000_000), name='exchange_kv',
     )(k, v)
 
 
@@ -270,11 +274,11 @@
 
 
 def start_kernel(n_model, hid_ref, sc_ref, wq_ref, wk_ref, wv_ref, wo_ref, wg_ref, wu_ref,
-                 x_ref, h_ref, sca_ref, wqkv_ref, woa_ref, g0_ref, u0_ref, g1_ref, u1_ref,
+                 x_ref, h_ref, sca_ref, wqkv_ref, woa_ref, u0_ref, g1_ref, u1_ref,
                  xin, scin, stage, xs, xr, ss, sr, ls, hs, hr, es, er):
     torus, line = Torus(), Line(n_model)
     rows = x_ref.shape[0]
-    shards = ((wg_ref, 0, g0_ref), (wu_ref, 0, u0_ref), (wg_ref, 1, g1_ref), (wu_ref, 1, u1_ref))
+    shards = ((wu_ref, 0, u0_ref), (wg_ref, 1, g1_ref), (wu_ref, 1, u1_ref))
     loads = [pltpu.make_async_copy(ref.at[layer], stage.at[k], ls.at[k]) for k, (ref, layer, _) in enumerate(shards)]
     stores = [pltpu.make_async_copy(stage.at[k], dst, ls.at[k]) for k, (_, _, dst) in enumerate(shards)]
     for c in loads:
@@ -319,17 +323,20 @@
         out_shape=(jax.ShapeDtypeStruct((rows, width), hidden_mine.dtype),
                    jax.ShapeDtypeStruct((rows * SIDE * SIDE, width), hidden_mine.dtype),
                    jax.ShapeDtypeStruct((scales.shape[0], width), scales.dtype)) + attn_weight_shapes(wq, wo, n_model)
-        + (jax.ShapeDtypeStruct(wg.shape[1:], wg.dtype),) * 4,
-        in_specs=[VMEM] * 6 + [ANY] * 2, out_specs=(VMEM,) * 5 + (ANY,) * 4,
+        + (jax.ShapeDtypeStruct(wg.shape[1:], wg.dtype),) * 3,
+        in_specs=[VMEM] * 6 + [ANY] * 2, out_specs=(VMEM,) * 5 + (ANY,) * 3,
         scratch_shapes=[pltpu.VMEM(hidden_mine.shape, hidden_mine.dtype), pltpu.VMEM((n_model,) + scales.shape, scales.dtype),
-                        pltpu.VMEM((4,) + wg.shape[1:], wg.dtype)]
-        + peer_sems + [pltpu.SemaphoreType.DMA((4,))] + GATHER_SEMS + exchange_sems(2),
-        compiler_params=params(cid), cost_estimate=cost(30_000_000_000), name='start',
+                        pltpu.VMEM((3,) + wg.shape[1:], wg.dtype)]
+        + peer_sems + [pltpu.SemaphoreType.DMA((3,))] + GATHER_SEMS + exchange_sems(2),
+        compiler_params=params(cid), cost_estimate=cost(100_000_000), name='start',
     )(hidden_mine, scales, wq, wk, wv, wo, wg, wu)
 
 
-def project_kernel(n_model, final, attn, down, a_ref, w_ref, res_ref, sa_ref, sb_ref, *rest):
+def project_kernel(n_model, ffn, final, attn, down, a_ref, w_ref, res_ref, sa_ref, sb_ref, *rest):
     rest = list(rest)
+    if ffn:
+        wg_any, wu_any = rest[:2]
+        rest = rest[2:]
     fetch = attn or down is not None
     if attn:
         wq_ref, wk_ref, wv_ref, wo_ref = rest[:4]
@@ -346,10 +353,27 @@
         wda_ref = rest.pop(0)
     far, right, left, own, from_l1, from_r1, from_l, from_r, q_l1, q_r1, q_l, q_r, s1, r1, s2, r2, hs, hr = rest[:18]
     rest = rest[18:]
+    if ffn:
+        hp, mid, wg_ref, wu_ref, wd_ref2, fs = rest[:6]
+        rest = rest[6:]
     torus, line = Torus(), Line(n_model)
     rows, width = res_ref.shape
     half = rows // 2
     cols = width // 2
+    if ffn:
+        span = wg_any.shape[1] // WIDE
+
+        def wide_load(k, n):
+            src, dst = ((wg_any, wg_ref), (wu_any, wu_ref))[k]
+            at = pl.ds(pl.multiple_of(n * span, span), span)
+            return pltpu.make_async_copy(src.at[:, at], dst.at[:, at], fs.at[k, n])
+
+        for n in range(WIDE):
+            wide_load(0, n).start()
+            wide_load(1, n).start()
+        down_load = pltpu.make_async_copy(w_ref, wd_ref2, fs.at[2, 0])
+        down_load.start()
+        w_ref = wd_ref2
     if final:
         meet(torus, others(line))
     elif fetch:
@@ -358,8 +382,31 @@
         meet(torus, ())
     order = (2, 1, -1, 0)
 
+    def feed(group):
+        these = slice(group * SIDE * rows, (group + 1) * SIDE * rows)
+
+        def step(n, carry):
+            if group == 0:
+                wide_load(0, n).wait()
+                wide_load(1, n).wait()
+            at = pl.ds(pl.multiple_of(n * span, span), span)
+            lhs = hp[these, :]
+            g = jnp.dot(lhs, wg_ref[:, at], preferred_element_type=jnp.float32).astype(jnp.bfloat16)
+            u = jnp.dot(lhs, wu_ref[:, at], preferred_element_type=jnp.float32).astype(jnp.bfloat16)
+            act = jax.nn.gelu(g.astype(jnp.float32), approximate=True)
+            mid[these, at] = (act * u.astype(jnp.float32)).astype(jnp.bfloat16)
+            return carry
+
+        lax.fori_loop(0, WIDE, step, 0)
+
+    def operand(q, off, o):
+        if ffn:
+            at = NEED.index((off, o) if q == 0 else (o, off)) * rows
+            return mid[at:at + rows, :]
+        return a_ref[pl.ds(pl.multiple_of(torus.at(q, off, o) * rows, rows), rows), :]
+
     def product(q, off, dst):
-        lhs = jnp.concatenate([a_ref[pl.ds(pl.multiple_of(torus.at(q, off, o) * rows, rows), rows), :] for o in order], axis=0)
+        lhs = jnp.concatenate([operand(q, off, o) for o in order], axis=0)
         piece = w_ref.shape[2]
         per = cols // piece
         for p in range(per):
@@ -381,7 +428,14 @@
         mine, ls = rest[2:]
         load = pltpu.make_async_copy(wd_ref.at[down], mine, ls.at[0])
         load.start()
-    for q in (0, 1):
+    if ffn:
+        for k, (dy, dz) in enumerate(NEED):
+            hp[k * rows:(k + 1) * rows, :] = a_ref[pl.ds(pl.multiple_of(torus.at(0, dy, dz) * rows, rows), rows), :]
+    for q in (0, 1):
+        if ffn:
+            feed(q)
+            if q == 0:
+                down_load.wait()
         product(q, 2, far)
         for n in range(SIDE):
             ring1(q, n, 0).start()
@@ -398,12 +452,17 @@
         ex = Exchange(line, [(wda_ref, stride, k * piece, piece, mine.at[pl.ds(k * piece, piece)]) for k in range(PIECES)], rest[0], rest[1])
         ex.begin()
     for q in (0, 1):
+        if ffn and q == 0:
+            feed(2)
         product(q, 1, right)
-        product(q, -1, left)
         for n in range(SIDE):
             ring1(q, n, 0).wait_recv()
             right[q, n, 0:half] += from_l1[q, n]
             ring1(q, n, 2).start()
+        if ffn and q == 0:
+            feed(3)
+        product(q, -1, left)
+        for n in range(SIDE):
             ring1(q, n, 1).wait_recv()
             left[q, n, half:rows] += from_r1[q, n]
             ring1(q, n, 3).start()
@@ -467,7 +526,7 @@
                 ring1(q, n, k).wait_send()
 
 
-def project(a, w, resid, scale_a, scale_b, n_model, cid, final=False, attn=None, down=None, layer=None):
+def project(a, w, resid, scale_a, scale_b, n_model, cid, wide=None, final=False, attn=None, down=None, layer=None):
     rows, width = resid.shape
     cols = width // 2
     half = rows // 2
@@ -481,6 +540,13 @@
     out_shape = (h_shape,) if final else (jax.ShapeDtypeStruct((rows, width), jnp.bfloat16), h_shape)
     args = (a, w, resid, scale_a, scale_b)
     in_specs, out_specs = [VMEM] * 5, (VMEM,) * len(out_shape)
+    if wide is not None:
+        args += tuple(wide)
+        in_specs[1] = ANY
+        in_specs += [ANY] * 2
+        gate = wide[0]
+        scratch += [pltpu.VMEM(a.shape, a.dtype), pltpu.VMEM((a.shape[0], gate.shape[1]), a.dtype), pltpu.VMEM(gate.shape, gate.dtype),
+                    pltpu.VMEM(gate.shape, gate.dtype), pltpu.VMEM(w.shape, w.dtype), pltpu.SemaphoreType.DMA((3, WIDE))]
     if attn is not None:
         args += tuple(attn)
         in_specs += [VMEM] * 4
@@ -498,9 +564,9 @@
         part = (n_model, rows, width // n_model)
         scratch += [pltpu.VMEM(part, jnp.bfloat16)] * 2 + [pltpu.SemaphoreType.DMA((n_model,))] * 2
     return pl.pallas_call(
-        functools.partial(project_kernel, n_model, final, attn is not None, layer),
+        functools.partial(project_kernel, n_model, wide is not None, final, attn is not None, layer),
         out_shape=out_shape, in_specs=in_specs, out_specs=out_specs, scratch_shapes=scratch,
-        compiler_params=params(cid), cost_estimate=cost(50_000_000_000), name='project_reduce',
+        compiler_params=params(cid), cost_estimate=cost(100_000_000), name='project_reduce',
     )(*args)
 
 
@@ -513,7 +579,6 @@
 
     def body(hidden_in, seg_ids, positions, w_query, w_key, w_value, w_out, w_gate, w_up, w_down, norm_scales, qk_scales):
         n_tok, width_loc = hidden_in.shape
-        width = width_loc * n_model
         head_dim = qk_scales.shape[-1]
         tok_m = n_tok // n_model
         tok_own = tok_m // n_heads
@@ -522,8 +587,9 @@
 
         attn_shards = (w_query, w_key, w_value, w_out)
         mine = lax.dynamic_index_in_dim(hidden_in.reshape(n_model, n_heads, tok_own, width_loc), hd, 1, keepdims=False)
+        gate_0 = lax.all_gather(w_gate[0], 'model', axis=0, tiled=True)
         resid, h, scales, wqkv, wo, *shards = start(mine, norm_scales.reshape(-1, width_loc), *attn_shards, w_gate, w_up, 0)
-        wide = [lax.all_gather(w, 'model', axis=0, tiled=True) for w in shards]
+        wide = [gate_0, lax.all_gather(shards[0], 'model', axis=0, tiled=True)]
 
         pos_m = lax.dynamic_slice_in_dim(positions, md * tok_m, tok_m)
         seg_m = lax.dynamic_slice_in_dim(seg_ids, md * tok_m, tok_m)
@@ -545,13 +611,12 @@
             row = 4 * l
             resid, h, wd = project(o, wo, resid, scales[row + 1:row + 2], scales[row + 2:row + 3], n_model, 2 + 3 * l, down=w_down, layer=l)
             wd = wd.reshape(n_model, w_down.shape[1], width_loc)
-            g = jnp.dot(h, wide[2 * l], preferred_element_type=jnp.float32).astype(jnp.bfloat16)
-            u = jnp.dot(h, wide[2 * l + 1], preferred_element_type=jnp.float32).astype(jnp.bfloat16)
-            mid = (jax.nn.gelu(g.astype(jnp.float32), approximate=True) * u.astype(jnp.float32)).astype(jnp.bfloat16)
             if l == 0:
-                resid, h, wqkv, wo = project(mid, wd, resid, scales[3:4], scales[4:5], n_model, 3, attn=attn_shards)
+                h, *late = lax.optimization_barrier((h, *shards[1:]))
+                wide_next = [lax.all_gather(w, 'model', axis=0, tiled=True) for w in late]
+                resid, h, wqkv, wo = project(h, wd, resid, scales[3:4], scales[4:5], n_model, 3, wide=wide, attn=attn_shards)
             else:
-                out, = project(mid, wd, resid, scales[7:8], scales[7:8], n_model, 6, final=True)
+                out, = project(h, wd, resid, scales[7:8], scales[7:8], n_model, 6, wide=wide_next, final=True)
         out = out.reshape(tok_m, n_model, width_loc).transpose(1, 0, 2).reshape(n_tok, width_loc)
         return out, jnp.stack(keys), jnp.stack(values)
 

time: 542 us -> 530 us (0.978)
  matrix products: 67.8 us -> 26.3 us
  Pallas kernels: 426 us -> 449 us
  waiting for transfers between devices: 1.96 us -> 8.58 us
    dot_general x4 -> x0, matrix products: 41.6 us -> none  [the longest x2 20.8 us: body(): jnp.dot(h, wide[2 * l], preferred_element_type=jnp.float32)]
    pallas_call x4, Pallas kernels: 297 us -> 320 us  [project(): pl.pallas_call(functools.partial(project_kernel, n_model, wide is not Non...]
    all_gather x4, waiting for transfers between devices: 0.05 us -> 8.01 us  [the longest x1 7.95 us: body(): gate_0 = lax.all_gather(w_gate[0], 'model', axis=0, tiled=True)]
  transfers between devices with their start and end apart: 4 -> 4, of which waited for: 0 -> 1; matrix products, arithmetic and copies ran while one was open for 13% -> 7% of each run, Pallas kernels for 57% -> 61%
where the time goes in v5:
time: 530 us; the launch traced here: 526 us
  Pallas kernels  449 us (85%)
  matrix products  26.3 us (5%)
  local copies, waits for them, and re-layouts  15.1 us (3%)
  between operations  14.3 us (3%)
  other arithmetic  12.7 us (2%)
  waiting for transfers between devices  8.58 us (2%)
    pallas_call x4, Pallas kernels, project(): pl.pallas_call(functools.partial(project_kernel, n_model, wide is not Non...  320 us
    pallas_call x2, Pallas kernels, exchange(): pl.pallas_call(functools.partial(exchange_kernel, n_model), out_shape=(fu...  85.9 us
    pallas_call x1, Pallas kernels, start(): pl.pallas_call(functools.partial(start_kernel, n_model), out_shape=(jax.S...  43.4 us
    dot_general x2, matrix products, body(): jnp.dot(h, wqkv, preferred_element_type=jnp.float32).astype(jnp.bfloat16)  11.8 us
  transfers between devices with their start and end apart: 4, of which 1 were waited for; matrix products, arithmetic and copies ran while one was open for 7% of the time, Pallas kernels for 61%

profile of v5, /device:TPU:0, one launch (start us, length us, event | category | flops | bytes accessed | tf_op | source)
XLA Modules:
  0.0 526.4 jit_solution(5120493478061361131)
XLA Ops:
  7.2 1.3 reshape.112.sc_ref
  8.5 1.6 dynamic-slice_bitcast_fusion.hid_ref
  10.2 43.4 %start.1 = (bf16[32,3072]{1,0:T(8,128)(2,1)}, bf16[512,3072]{1,0:T(8,128)(2,1)}, f32[8,3072]{1,0:T(8,128)}, bf16[3072,768]{1,0:T(8,128)(2,1)}, bf16[2048,384]{1,...) custom-call(bf16[8,32,384]{2,1,0:T(8,128)(2,1)} %dynamic-slice_bitcast_fusion.hid_r, ...), custom_call_target="tpu_custom_call" | custom-call | flops 100000000 | bytes 10000000 | tf_op jit(solution)/shard_map/start/pallas_call | solution.py:321
  53.6 2.4 slice.92
  56.1 5.9 %convolution_convert_fusion.1 = bf16[512,768]{1,0:T(8,128)(2,1)S(1)} fusion(bf16[512,3072]{1,0:T(8,128)(2,1)} %get-tuple-element.28, bf16[3072,768]{1,0:T(8,128)(2,1)} %get-tuple-element.29), kind=kOutput, calls=%fused_computation.19 | convolution fusion | flops 2416312320 | bytes 8650752 | tf_op jit(solution)/shard_map/dot_general | solution.py:601
  63.4 1.4 fusion.34
  65.5 42.9 %exchange_kv.2 = (bf16[4096,256]{1,0:T(8,128)(2,1)}, bf16[4096,256]{1,0:T(8,128)(2,1)}) custom-call(bf16[512,256]{1,0:T(8,128)(2,1)} %pad_maximum_fusion.2.k_ref, bf16[512,256]{1,0:T(8,128)(2,1)} %slice.111.v_ref), custom_call_target="tpu_custom_call" | custom-call | flops 100000000 | bytes 10000000 | tf_op jit(solution)/shard_map/exchange_kv/pallas_call | solution.py:245
  108.5 4.7 fusion.60
  115.2 2.5 fusion.8.a_ref
  117.6 76.6 %project_reduce.4 = (bf16[32,3072]{1,0:T(8,128)(2,1)}, bf16[512,3072]{1,0:T(8,128)(2,1)}, bf16[12288,384]{1,0:T(8,128)(2,1)}) custom-call(bf16[512,256]{1,0:T(8,128)(2,1)} %fusion.8.a_ref, bf16[8,256,384]{2,1,0:T(8,128)(2,1)} %bitcast.41, bf16[32,3072]{1,0:T(8,128)(2,1)} %get-tuple-element.33.res_ref, f32[1,3072]{1,0:T(1,128)} %get-tuple-element.77.sa_ref, ...), custom_call_target="tpu_custom_call" | custom-call | flops 100000000 | bytes 10000000 | tf_op jit(solution)/shard_map/project_reduce/pallas_call | solution.py:566
  194.9 7.9 %all-gather.12.cloned.1.call-done = bf16[1,3072,1536]{2,1,0:T(8,128)(2,1)} async-done(((bf16[1,384,1536]{2,1,0:T(8,128)(2,1)}), bf16[1,3072,1536]{2,1,0:T(8,128)(2,1)}) %all-gather.12.cloned.1.call-update) | async-done | bytes 9437200 | tf_op jit(solution)/shard_map/all_gather | solution.py:590
  202.9 88.8 %project_reduce.5 = (bf16[32,3072]{1,0:T(8,128)(2,1)}, bf16[512,3072]{1,0:T(8,128)(2,1)}, bf16[3072,768]{1,0:T(8,128)(2,1)}, bf16[2048,384]{1,0:T(8,128)(2,1)}) custom-call(bf16[512,3072]{1,0:T(8,128)(2,1)} %get-tuple-element.38.a_ref, bf16[8,1536,384]{2,1,0:T(8,128)(2,1)} %bitcast.34, bf16[32,3072]{1,0:T(8,128)(2,1)} %get-tuple-element.40.res_ref, ...), custom_call_target="tpu_custom_call" | custom-call | flops 100000000 | bytes 10000000 | tf_op jit(solution)/shard_map/project_reduce/pallas_call | solution.py:566
  291.6 5.9 %convolution_convert_fusion = bf16[512,768]{1,0:T(8,128)(2,1)S(1)} fusion(bf16[512,3072]{1,0:T(8,128)(2,1)} %get-tuple-element.42, bf16[3072,768]{1,0:T(8,128)(2,1)} %get-tuple-element.43), kind=kOutput, calls=%fused_computation.18 | convolution fusion | flops 2416312320 | bytes 8650752 | tf_op jit(solution)/shard_map/dot_general | solution.py:601
  298.7 1.4 fusion.42
  300.9 43.0 %exchange_kv.3 = (bf16[4096,256]{1,0:T(8,128)(2,1)}, bf16[4096,256]{1,0:T(8,128)(2,1)}) custom-call(bf16[512,256]{1,0:T(8,128)(2,1)} %pad_maximum_fusion.3.k_ref, bf16[512,256]{1,0:T(8,128)(2,1)} %slice.118.v_ref), custom_call_target="tpu_custom_call" | custom-call | flops 100000000 | bytes 10000000 | tf_op jit(solution)/shard_map/exchange_kv/pallas_call | solution.py:245
  343.9 4.8 fusion.61
  348.7 1.3 fusion.4
  350.3 2.5 fusion.7.a_ref
  352.8 69.3 %project_reduce.6 = (bf16[32,3072]{1,0:T(8,128)(2,1)}, bf16[512,3072]{1,0:T(8,128)(2,1)}, bf16[12288,384]{1,0:T(8,128)(2,1)}) custom-call(bf16[512,256]{1,0:T(8,128)(2,1)} %fusion.7.a_ref, bf16[8,256,384]{2,1,0:T(8,128)(2,1)} %bitcast.42, bf16[32,3072]{1,0:T(8,128)(2,1)} %get-tuple-element.47.res_ref, f32[1,3072]{1,0:T(1,128)} %get-tuple-element.73.sa_ref, ...), custom_call_target="tpu_custom_call" | custom-call | flops 100000000 | bytes 10000000 | tf_op jit(solution)/shard_map/project_reduce/pallas_call | solution.py:566
  422.2 85.4 %project_reduce.7 = bf16[512,3072]{1,0:T(8,128)(2,1)} custom-call(bf16[512,3072]{1,0:T(8,128)(2,1)} %get-tuple-element.48.a_ref, bf16[8,1536,384]{2,1,0:T(8,128)(2,1)} %bitcast.35, bf16[32,3072]{1,0:T(8,128)(2,1)} %get-tuple-element.50.res_ref, f32[1,3072]{1,0:T(1,128)} %get-tuple-element.71.sa_ref.sb_ref, f32[1,3072]{1,0:T(1,128)} %get-tuple-element.71.sa_ref.sb_ref, ...), custom_call_target="tpu_custom_call" | custom-call | flops 100000000 | bytes 10000000 | tf_op jit(solution)/shard_map/project_reduce/pallas_call | solution.py:566
  507.6 2.6 copy.18
  510.2 2.1 copy.16
  513.6 2.5 pad_maximum_fusion
  517.3 2.4 pad_maximum_fusion.1
  (50 shorter events, 9.6 us)
Async XLA Ops:
  7.2 187.8 %all-gather.6.cloned.1.call-start = ((), (), s32[]{:S(2)}) async-start(), calls=%async_computation | async-start | bytes 10616832 | tf_op jit(solution)/shard_map/all_gather | solution.py:592
  53.5 149.3 %all-gather.12.cloned.1.call-start = ((), (), s32[]{:S(2)}) async-start(), calls=%async_computation.3 | async-start | bytes 10616832 | tf_op jit(solution)/shard_map/all_gather | solution.py:590
  56.0 366.2 %all-gather.10.cloned.1.call-start = ((), (), s32[]{:S(2)}) async-start(), calls=%async_computation.2 | async-start | bytes 10616832 | tf_op jit(solution)/shard_map/all_gather | solution.py:616
  56.0 6.7 %copy-start.9 = (s32[4096]{0:T(1024)S(1)}, s32[4096]{0:T(1024)}, u32[]{:S(2)}) copy-start(s32[4096]{0:T(1024)} %param.13) | copy-start | bytes 49156
  56.0 6.7 %copy-start.8 = (s32[4096]{0:T(1024)S(1)}, s32[4096]{0:T(1024)}, u32[]{:S(2)}) copy-start(s32[4096]{0:T(1024)} %param.14) | copy-start | bytes 49156
  56.1 7.0 %copy-start.7 = (f32[2,2,256]{2,1,0:T(2,128)S(1)}, f32[2,2,256]{2,1,0:T(2,128)}, u32[]{:S(2)}) copy-start(f32[2,2,256]{2,1,0:T(2,128)} %param.23) | copy-start | bytes 12292
  113.2 1.3 copy-start.6
  113.2 2.0 copy-start
  194.3 227.9 %all-gather.8.cloned.1.call-start = ((), (), s32[]{:S(2)}) async-start(), calls=%async_computation.1 | async-start | bytes 10616832 | tf_op jit(solution)/shard_map/all_gather | solution.py:616
  348.7 1.6 copy-start.3
  510.2 2.1 copy-start.2
  510.2 3.4 copy-start.5
  513.5 2.5 copy-start.1
  513.6 3.7 copy-start.4
Sparse Core Ops, SparseCore 0:
  53.7 70.1 all-gather.5
  126.1 76.7 all-gather.11
  204.6 69.4 all-gather.9
  275.6 72.7 all-gather.7

commit v6 on v5

--- a/solution.py
+++ b/solution.py
@@ -100,12 +100,15 @@
 
 
 def gather_blocks(torus, h_ref, send, recv, between=lambda: None):
-    rows = h_ref.shape[0] // (SIDE * SIDE)
-    cols = h_ref.shape[1] // 2
+    apart = len(h_ref.shape) == 3
+    rows = h_ref.shape[-2] // (SIDE * SIDE)
+    cols = h_ref.shape[0 if apart else 1] // 2
     half = rows // 2
 
     def view(q, da, db, part):
         start = torus.at(q, da, db) * rows + (half if part == 2 else 0)
+        if apart:
+            return h_ref.at[pl.ds(q * cols, cols), pl.ds(pl.multiple_of(start, half), rows if part == 0 else half), :]
         return h_ref.at[pl.ds(pl.multiple_of(start, half), rows if part == 0 else half), pl.ds(q * cols, cols)]
 
     def ring(q, axis, base, offsets):
@@ -217,7 +220,8 @@
     here = pl.ds(pl.multiple_of(line.me * rows, rows), rows)
     ka_ref[here, :] = k_ref[...]
     va_ref[here, :] = v_ref[...]
-    ex = Exchange(line, [(ka_ref, rows, 0, rows, None), (va_ref, rows, 0, rows, None)], send, recv)
+    piece = rows // 2
+    ex = Exchange(line, [(ref, rows, at, piece, None) for at in (0, piece) for ref in (ka_ref, va_ref)], send, recv)
     ex.begin()
     ex.onward()
     ex.finish()
@@ -226,7 +230,7 @@
 VMEM = pl.BlockSpec(memory_space=pltpu.VMEM)
 ANY = pl.BlockSpec(memory_space=pl.ANY)
 PIECES = 4
-WIDE = 3
+WIDE = 6
 NEED = ((2, 2), (2, 1), (2, -1), (2, 0), (1, 2), (-1, 2), (0, 2), (1, 1),
         (1, -1), (1, 0), (-1, 1), (-1, -1), (-1, 0), (0, 1), (0, -1), (0, 0))
 
@@ -245,7 +249,7 @@
     return pl.pallas_call(
         functools.partial(exchange_kernel, n_model),
         out_shape=(full, full), in_specs=[VMEM] * 2, out_specs=(VMEM, VMEM),
-        scratch_shapes=exchange_sems(2), compiler_params=params(cid), cost_estimate=cost(100_000_000), name='exchange_kv',
+        scratch_shapes=exchange_sems(4), compiler_params=params(cid), cost_estimate=cost(100_000_000), name='exchange_kv',
     )(k, v)
 
 
@@ -354,8 +358,8 @@
     far, right, left, own, from_l1, from_r1, from_l, from_r, q_l1, q_r1, q_l, q_r, s1, r1, s2, r2, hs, hr = rest[:18]
     rest = rest[18:]
     if ffn:
-        hp, mid, wg_ref, wu_ref, wd_ref2, fs = rest[:6]
-        rest = rest[6:]
+        hp, mid, wg_ref, wu_ref, wd_ref2, lhs_ref, fs = rest[:7]
+        rest = rest[7:]
     torus, line = Torus(), Line(n_model)
     rows, width = res_ref.shape
     half = rows // 2
@@ -409,10 +413,25 @@
         lhs = jnp.concatenate([operand(q, off, o) for o in order], axis=0)
         piece = w_ref.shape[2]
         per = cols // piece
+        if ffn:
+            lhs_ref[...] = lhs
+
+            def step(p, carry):
+                res = jnp.dot(lhs_ref[...], w_ref[q * per + p], preferred_element_type=jnp.float32)
+                at = pl.ds(pl.multiple_of(p * piece, piece), piece)
+                for n in range(SIDE):
+                    dst[q, n, :, at] = res[n * rows:(n + 1) * rows]
+                return carry
+
+            lax.fori_loop(0, per, step, 0)
+            return
         for p in range(per):
             res = jnp.dot(lhs, w_ref[q * per + p], preferred_element_type=jnp.float32)
             for n in range(SIDE):
                 dst[q, n, :, p * piece:(p + 1) * piece] = res[n * rows:(n + 1) * rows]
+
+    def held(q):
+        return q == 1 or not ffn
 
     def ring1(q, n, k):
         src, dst, step = ((far.at[q, n, pl.ds(0, half)], from_l1.at[q, n], 1), (far.at[q, n, pl.ds(half, half)], from_r1.at[q, n], -1),
@@ -458,14 +477,16 @@
         for n in range(SIDE):
             ring1(q, n, 0).wait_recv()
             right[q, n, 0:half] += from_l1[q, n]
-            ring1(q, n, 2).start()
+            if n < 2 or not held(q):
+                ring1(q, n, 2).start()
         if ffn and q == 0:
             feed(3)
         product(q, -1, left)
         for n in range(SIDE):
             ring1(q, n, 1).wait_recv()
             left[q, n, half:rows] += from_r1[q, n]
-            ring1(q, n, 3).start()
+            if n < 2 or not held(q):
+                ring1(q, n, 3).start()
     for q in (0, 1):
         product(q, 0, own)
     if down is not None:
@@ -486,6 +507,10 @@
                 ring2(q, 1).wait_recv()
                 own[q, 2, half:rows] += q_r1[q]
                 ring2(q, 3).start()
+        for q in (0, 1):
+            if n < 2 and held(q):
+                ring1(q, n + 2, 2).start()
+                ring1(q, n + 2, 3).start()
     total = []
     for q in (0, 1):
         ring2(q, 2).wait_recv()
@@ -503,7 +528,8 @@
         copies = to_all(line, lambda step, peer: remote(outgo.at[peer], income.at[line.me], cs.at[step], cr.at[step], {'model': peer}))
         for c in copies:
             c.wait_recv()
-        h_ref[here, :] = jnp.concatenate([income[m] for m in range(n_model)], axis=1)
+        for m in range(n_model):
+            h_ref[m, here, :] = income[m]
     else:
         x_ref[...] = x_new
         h_ref[here, :] = norm(x_new.astype(jnp.float32), sb_ref[...]).astype(jnp.bfloat16)
@@ -536,7 +562,8 @@
 
     scratch = [f32(SIDE, rows)] * 4 + [f32(SIDE, half)] * 2 + [f32(SIDE, rows)] * 2 + [f32(half)] * 2 + [f32(rows)] * 2
     scratch += [pltpu.SemaphoreType.DMA((2, SIDE, 4))] * 2 + [pltpu.SemaphoreType.DMA((2, 4))] * 2 + GATHER_SEMS
-    h_shape = jax.ShapeDtypeStruct((rows * SIDE * SIDE, width), jnp.bfloat16)
+    h_dims = (n_model, rows * SIDE * SIDE, width // n_model) if final else (rows * SIDE * SIDE, width)
+    h_shape = jax.ShapeDtypeStruct(h_dims, jnp.bfloat16)
     out_shape = (h_shape,) if final else (jax.ShapeDtypeStruct((rows, width), jnp.bfloat16), h_shape)
     args = (a, w, resid, scale_a, scale_b)
     in_specs, out_specs = [VMEM] * 5, (VMEM,) * len(out_shape)
@@ -546,7 +573,8 @@
         in_specs += [ANY] * 2
         gate = wide[0]
         scratch += [pltpu.VMEM(a.shape, a.dtype), pltpu.VMEM((a.shape[0], gate.shape[1]), a.dtype), pltpu.VMEM(gate.shape, gate.dtype),
-                    pltpu.VMEM(gate.shape, gate.dtype), pltpu.VMEM(w.shape, w.dtype), pltpu.SemaphoreType.DMA((3, WIDE))]
+                    pltpu.VMEM(gate.shape, gate.dtype), pltpu.VMEM(w.shape, w.dtype),
+                    pltpu.VMEM((SIDE * rows, w.shape[1]), w.dtype), pltpu.SemaphoreType.DMA((3, WIDE))]
     if attn is not None:
         args += tuple(attn)
         in_specs += [VMEM] * 4
@@ -604,6 +632,9 @@
             q = apply_rope(norm(q.astype(jnp.float32), qk_scales[l, 0]), cos_tab, sin_tab).astype(jnp.bfloat16)
             k = apply_rope(norm(k.astype(jnp.float32), qk_scales[l, 1]), cos_tab, sin_tab).astype(jnp.bfloat16)
             k_all, v_all = exchange(k, v, n_model, 1 + 3 * l)
+            if l == 1:
+                k_all, up_last = lax.optimization_barrier((k_all, late[1]))
+                wide_next.append(lax.all_gather(up_last, 'model', axis=0, tiled=True))
             keys.append(k_all[:, None, :])
             values.append(v_all[:, None, :])
             o = attend(q, k_all, v_all, seg_m, pos_m, seg_ids, positions, window)
@@ -613,11 +644,11 @@
             wd = wd.reshape(n_model, w_down.shape[1], width_loc)
             if l == 0:
                 h, *late = lax.optimization_barrier((h, *shards[1:]))
-                wide_next = [lax.all_gather(w, 'model', axis=0, tiled=True) for w in late]
+                wide_next = [lax.all_gather(late[0], 'model', axis=0, tiled=True)]
                 resid, h, wqkv, wo = project(h, wd, resid, scales[3:4], scales[4:5], n_model, 3, wide=wide, attn=attn_shards)
             else:
                 out, = project(h, wd, resid, scales[7:8], scales[7:8], n_model, 6, wide=wide_next, final=True)
-        out = out.reshape(tok_m, n_model, width_loc).transpose(1, 0, 2).reshape(n_tok, width_loc)
+        out = out.reshape(n_tok, width_loc)
         return out, jnp.stack(keys), jnp.stack(values)
 
     return jax.shard_map(body, mesh=mesh,

time: 530 us -> 533 us (level)
    pallas_call x4, Pallas kernels: 320 us -> 340 us  [project(): pl.pallas_call(functools.partial(project_kernel, n_model, wide is not Non...]
    pallas_call x2, Pallas kernels: 85.9 us -> 68.8 us  [exchange(): pl.pallas_call(functools.partial(exchange_kernel, n_model), out_shape=(fu...]
  transfers between devices with their start and end apart: 4 -> 4, of which waited for: 1 -> 1; matrix products, arithmetic and copies ran while one was open for 7% -> 9% of each run, Pallas kernels for 61% -> 60%
where the time goes in v6:
time: 533 us; the launch traced here: 529 us
  Pallas kernels  452 us (85%)
  matrix products  26.2 us (5%)
  other arithmetic  15.4 us (3%)
  between operations  14.3 us (3%)
  local copies, waits for them, and re-layouts  11.7 us (2%)
  waiting for transfers between devices  9.55 us (2%)
    pallas_call x4, Pallas kernels, project(): pl.pallas_call(functools.partial(project_kernel, n_model, wide is not Non...  340 us
    pallas_call x2, Pallas kernels, exchange(): pl.pallas_call(functools.partial(exchange_kernel, n_model), out_shape=(fu...  68.8 us
    pallas_call x1, Pallas kernels, start(): pl.pallas_call(functools.partial(start_kernel, n_model), out_shape=(jax.S...  43.5 us
    dot_general x2, matrix products, body(): jnp.dot(h, wqkv, preferred_element_type=jnp.float32).astype(jnp.bfloat16)  11.8 us
  transfers between devices with their start and end apart: 4, of which 1 were waited for; matrix products, arithmetic and copies ran while one was open for 9% of the time, Pallas kernels for 60%

profile of v6, /device:TPU:0, one launch (start us, length us, event | category | flops | bytes accessed | tf_op | source)
XLA Modules:
  0.0 529.1 jit_solution(6136245957529976042)
XLA Ops:
  7.2 1.3 reshape.109.sc_ref
  8.5 1.6 dynamic-slice_bitcast_fusion.hid_ref
  10.2 43.5 %start.1 = (bf16[32,3072]{1,0:T(8,128)(2,1)}, bf16[512,3072]{1,0:T(8,128)(2,1)}, f32[8,3072]{1,0:T(8,128)}, bf16[3072,768]{1,0:T(8,128)(2,1)}, bf16[2048,384]{1,...) custom-call(bf16[8,32,384]{2,1,0:T(8,128)(2,1)} %dynamic-slice_bitcast_fusion.hid_r, ...), custom_call_target="tpu_custom_call" | custom-call | flops 100000000 | bytes 10000000 | tf_op jit(solution)/shard_map/start/pallas_call | solution.py:325
  53.7 2.4 slice.92
  56.2 5.9 %convolution_convert_fusion.1 = bf16[512,768]{1,0:T(8,128)(2,1)S(1)} fusion(bf16[512,3072]{1,0:T(8,128)(2,1)} %get-tuple-element.30, bf16[3072,768]{1,0:T(8,128)(2,1)} %get-tuple-element.31), kind=kOutput, calls=%fused_computation.19 | convolution fusion | flops 2416312320 | bytes 8650752 | tf_op jit(solution)/shard_map/dot_general | solution.py:629
  63.5 1.8 fusion.34
  66.0 43.1 %exchange_kv.2 = (bf16[4096,256]{1,0:T(8,128)(2,1)}, bf16[4096,256]{1,0:T(8,128)(2,1)}) custom-call(bf16[512,256]{1,0:T(8,128)(2,1)} %pad_maximum_fusion.2.k_ref, bf16[512,256]{1,0:T(8,128)(2,1)} %slice.111.v_ref), custom_call_target="tpu_custom_call" | custom-call | flops 100000000 | bytes 10000000 | tf_op jit(solution)/shard_map/exchange_kv/pallas_call | solution.py:249
  109.1 4.7 fusion.60
  113.8 1.3 fusion.3
  115.8 2.5 fusion.8.a_ref
  118.3 76.1 %project_reduce.4 = (bf16[32,3072]{1,0:T(8,128)(2,1)}, bf16[512,3072]{1,0:T(8,128)(2,1)}, bf16[12288,384]{1,0:T(8,128)(2,1)}) custom-call(bf16[512,256]{1,0:T(8,128)(2,1)} %fusion.8.a_ref, bf16[8,256,384]{2,1,0:T(8,128)(2,1)} %bitcast.35, bf16[32,3072]{1,0:T(8,128)(2,1)} %get-tuple-element.35.res_ref, f32[1,3072]{1,0:T(1,128)} %get-tuple-element.81.sa_ref, ...), custom_call_target="tpu_custom_call" | custom-call | flops 100000000 | bytes 10000000 | tf_op jit(solution)/shard_map/project_reduce/pallas_call | solution.py:594
  194.4 9.5 %all-gather.12.cloned.1.call-done = bf16[1,3072,1536]{2,1,0:T(8,128)(2,1)} async-done(((bf16[1,384,1536]{2,1,0:T(8,128)(2,1)}), bf16[1,3072,1536]{2,1,0:T(8,128)(2,1)}) %all-gather.12.cloned.1.call-update) | async-done | bytes 9437200 | tf_op jit(solution)/shard_map/all_gather | solution.py:618
  203.9 90.2 %project_reduce.5 = (bf16[32,3072]{1,0:T(8,128)(2,1)}, bf16[512,3072]{1,0:T(8,128)(2,1)}, bf16[3072,768]{1,0:T(8,128)(2,1)}, bf16[2048,384]{1,0:T(8,128)(2,1)}) custom-call(bf16[512,3072]{1,0:T(8,128)(2,1)} %get-tuple-element.40.a_ref, bf16[8,1536,384]{2,1,0:T(8,128)(2,1)} %bitcast.29, bf16[32,3072]{1,0:T(8,128)(2,1)} %get-tuple-element.42.res_ref, ...), custom_call_target="tpu_custom_call" | custom-call | flops 100000000 | bytes 10000000 | tf_op jit(solution)/shard_map/project_reduce/pallas_call | solution.py:594
  294.1 5.9 %convolution_convert_fusion = bf16[512,768]{1,0:T(8,128)(2,1)S(1)} fusion(bf16[512,3072]{1,0:T(8,128)(2,1)} %get-tuple-element.44, bf16[3072,768]{1,0:T(8,128)(2,1)} %get-tuple-element.45), kind=kOutput, calls=%fused_computation.18 | convolution fusion | flops 2416312320 | bytes 8650752 | tf_op jit(solution)/shard_map/dot_general | solution.py:629
  301.2 1.5 fusion.42
  303.4 25.7 %exchange_kv.3 = (bf16[4096,256]{1,0:T(8,128)(2,1)}, bf16[4096,256]{1,0:T(8,128)(2,1)}) custom-call(bf16[512,256]{1,0:T(8,128)(2,1)} %pad_maximum_fusion.3.k_ref, bf16[512,256]{1,0:T(8,128)(2,1)} %slice.118.v_ref), custom_call_target="tpu_custom_call" | custom-call | flops 100000000 | bytes 10000000 | tf_op jit(solution)/shard_map/exchange_kv/pallas_call | solution.py:249
  329.2 4.7 fusion.61
  333.9 1.3 fusion.4
  335.5 2.5 fusion.7.a_ref
  338.0 84.6 %project_reduce.6 = (bf16[32,3072]{1,0:T(8,128)(2,1)}, bf16[512,3072]{1,0:T(8,128)(2,1)}, bf16[12288,384]{1,0:T(8,128)(2,1)}) custom-call(bf16[512,256]{1,0:T(8,128)(2,1)} %fusion.7.a_ref, bf16[8,256,384]{2,1,0:T(8,128)(2,1)} %bitcast.36, bf16[32,3072]{1,0:T(8,128)(2,1)} %get-tuple-element.51.res_ref, f32[1,3072]{1,0:T(1,128)} %get-tuple-element.77.sa_ref, ...), custom_call_target="tpu_custom_call" | custom-call | flops 100000000 | bytes 10000000 | tf_op jit(solution)/shard_map/project_reduce/pallas_call | solution.py:594
  422.6 4.8 pad_maximum_fusion
  427.4 2.4 pad_maximum_fusion.1
  429.7 88.6 %project_reduce.7 = bf16[8,512,384]{2,1,0:T(8,128)(2,1)} custom-call(bf16[512,3072]{1,0:T(8,128)(2,1)} %get-tuple-element.52.a_ref, bf16[8,1536,384]{2,1,0:T(8,128)(2,1)} %bitcast.30, bf16[32,3072]{1,0:T(8,128)(2,1)} %get-tuple-element.54.res_ref, f32[1,3072]{1,0:T(1,128)} %get-tuple-element.75.sa_ref.sb_ref, f32[1,3072]{1,0:T(1,128)} %get-tuple-element.75.sa_ref.sb_ref, ...), custom_call_target="tpu_custom_call" | custom-call | flops 100000000 | bytes 10000000 | tf_op jit(solution)/shard_map/project_reduce/pallas_call | solution.py:594
  518.4 3.9 copy.18
  (45 shorter events, 5.3 us)
Async XLA Ops:
  7.2 187.3 %all-gather.6.cloned.1.call-start = ((), (), s32[]{:S(2)}) async-start(), calls=%async_computation | async-start | bytes 10616832 | tf_op jit(solution)/shard_map/all_gather | solution.py:620
  53.7 150.2 %all-gather.12.cloned.1.call-start = ((), (), s32[]{:S(2)}) async-start(), calls=%async_computation.3 | async-start | bytes 10616832 | tf_op jit(solution)/shard_map/all_gather | solution.py:618
  56.1 373.6 %all-gather.8.cloned.1.call-start = ((), (), s32[]{:S(2)}) async-start(), calls=%async_computation.1 | async-start | bytes 10616832 | tf_op jit(solution)/shard_map/all_gather | solution.py:647
  56.2 6.7 %copy-start.7 = (s32[4096]{0:T(1024)S(1)}, s32[4096]{0:T(1024)}, u32[]{:S(2)}) copy-start(s32[4096]{0:T(1024)} %param.13) | copy-start | bytes 49156
  56.2 6.7 %copy-start.6 = (s32[4096]{0:T(1024)S(1)}, s32[4096]{0:T(1024)}, u32[]{:S(2)}) copy-start(s32[4096]{0:T(1024)} %param.14) | copy-start | bytes 49156
  56.2 7.0 %copy-start.5 = (f32[2,2,256]{2,1,0:T(2,128)S(1)}, f32[2,2,256]{2,1,0:T(2,128)}, u32[]{:S(2)}) copy-start(f32[2,2,256]{2,1,0:T(2,128)} %param.23) | copy-start | bytes 12292
  113.8 1.3 copy-start.4
  113.8 2.0 copy-start
  194.3 235.4 %all-gather.10.cloned.1.call-start = ((), (), s32[]{:S(2)}) async-start(), calls=%async_computation.2 | async-start | bytes 10616832 | tf_op jit(solution)/shard_map/all_gather | solution.py:637
  333.9 1.6 copy-start.2
  422.6 4.8 copy-start.1
  422.6 4.8 copy-start.3
Sparse Core Ops, SparseCore 0:
  53.8 70.1 all-gather.5
  126.2 77.6 all-gather.11
  205.6 69.1 all-gather.7
  329.3 85.2 all-gather.9

commit v7 on v5

--- a/solution.py
+++ b/solution.py
@@ -100,12 +100,15 @@
 
 
 def gather_blocks(torus, h_ref, send, recv, between=lambda: None):
-    rows = h_ref.shape[0] // (SIDE * SIDE)
-    cols = h_ref.shape[1] // 2
+    apart = len(h_ref.shape) == 3
+    rows = h_ref.shape[-2] // (SIDE * SIDE)
+    cols = h_ref.shape[0 if apart else 1] // 2
     half = rows // 2
 
     def view(q, da, db, part):
         start = torus.at(q, da, db) * rows + (half if part == 2 else 0)
+        if apart:
+            return h_ref.at[pl.ds(q * cols, cols), pl.ds(pl.multiple_of(start, half), rows if part == 0 else half), :]
         return h_ref.at[pl.ds(pl.multiple_of(start, half), rows if part == 0 else half), pl.ds(q * cols, cols)]
 
     def ring(q, axis, base, offsets):
@@ -178,8 +181,8 @@
                 group.append(remote(src if src is not None and slot < 3 else v, v, send.at[a, slot], recv.at[a, slot], {'model': to}))
             self.copies.append(group)
 
-    def begin(self):
-        for c in self.copies:
+    def begin(self, lo=0, hi=None):
+        for c in self.copies[lo:hi]:
             c[0].start()
             c[1].start()
             c[2].start()
@@ -210,15 +213,30 @@
     return [pltpu.SemaphoreType.DMA((count, 9)), pltpu.SemaphoreType.DMA((count, 9))]
 
 
-def exchange_kernel(n_model, k_ref, v_ref, ka_ref, va_ref, send, recv):
+def qkv_kernel(n_model, h_ref, w_any, cos_ref, sin_ref, qk_ref, q_ref, ka_ref, va_ref, w_ref, ls, send, recv):
     line = Line(n_model)
-    rows = k_ref.shape[0]
+    rows, dim = q_ref.shape
+    parts = [pl.ds(at * dim, dim) for at in range(3)]
+    loads = [pltpu.make_async_copy(w_any.at[:, p], w_ref.at[:, p], ls.at[k]) for k, p in enumerate(parts)]
+    for k in (1, 2, 0):
+        loads[k].start()
     meet(None, (line.right, line.left, line.mate))
     here = pl.ds(pl.multiple_of(line.me * rows, rows), rows)
-    ka_ref[here, :] = k_ref[...]
-    va_ref[here, :] = v_ref[...]
-    ex = Exchange(line, [(ka_ref, rows, 0, rows, None), (va_ref, rows, 0, rows, None)], send, recv)
-    ex.begin()
+    piece = rows // 2
+    ex = Exchange(line, [(ref, rows, at, piece, None) for ref in (ka_ref, va_ref) for at in (0, piece)], send, recv)
+
+    def made(k):
+        loads[k].wait()
+        return jnp.dot(h_ref[...], w_ref[:, k * dim:(k + 1) * dim], preferred_element_type=jnp.float32).astype(jnp.bfloat16)
+
+    def turned(values, row):
+        return apply_rope(norm(values.astype(jnp.float32), qk_ref[row:row + 1]), cos_ref[...], sin_ref[...]).astype(jnp.bfloat16)
+
+    ka_ref[here, :] = turned(made(1), 1)
+    ex.begin(0, 2)
+    va_ref[here, :] = made(2)
+    ex.begin(2)
+    q_ref[...] = turned(made(0), 0)
     ex.onward()
     ex.finish()
 
@@ -226,7 +244,7 @@
 VMEM = pl.BlockSpec(memory_space=pltpu.VMEM)
 ANY = pl.BlockSpec(memory_space=pl.ANY)
 PIECES = 4
-WIDE = 3
+WIDE = 4
 NEED = ((2, 2), (2, 1), (2, -1), (2, 0), (1, 2), (-1, 2), (0, 2), (1, 1),
         (1, -1), (1, 0), (-1, 1), (-1, -1), (-1, 0), (0, 1), (0, -1), (0, 0))
 
@@ -239,14 +257,15 @@
     return pl.CostEstimate(flops=flops, bytes_accessed=10_000_000, transcendentals=0)
 
 
-def exchange(k, v, n_model, cid):
-    rows, dim = k.shape
-    full = jax.ShapeDtypeStruct((rows * n_model, dim), k.dtype)
+def make_qkv(h, w, cos_tab, sin_tab, qk_rows, n_model, cid):
+    rows, dim = h.shape[0], qk_rows.shape[1]
+    full = jax.ShapeDtypeStruct((rows * n_model, dim), h.dtype)
     return pl.pallas_call(
-        functools.partial(exchange_kernel, n_model),
-        out_shape=(full, full), in_specs=[VMEM] * 2, out_specs=(VMEM, VMEM),
-        scratch_shapes=exchange_sems(2), compiler_params=params(cid), cost_estimate=cost(100_000_000), name='exchange_kv',
-    )(k, v)
+        functools.partial(qkv_kernel, n_model),
+        out_shape=(jax.ShapeDtypeStruct((rows, dim), h.dtype), full, full), in_specs=[VMEM, ANY, VMEM, VMEM, VMEM], out_specs=(VMEM,) * 3,
+        scratch_shapes=[pltpu.VMEM(w.shape, w.dtype), pltpu.SemaphoreType.DMA((3,))] + exchange_sems(4),
+        compiler_params=params(cid), cost_estimate=cost(100_000_000), name='make_qkv',
+    )(h, w, cos_tab, sin_tab, qk_rows)
 
 
 def load_attn_weights(line, layer, wq_ref, wk_ref, wv_ref, wo_ref, wqkv_ref, woa_ref):
@@ -274,13 +293,19 @@
 
 
 def start_kernel(n_model, hid_ref, sc_ref, wq_ref, wk_ref, wv_ref, wo_ref, wg_ref, wu_ref,
-                 x_ref, h_ref, sca_ref, wqkv_ref, woa_ref, u0_ref, g1_ref, u1_ref,
+                 x_ref, h_ref, sca_ref, wqkv_ref, woa_ref, u0a_ref, u0b_ref, g1_ref, u1a_ref, u1b_ref,
                  xin, scin, stage, xs, xr, ss, sr, ls, hs, hr, es, er):
     torus, line = Torus(), Line(n_model)
     rows = x_ref.shape[0]
-    shards = ((wu_ref, 0, u0_ref), (wg_ref, 1, g1_ref), (wu_ref, 1, u1_ref))
+    part = wg_ref.shape[2] // 2
+    shards = ((wu_ref, 0, (u0a_ref, u0b_ref)), (wg_ref, 1, (g1_ref,)), (wu_ref, 1, (u1a_ref, u1b_ref)))
     loads = [pltpu.make_async_copy(ref.at[layer], stage.at[k], ls.at[k]) for k, (ref, layer, _) in enumerate(shards)]
-    stores = [pltpu.make_async_copy(stage.at[k], dst, ls.at[k]) for k, (_, _, dst) in enumerate(shards)]
+    stores = []
+    for k, (_, _, dsts) in enumerate(shards):
+        if len(dsts) == 1:
+            stores.append([pltpu.make_async_copy(stage.at[k], dsts[0], ls.at[k])])
+        else:
+            stores.append([pltpu.make_async_copy(stage.at[k, :, pl.ds(i * part, part)], dst, ls.at[k + 3 * i]) for i, dst in enumerate(dsts)])
     for c in loads:
         c.start()
     meet(torus, others(line))
@@ -292,7 +317,8 @@
     ex.begin()
     for load, store in zip(loads, stores):
         load.wait()
-        store.start()
+        for c in store:
+            c.start()
     for c in xc + sc:
         c.wait_recv()
     sca_ref[...] = jnp.concatenate([scin[m] for m in range(n_model)], axis=1)
@@ -302,7 +328,7 @@
     h_ref[pl.ds(pl.multiple_of(mine * rows, rows), rows), :] = norm(x.astype(jnp.float32), sca_ref[0:1]).astype(jnp.bfloat16)
     gather_blocks(torus, h_ref, hs, hr, ex.onward)
     ex.finish()
-    for c in stores:
+    for c in sum(stores, []):
         c.wait()
     for c in xc + sc:
         c.wait_send()
@@ -323,11 +349,11 @@
         out_shape=(jax.ShapeDtypeStruct((rows, width), hidden_mine.dtype),
                    jax.ShapeDtypeStruct((rows * SIDE * SIDE, width), hidden_mine.dtype),
                    jax.ShapeDtypeStruct((scales.shape[0], width), scales.dtype)) + attn_weight_shapes(wq, wo, n_model)
-        + (jax.ShapeDtypeStruct(wg.shape[1:], wg.dtype),) * 3,
-        in_specs=[VMEM] * 6 + [ANY] * 2, out_specs=(VMEM,) * 5 + (ANY,) * 3,
+        + tuple(jax.ShapeDtypeStruct((wg.shape[1], wg.shape[2] // cut), wg.dtype) for cut in (2, 2, 1, 2, 2)),
+        in_specs=[VMEM] * 6 + [ANY] * 2, out_specs=(VMEM,) * 5 + (ANY,) * 5,
         scratch_shapes=[pltpu.VMEM(hidden_mine.shape, hidden_mine.dtype), pltpu.VMEM((n_model,) + scales.shape, scales.dtype),
                         pltpu.VMEM((3,) + wg.shape[1:], wg.dtype)]
-        + peer_sems + [pltpu.SemaphoreType.DMA((3,))] + GATHER_SEMS + exchange_sems(2),
+        + peer_sems + [pltpu.SemaphoreType.DMA((6,))] + GATHER_SEMS + exchange_sems(2),
         compiler_params=params(cid), cost_estimate=cost(100_000_000), name='start',
     )(hidden_mine, scales, wq, wk, wv, wo, wg, wu)
 
@@ -335,8 +361,8 @@
 def project_kernel(n_model, ffn, final, attn, down, a_ref, w_ref, res_ref, sa_ref, sb_ref, *rest):
     rest = list(rest)
     if ffn:
-        wg_any, wu_any = rest[:2]
-        rest = rest[2:]
+        wg_any, wu_lo, wu_hi = rest[:3]
+        rest = rest[3:]
     fetch = attn or down is not None
     if attn:
         wq_ref, wk_ref, wv_ref, wo_ref = rest[:4]
@@ -364,13 +390,14 @@
         span = wg_any.shape[1] // WIDE
 
         def wide_load(k, n):
-            src, dst = ((wg_any, wg_ref), (wu_any, wu_ref))[k]
             at = pl.ds(pl.multiple_of(n * span, span), span)
-            return pltpu.make_async_copy(src.at[:, at], dst.at[:, at], fs.at[k, n])
+            dst = (wg_ref, wu_ref)[k]
+            return pltpu.make_async_copy(wg_any.at[:, at], dst.at[:, at], fs.at[k, n])
 
         for n in range(WIDE):
             wide_load(0, n).start()
-            wide_load(1, n).start()
+            part = wu_lo if n < WIDE // 2 else wu_hi
+            pltpu.make_async_copy(part.at[:, pl.ds(n % (WIDE // 2) * span, span)], wu_ref.at[:, pl.ds(n * span, span)], fs.at[1, n]).start()
         down_load = pltpu.make_async_copy(w_ref, wd_ref2, fs.at[2, 0])
         down_load.start()
         w_ref = wd_ref2
@@ -503,7 +530,8 @@
         copies = to_all(line, lambda step, peer: remote(outgo.at[peer], income.at[line.me], cs.at[step], cr.at[step], {'model': peer}))
         for c in copies:
             c.wait_recv()
-        h_ref[here, :] = jnp.concatenate([income[m] for m in range(n_model)], axis=1)
+        for m in range(n_model):
+            h_ref[m, here, :] = income[m]
     else:
         x_ref[...] = x_new
         h_ref[here, :] = norm(x_new.astype(jnp.float32), sb_ref[...]).astype(jnp.bfloat16)
@@ -536,14 +564,15 @@
 
     scratch = [f32(SIDE, rows)] * 4 + [f32(SIDE, half)] * 2 + [f32(SIDE, rows)] * 2 + [f32(half)] * 2 + [f32(rows)] * 2
     scratch += [pltpu.SemaphoreType.DMA((2, SIDE, 4))] * 2 + [pltpu.SemaphoreType.DMA((2, 4))] * 2 + GATHER_SEMS
-    h_shape = jax.ShapeDtypeStruct((rows * SIDE * SIDE, width), jnp.bfloat16)
+    h_dims = (n_model, rows * SIDE * SIDE, width // n_model) if final else (rows * SIDE * SIDE, width)
+    h_shape = jax.ShapeDtypeStruct(h_dims, jnp.bfloat16)
     out_shape = (h_shape,) if final else (jax.ShapeDtypeStruct((rows, width), jnp.bfloat16), h_shape)
     args = (a, w, resid, scale_a, scale_b)
     in_specs, out_specs = [VMEM] * 5, (VMEM,) * len(out_shape)
     if wide is not None:
         args += tuple(wide)
         in_specs[1] = ANY
-        in_specs += [ANY] * 2
+        in_specs += [ANY] * 3
         gate = wide[0]
         scratch += [pltpu.VMEM(a.shape, a.dtype), pltpu.VMEM((a.shape[0], gate.shape[1]), a.dtype), pltpu.VMEM(gate.shape, gate.dtype),
                     pltpu.VMEM(gate.shape, gate.dtype), pltpu.VMEM(w.shape, w.dtype), pltpu.SemaphoreType.DMA((3, WIDE))]
@@ -589,7 +618,7 @@
         mine = lax.dynamic_index_in_dim(hidden_in.reshape(n_model, n_heads, tok_own, width_loc), hd, 1, keepdims=False)
         gate_0 = lax.all_gather(w_gate[0], 'model', axis=0, tiled=True)
         resid, h, scales, wqkv, wo, *shards = start(mine, norm_scales.reshape(-1, width_loc), *attn_shards, w_gate, w_up, 0)
-        wide = [gate_0, lax.all_gather(shards[0], 'model', axis=0, tiled=True)]
+        wide = [gate_0] + [lax.all_gather(w, 'model', axis=0, tiled=True) for w in shards[:2]]
 
         pos_m = lax.dynamic_slice_in_dim(positions, md * tok_m, tok_m)
         seg_m = lax.dynamic_slice_in_dim(seg_ids, md * tok_m, tok_m)
@@ -598,12 +627,11 @@
         keys, values = [], []
         for l in range(2):
             rope_base, pos_factor, window = settings[l]
-            qkv = jnp.dot(h, wqkv, preferred_element_type=jnp.float32).astype(jnp.bfloat16)
-            q, k, v = qkv[:, :head_dim], qkv[:, head_dim:2 * head_dim], qkv[:, 2 * head_dim:]
             cos_tab, sin_tab = rope_tables(pos_m, head_dim, rope_base, pos_factor)
-            q = apply_rope(norm(q.astype(jnp.float32), qk_scales[l, 0]), cos_tab, sin_tab).astype(jnp.bfloat16)
-            k = apply_rope(norm(k.astype(jnp.float32), qk_scales[l, 1]), cos_tab, sin_tab).astype(jnp.bfloat16)
-            k_all, v_all = exchange(k, v, n_model, 1 + 3 * l)
+            q, k_all, v_all = make_qkv(h, wqkv, cos_tab, sin_tab, qk_scales[l], n_model, 1 + 3 * l)
+            if l == 1:
+                k_all, up_last = lax.optimization_barrier((k_all, late[2]))
+                wide_next.append(lax.all_gather(up_last, 'model', axis=0, tiled=True))
             keys.append(k_all[:, None, :])
             values.append(v_all[:, None, :])
             o = attend(q, k_all, v_all, seg_m, pos_m, seg_ids, positions, window)
@@ -612,12 +640,12 @@
             resid, h, wd = project(o, wo, resid, scales[row + 1:row + 2], scales[row + 2:row + 3], n_model, 2 + 3 * l, down=w_down, layer=l)
             wd = wd.reshape(n_model, w_down.shape[1], width_loc)
             if l == 0:
-                h, *late = lax.optimization_barrier((h, *shards[1:]))
-                wide_next = [lax.all_gather(w, 'model', axis=0, tiled=True) for w in late]
+                h, *late = lax.optimization_barrier((h, *shards[2:]))
+                wide_next = [lax.all_gather(w, 'model', axis=0, tiled=True) for w in late[:2]]
                 resid, h, wqkv, wo = project(h, wd, resid, scales[3:4], scales[4:5], n_model, 3, wide=wide, attn=attn_shards)
             else:
                 out, = project(h, wd, resid, scales[7:8], scales[7:8], n_model, 6, wide=wide_next, final=True)
-        out = out.reshape(tok_m, n_model, width_loc).transpose(1, 0, 2).reshape(n_tok, width_loc)
+        out = out.reshape(n_tok, width_loc)
         return out, jnp.stack(keys), jnp.stack(values)
 
     return jax.shard_map(body, mesh=mesh,

time: 530 us -> 541 us (1.021)
  waiting for transfers between devices: 8.58 us -> 24.5 us
  matrix products: 26.3 us -> 15.1 us
  Pallas kernels: 449 us -> 456 us
    all_gather x1, waiting for transfers between devices: 7.95 us -> 23.2 us  [body(): gate_0 = lax.all_gather(w_gate[0], 'model', axis=0, tiled=True)]
    pallas_call x4, Pallas kernels: 320 us -> 333 us  [project(): pl.pallas_call(functools.partial(project_kernel, n_model, wide is not Non...]
    dot_general x2 -> x0, matrix products: 11.8 us -> none  [body(): jnp.dot(h, wqkv, preferred_element_type=jnp.float32).astype(jnp.bfloat16)]
    pallas_call x2, Pallas kernels: 85.9 us -> 79.3 us  [make_qkv(): pl.pallas_call(functools.partial(qkv_kernel, n_model), out_shape=(jax.Sha...]
  transfers between devices with their start and end apart: 4 -> 6, of which waited for: 1 -> 1; matrix products, arithmetic and copies ran while one was open for 7% -> 6% of each run, Pallas kernels for 61% -> 61%
where the time goes in v7:
time: 541 us; the launch traced here: 533 us
  Pallas kernels  456 us (84%)
  waiting for transfers between devices  24.5 us (5%)
  matrix products  15.1 us (3%)
  between operations  14.4 us (3%)
  other arithmetic  12.2 us (2%)
  local copies, waits for them, and re-layouts  10.8 us (2%)
    pallas_call x4, Pallas kernels, project(): pl.pallas_call(functools.partial(project_kernel, n_model, wide is not Non...  333 us
    pallas_call x2, Pallas kernels, make_qkv(): pl.pallas_call(functools.partial(qkv_kernel, n_model), out_shape=(jax.Sha...  79.3 us
    pallas_call x1, Pallas kernels, start(): pl.pallas_call(functools.partial(start_kernel, n_model), out_shape=(jax.S...  43.6 us
    all_gather x1, waiting for transfers between devices, body(): gate_0 = lax.all_gather(w_gate[0], 'model', axis=0, tiled=True)  23.2 us
  transfers between devices with their start and end apart: 6, of which 1 were waited for; matrix products, arithmetic and copies ran while one was open for 6% of the time, Pallas kernels for 61%

profile of v7, /device:TPU:0, one launch (start us, length us, event | category | flops | bytes accessed | tf_op | source)
XLA Modules:
  0.0 533.5 jit_solution(16611357625384068703)
XLA Ops:
  7.2 1.3 reshape.49.sc_ref
  8.5 1.6 dynamic-slice_bitcast_fusion.hid_ref
  10.2 43.6 %start.1 = (bf16[32,3072]{1,0:T(8,128)(2,1)}, bf16[512,3072]{1,0:T(8,128)(2,1)}, f32[8,3072]{1,0:T(8,128)}, bf16[3072,768]{1,0:T(8,128)(2,1)}, bf16[2048,384]{1,...) custom-call(bf16[8,32,384]{2,1,0:T(8,128)(2,1)} %dynamic-slice_bitca, ...), custom_call_target="tpu_custom_call" | custom-call | flops 100000000 | bytes 10000000 | tf_op jit(solution)/shard_map/start/pallas_call | solution.py:347
  53.8 0.7 all-gather.8.cloned.1.call-update
  54.6 2.4 slice.36
  57.2 0.6 slice_bitcast_fusion
  57.8 1.8 multiply_sine_fusion.1
  59.6 44.8 %make_qkv.2 = (bf16[512,256]{1,0:T(8,128)(2,1)}, bf16[4096,256]{1,0:T(8,128)(2,1)}, bf16[4096,256]{1,0:T(8,128)(2,1)}) custom-call(bf16[512,3072]{1,0:T(8,128)(2,1)} %get-tuple-element.35.h_ref, bf16[3072,768]{1,0:T(8,128)(2,1)} %get-tuple-element.36.w_any, f32[512,128]{1,0:T(8,128)} %get-tuple-element.81.cos_ref, f32[512,128]{1,0:T(8,128)} %get-tuple-element.80.sin_ref, ...), custom_call_target="tpu_custom_call" | custom-call | flops 100000000 | bytes 10000000 | tf_op jit(solution)/shard_map/make_qkv/pallas_call | solution.py:263
  104.4 4.8 fusion.12
  109.2 1.3 fusion.3
  110.5 0.7 fusion.11
  111.2 2.6 fusion.8.a_ref
  113.8 77.3 %project_reduce.4 = (bf16[32,3072]{1,0:T(8,128)(2,1)}, bf16[512,3072]{1,0:T(8,128)(2,1)}, bf16[12288,384]{1,0:T(8,128)(2,1)}) custom-call(bf16[512,256]{1,0:T(8,128)(2,1)} %fusion.8.a_ref, bf16[8,256,384]{2,1,0:T(8,128)(2,1)} %bitcast.33, bf16[32,3072]{1,0:T(8,128)(2,1)} %get-tuple-element.41.res_ref, f32[1,3072]{1,0:T(1,128)} %get-tuple-element.75.sa_ref, ...), custom_call_target="tpu_custom_call" | custom-call | flops 100000000 | bytes 10000000 | tf_op jit(solution)/shard_map/project_reduce/pallas_call | solution.py:595
  191.8 1.8 multiply_sine_fusion
  193.6 23.2 %all-gather.18.cloned.1.call-done = bf16[1,3072,1536]{2,1,0:T(8,128)(2,1)} async-done(((bf16[1,384,1536]{2,1,0:T(8,128)(2,1)}), bf16[1,3072,1536]{2,1,0:T(8,128)(2,1)}) %all-gather.18.cloned.1.call-update) | async-done | bytes 9437200 | tf_op jit(solution)/shard_map/all_gather | solution.py:619
  216.8 97.2 %project_reduce.5 = (bf16[32,3072]{1,0:T(8,128)(2,1)}, bf16[512,3072]{1,0:T(8,128)(2,1)}, bf16[3072,768]{1,0:T(8,128)(2,1)}, bf16[2048,384]{1,0:T(8,128)(2,1)}) custom-call(bf16[512,3072]{1,0:T(8,128)(2,1)} %get-tuple-element.47.a_ref, bf16[8,1536,384]{2,1,0:T(8,128)(2,1)} %bitcast.27, bf16[32,3072]{1,0:T(8,128)(2,1)} %get-tuple-element.49.res_ref, ...), custom_call_target="tpu_custom_call" | custom-call | flops 100000000 | bytes 10000000 | tf_op jit(solution)/shard_map/project_reduce/pallas_call | solution.py:595
  314.0 34.5 %make_qkv.3 = (bf16[512,256]{1,0:T(8,128)(2,1)}, bf16[4096,256]{1,0:T(8,128)(2,1)}, bf16[4096,256]{1,0:T(8,128)(2,1)}) custom-call(bf16[512,3072]{1,0:T(8,128)(2,1)} %get-tuple-element.52.h_ref, bf16[3072,768]{1,0:T(8,128)(2,1)} %get-tuple-element.53.w_any, f32[512,128]{1,0:T(8,128)} %get-tuple-element.79.cos_ref, f32[512,128]{1,0:T(8,128)} %get-tuple-element.78.sin_ref, ...), custom_call_target="tpu_custom_call" | custom-call | flops 100000000 | bytes 10000000 | tf_op jit(solution)/shard_map/make_qkv/pallas_call | solution.py:263
  348.5 5.2 fusion.13
  353.7 1.3 fusion.4
  355.3 2.5 fusion.7.a_ref
  357.8 71.9 %project_reduce.6 = (bf16[32,3072]{1,0:T(8,128)(2,1)}, bf16[512,3072]{1,0:T(8,128)(2,1)}, bf16[12288,384]{1,0:T(8,128)(2,1)}) custom-call(bf16[512,256]{1,0:T(8,128)(2,1)} %fusion.7.a_ref, bf16[8,256,384]{2,1,0:T(8,128)(2,1)} %bitcast.34, bf16[32,3072]{1,0:T(8,128)(2,1)} %get-tuple-element.60.res_ref, f32[1,3072]{1,0:T(1,128)} %get-tuple-element.71.sa_ref, ...), custom_call_target="tpu_custom_call" | custom-call | flops 100000000 | bytes 10000000 | tf_op jit(solution)/shard_map/project_reduce/pallas_call | solution.py:595
  429.8 5.9 %pad_maximum_fusion = (bf16[2,4096,1,256]{3,1,2,0:T(8,128)(2,1)}, bf16[2,4096,1,256]{3,1,2,0:T(8,128)(2,1)}) fusion(bf16[1,4096,1,256]{3,1,2,0:T(8,128)(2,1)} %bitcast.31, bf16[1,4096,1,256]{3,1,2,0:T(8,128)(2,1)} %bitcast.29, bf16[1,4096,1,256]{3,1,2,0:T(8,128)(2,1)} %bitcast.32, bf16[1,4096,1,256]{3,1,2,0:T(8,128)(2,1)} %bitcast.30), kind=kLoop, calls=%fused_computation.14 | loop fusion | flops 4194304 | bytes 16777216 | tf_op jit(solution)/shard_map/stack | solution.py:649
  435.7 86.9 %project_reduce.7 = bf16[8,512,384]{2,1,0:T(8,128)(2,1)} custom-call(bf16[512,3072]{1,0:T(8,128)(2,1)} %get-tuple-element.61.a_ref, bf16[8,1536,384]{2,1,0:T(8,128)(2,1)} %bitcast.28, bf16[32,3072]{1,0:T(8,128)(2,1)} %get-tuple-element.63.res_ref, f32[1,3072]{1,0:T(1,128)} %get-tuple-element.69.sa_ref.sb_ref, f32[1,3072]{1,0:T(1,128)} %get-tuple-element.69.sa_ref.sb_ref, ...), custom_call_target="tpu_custom_call" | custom-call | flops 100000000 | bytes 10000000 | tf_op jit(solution)/shard_map/project_reduce/pallas_call | solution.py:595
  522.6 3.9 copy.18
  (33 shorter events, 1.4 us)
Async XLA Ops:
  7.2 186.4 %all-gather.10.cloned.1.call-start = ((), (), s32[]{:S(2)}) async-start(), calls=%async_computation.1 | async-start | bytes 5308416 | tf_op jit(solution)/shard_map/all_gather | solution.py:621
  10.2 46.8 %copy-start.5 = (s32[4096]{0:T(1024)S(1)}, s32[4096]{0:T(1024)}, u32[]{:S(2)}) copy-start(s32[4096]{0:T(1024)} %param.13) | copy-start | bytes 49156
  10.2 46.9 %copy-start.4 = (s32[4096]{0:T(1024)S(1)}, s32[4096]{0:T(1024)}, u32[]{:S(2)}) copy-start(s32[4096]{0:T(1024)} %param.14) | copy-start | bytes 49156
  10.2 47.0 %copy-start.3 = (f32[2,2,256]{2,1,0:T(2,128)S(1)}, f32[2,2,256]{2,1,0:T(2,128)}, u32[]{:S(2)}) copy-start(f32[2,2,256]{2,1,0:T(2,128)} %param.23) | copy-start | bytes 12292
  53.8 139.9 %all-gather.8.cloned.1.call-start = ((), (), s32[]{:S(2)}) async-start(), calls=%async_computation | async-start | bytes 5308416 | tf_op jit(solution)/shard_map/all_gather | solution.py:621
  54.5 162.3 %all-gather.18.cloned.1.call-start = ((), (), s32[]{:S(2)}) async-start(), calls=%async_computation.5 | async-start | bytes 10616832 | tf_op jit(solution)/shard_map/all_gather | solution.py:619
  56.9 378.7 %all-gather.14.cloned.1.call-start = ((), (), s32[]{:S(2)}) async-start(), calls=%async_computation.3 | async-start | bytes 5308416 | tf_op jit(solution)/shard_map/all_gather | solution.py:644
  109.2 1.3 copy-start.2
  109.2 2.0 copy-start
  191.1 244.5 %all-gather.12.cloned.1.call-start = ((), (), s32[]{:S(2)}) async-start(), calls=%async_computation.2 | async-start | bytes 10616832 | tf_op jit(solution)/shard_map/all_gather | solution.py:644
  191.7 244.0 %all-gather.16.cloned.1.call-start = ((), (), s32[]{:S(2)}) async-start(), calls=%async_computation.4 | async-start | bytes 5308416 | tf_op jit(solution)/shard_map/all_gather | solution.py:634
  353.7 1.6 copy-start.1
Sparse Core Ops, SparseCore 0:
  53.9 50.3 all-gather.9
  105.9 48.5 all-gather.7
  156.8 59.9 all-gather.17
  218.3 45.2 all-gather.13
  265.2 70.2 all-gather.11
  348.7 50.5 all-gather.15

commit v8 on v7

--- a/solution.py
+++ b/solution.py
@@ -244,7 +244,7 @@
 VMEM = pl.BlockSpec(memory_space=pltpu.VMEM)
 ANY = pl.BlockSpec(memory_space=pl.ANY)
 PIECES = 4
-WIDE = 4
+WIDE = 2
 NEED = ((2, 2), (2, 1), (2, -1), (2, 0), (1, 2), (-1, 2), (0, 2), (1, 1),
         (1, -1), (1, 0), (-1, 1), (-1, -1), (-1, 0), (0, 1), (0, -1), (0, 0))
 
@@ -436,10 +436,11 @@
         lhs = jnp.concatenate([operand(q, off, o) for o in order], axis=0)
         piece = w_ref.shape[2]
         per = cols // piece
-        for p in range(per):
-            res = jnp.dot(lhs, w_ref[q * per + p], preferred_element_type=jnp.float32)
+        for p in range(0, per, 2):
+            pair = jnp.concatenate([w_ref[q * per + p], w_ref[q * per + p + 1]], axis=1)
+            res = jnp.dot(lhs, pair, preferred_element_type=jnp.float32)
             for n in range(SIDE):
-                dst[q, n, :, p * piece:(p + 1) * piece] = res[n * rows:(n + 1) * rows]
+                dst[q, n, :, p * piece:(p + 2) * piece] = res[n * rows:(n + 1) * rows]
 
     def ring1(q, n, k):
         src, dst, step = ((far.at[q, n, pl.ds(0, half)], from_l1.at[q, n], 1), (far.at[q, n, pl.ds(half, half)], from_r1.at[q, n], -1),

time: 541 us -> 541 us (level)
    pallas_call x4, Pallas kernels: 333 us -> 326 us  [project(): pl.pallas_call(functools.partial(project_kernel, n_model, wide is not Non...]
where the time goes in v8:
time: 541 us; the launch traced here: 531 us
  Pallas kernels  453 us (84%)
  waiting for transfers between devices  25 us (5%)
  matrix products  15 us (3%)
  between operations  14.4 us (3%)
  other arithmetic  12.2 us (2%)
  local copies, waits for them, and re-layouts  10.8 us (2%)
    pallas_call x4, Pallas kernels, project(): pl.pallas_call(functools.partial(project_kernel, n_model, wide is not Non...  326 us
    pallas_call x2, Pallas kernels, make_qkv(): pl.pallas_call(functools.partial(qkv_kernel, n_model), out_shape=(jax.Sha...  83.3 us
    pallas_call x1, Pallas kernels, start(): pl.pallas_call(functools.partial(start_kernel, n_model), out_shape=(jax.S...  43.6 us
    all_gather x1, waiting for transfers between devices, body(): gate_0 = lax.all_gather(w_gate[0], 'model', axis=0, tiled=True)  23.6 us
  transfers between devices with their start and end apart: 6, of which 1 were waited for; matrix products, arithmetic and copies ran while one was open for 6% of the time, Pallas kernels for 61%

profile of v8, /device:TPU:0, one launch (start us, length us, event | category | flops | bytes accessed | tf_op | source)
XLA Modules:
  0.0 531.0 jit_solution(12910453596352944476)
XLA Ops:
  7.2 1.3 reshape.49.sc_ref
  8.5 1.6 dynamic-slice_bitcast_fusion.hid_ref
  10.2 43.6 %start.1 = (bf16[32,3072]{1,0:T(8,128)(2,1)}, bf16[512,3072]{1,0:T(8,128)(2,1)}, f32[8,3072]{1,0:T(8,128)}, bf16[3072,768]{1,0:T(8,128)(2,1)}, bf16[2048,384]{1,...) custom-call(bf16[8,32,384]{2,1,0:T(8,128)(2,1)} %dynamic-slice_bitca, ...), custom_call_target="tpu_custom_call" | custom-call | flops 100000000 | bytes 10000000 | tf_op jit(solution)/shard_map/start/pallas_call | solution.py:347
  53.8 0.7 all-gather.8.cloned.1.call-update
  54.6 2.4 slice.36
  57.2 0.6 slice_bitcast_fusion
  57.8 1.8 multiply_sine_fusion.1
  59.6 44.8 %make_qkv.2 = (bf16[512,256]{1,0:T(8,128)(2,1)}, bf16[4096,256]{1,0:T(8,128)(2,1)}, bf16[4096,256]{1,0:T(8,128)(2,1)}) custom-call(bf16[512,3072]{1,0:T(8,128)(2,1)} %get-tuple-element.35.h_ref, bf16[3072,768]{1,0:T(8,128)(2,1)} %get-tuple-element.36.w_any, f32[512,128]{1,0:T(8,128)} %get-tuple-element.81.cos_ref, f32[512,128]{1,0:T(8,128)} %get-tuple-element.80.sin_ref, ...), custom_call_target="tpu_custom_call" | custom-call | flops 100000000 | bytes 10000000 | tf_op jit(solution)/shard_map/make_qkv/pallas_call | solution.py:263
  104.4 4.8 fusion.12
  109.2 1.3 fusion.3
  110.5 0.7 fusion.11
  111.2 2.5 fusion.8.a_ref
  113.7 77.1 %project_reduce.4 = (bf16[32,3072]{1,0:T(8,128)(2,1)}, bf16[512,3072]{1,0:T(8,128)(2,1)}, bf16[12288,384]{1,0:T(8,128)(2,1)}) custom-call(bf16[512,256]{1,0:T(8,128)(2,1)} %fusion.8.a_ref, bf16[8,256,384]{2,1,0:T(8,128)(2,1)} %bitcast.33, bf16[32,3072]{1,0:T(8,128)(2,1)} %get-tuple-element.41.res_ref, f32[1,3072]{1,0:T(1,128)} %get-tuple-element.75.sa_ref, ...), custom_call_target="tpu_custom_call" | custom-call | flops 100000000 | bytes 10000000 | tf_op jit(solution)/shard_map/project_reduce/pallas_call | solution.py:596
  191.6 1.8 multiply_sine_fusion
  193.5 23.6 %all-gather.18.cloned.1.call-done = bf16[1,3072,1536]{2,1,0:T(8,128)(2,1)} async-done(((bf16[1,384,1536]{2,1,0:T(8,128)(2,1)}), bf16[1,3072,1536]{2,1,0:T(8,128)(2,1)}) %all-gather.18.cloned.1.call-update) | async-done | bytes 9437200 | tf_op jit(solution)/shard_map/all_gather | solution.py:620
  217.1 94.4 %project_reduce.5 = (bf16[32,3072]{1,0:T(8,128)(2,1)}, bf16[512,3072]{1,0:T(8,128)(2,1)}, bf16[3072,768]{1,0:T(8,128)(2,1)}, bf16[2048,384]{1,0:T(8,128)(2,1)}) custom-call(bf16[512,3072]{1,0:T(8,128)(2,1)} %get-tuple-element.47.a_ref, bf16[8,1536,384]{2,1,0:T(8,128)(2,1)} %bitcast.27, bf16[32,3072]{1,0:T(8,128)(2,1)} %get-tuple-element.49.res_ref, ...), custom_call_target="tpu_custom_call" | custom-call | flops 100000000 | bytes 10000000 | tf_op jit(solution)/shard_map/project_reduce/pallas_call | solution.py:596
  311.5 38.5 %make_qkv.3 = (bf16[512,256]{1,0:T(8,128)(2,1)}, bf16[4096,256]{1,0:T(8,128)(2,1)}, bf16[4096,256]{1,0:T(8,128)(2,1)}) custom-call(bf16[512,3072]{1,0:T(8,128)(2,1)} %get-tuple-element.52.h_ref, bf16[3072,768]{1,0:T(8,128)(2,1)} %get-tuple-element.53.w_any, f32[512,128]{1,0:T(8,128)} %get-tuple-element.79.cos_ref, f32[512,128]{1,0:T(8,128)} %get-tuple-element.78.sin_ref, ...), custom_call_target="tpu_custom_call" | custom-call | flops 100000000 | bytes 10000000 | tf_op jit(solution)/shard_map/make_qkv/pallas_call | solution.py:263
  350.0 4.8 fusion.13
  354.8 1.3 fusion.4
  356.4 2.9 fusion.7.a_ref
  359.3 70.9 %project_reduce.6 = (bf16[32,3072]{1,0:T(8,128)(2,1)}, bf16[512,3072]{1,0:T(8,128)(2,1)}, bf16[12288,384]{1,0:T(8,128)(2,1)}) custom-call(bf16[512,256]{1,0:T(8,128)(2,1)} %fusion.7.a_ref, bf16[8,256,384]{2,1,0:T(8,128)(2,1)} %bitcast.34, bf16[32,3072]{1,0:T(8,128)(2,1)} %get-tuple-element.60.res_ref, f32[1,3072]{1,0:T(1,128)} %get-tuple-element.71.sa_ref, ...), custom_call_target="tpu_custom_call" | custom-call | flops 100000000 | bytes 10000000 | tf_op jit(solution)/shard_map/project_reduce/pallas_call | solution.py:596
  430.2 5.9 %pad_maximum_fusion = (bf16[2,4096,1,256]{3,1,2,0:T(8,128)(2,1)}, bf16[2,4096,1,256]{3,1,2,0:T(8,128)(2,1)}) fusion(bf16[1,4096,1,256]{3,1,2,0:T(8,128)(2,1)} %bitcast.31, bf16[1,4096,1,256]{3,1,2,0:T(8,128)(2,1)} %bitcast.29, bf16[1,4096,1,256]{3,1,2,0:T(8,128)(2,1)} %bitcast.32, bf16[1,4096,1,256]{3,1,2,0:T(8,128)(2,1)} %bitcast.30), kind=kLoop, calls=%fused_computation.14 | loop fusion | flops 4194304 | bytes 16777216 | tf_op jit(solution)/shard_map/stack | solution.py:650
  436.2 84.0 %project_reduce.7 = bf16[8,512,384]{2,1,0:T(8,128)(2,1)} custom-call(bf16[512,3072]{1,0:T(8,128)(2,1)} %get-tuple-element.61.a_ref, bf16[8,1536,384]{2,1,0:T(8,128)(2,1)} %bitcast.28, bf16[32,3072]{1,0:T(8,128)(2,1)} %get-tuple-element.63.res_ref, f32[1,3072]{1,0:T(1,128)} %get-tuple-element.69.sa_ref.sb_ref, f32[1,3072]{1,0:T(1,128)} %get-tuple-element.69.sa_ref.sb_ref, ...), custom_call_target="tpu_custom_call" | custom-call | flops 100000000 | bytes 10000000 | tf_op jit(solution)/shard_map/project_reduce/pallas_call | solution.py:596
  520.1 3.9 copy.18
  (33 shorter events, 1.6 us)
Async XLA Ops:
  7.2 186.3 %all-gather.10.cloned.1.call-start = ((), (), s32[]{:S(2)}) async-start(), calls=%async_computation.1 | async-start | bytes 5308416 | tf_op jit(solution)/shard_map/all_gather | solution.py:622
  10.2 46.8 %copy-start.5 = (s32[4096]{0:T(1024)S(1)}, s32[4096]{0:T(1024)}, u32[]{:S(2)}) copy-start(s32[4096]{0:T(1024)} %param.13) | copy-start | bytes 49156
  10.2 46.9 %copy-start.4 = (s32[4096]{0:T(1024)S(1)}, s32[4096]{0:T(1024)}, u32[]{:S(2)}) copy-start(s32[4096]{0:T(1024)} %param.14) | copy-start | bytes 49156
  10.2 47.0 %copy-start.3 = (f32[2,2,256]{2,1,0:T(2,128)S(1)}, f32[2,2,256]{2,1,0:T(2,128)}, u32[]{:S(2)}) copy-start(f32[2,2,256]{2,1,0:T(2,128)} %param.23) | copy-start | bytes 12292
  53.8 139.7 %all-gather.8.cloned.1.call-start = ((), (), s32[]{:S(2)}) async-start(), calls=%async_computation | async-start | bytes 5308416 | tf_op jit(solution)/shard_map/all_gather | solution.py:622
  54.5 162.6 %all-gather.18.cloned.1.call-start = ((), (), s32[]{:S(2)}) async-start(), calls=%async_computation.5 | async-start | bytes 10616832 | tf_op jit(solution)/shard_map/all_gather | solution.py:620
  56.9 379.2 %all-gather.14.cloned.1.call-start = ((), (), s32[]{:S(2)}) async-start(), calls=%async_computation.3 | async-start | bytes 5308416 | tf_op jit(solution)/shard_map/all_gather | solution.py:645
  109.2 1.3 copy-start.2
  109.2 2.0 copy-start
  190.8 245.3 %all-gather.12.cloned.1.call-start = ((), (), s32[]{:S(2)}) async-start(), calls=%async_computation.2 | async-start | bytes 10616832 | tf_op jit(solution)/shard_map/all_gather | solution.py:645
  191.4 244.8 %all-gather.16.cloned.1.call-start = ((), (), s32[]{:S(2)}) async-start(), calls=%async_computation.4 | async-start | bytes 5308416 | tf_op jit(solution)/shard_map/all_gather | solution.py:635
  354.8 1.6 copy-start.1
Sparse Core Ops, SparseCore 0:
  53.9 50.3 all-gather.9
  105.9 48.6 all-gather.7
  156.9 60.1 all-gather.17
  218.6 46.2 all-gather.13
  266.5 74.4 all-gather.11
  350.1 46.6 all-gather.15
